TPU v7x, 8 devices: a whole 2x2x1 slice. The times are simulated.
8 devices in a mesh: data: 1 (over z), model: 2 (over y), seq: 4 (over x, core).
Axes of the slice: x: 2, y: 2, z: 1, core: 2. Of those that a mesh axis runs over, the one named last changes fastest.
Arguments:
- tokens: bfloat16 [64, 2048, 1280], P('data', 'seq')
- lengths: int32 [64], P('data')
- slot_params: bfloat16 [1280, 128], replicated
- logit_scale: float32 [], replicated
- w_in: bfloat16 [32, 1280, 5120], P('seq', None, 'model')
- w_out: bfloat16 [32, 5120, 1280], P('seq', 'model')
Outputs:
- output: bfloat16 [64, 2048, 1280], P('data', 'seq')
All inputs are finite; a program needn't handle non-finite values.
Results may differ from a plain program's by a relative error of at most 0.0143614.
Values are sent between devices in bfloat16 or wider.
A program may use at most 1.25 GiB of HBM per device.

v0:
```python
import jax
import jax.numpy as jnp
from jax import lax
from jax.sharding import PartitionSpec as P

NORM_EPS = 1e-6


def unit_vectors(values, axis):
    v32 = values.astype(jnp.float32)
    return (v32 * lax.rsqrt(jnp.sum(v32 * v32, axis=axis, keepdims=True) + NORM_EPS)).astype(jnp.bfloat16)


def solution(mesh):
    seq_size = mesh.shape["seq"]

    def local_layer(tokens, lengths, slot_params, logit_scale, w_in, w_out):
        batch_size, tok_count, model_dim = tokens.shape
        n_slots = slot_params.shape[1]
        local_experts = w_in.shape[0]
        local_slots = n_slots // seq_size
        slot_per = local_slots // local_experts
        positions = lax.axis_index("seq") * tok_count + jnp.arange(tok_count)
        is_valid = positions[None, :] < lengths[:, None]
        logits = logit_scale * jnp.einsum("bmd,dn->bmn", unit_vectors(tokens, 2), unit_vectors(slot_params, 0), preferred_element_type=jnp.float32)
        masked = jnp.where(is_valid[:, :, None], logits, -1e30)
        col_max = lax.pmax(jnp.max(masked, axis=1, keepdims=True), "seq")
        weights = jnp.exp(masked - col_max)
        col_sum = lax.psum_scatter(jnp.sum(weights, axis=1), "seq", scatter_dimension=1, tiled=True)
        part_sum = jnp.einsum("bmn,bmd->bnd", weights.astype(jnp.bfloat16), tokens, preferred_element_type=jnp.float32)
        slot_sum = lax.psum_scatter(part_sum.astype(jnp.bfloat16), "seq", scatter_dimension=1, tiled=True)
        slot_in = (slot_sum.astype(jnp.float32) / col_sum[:, :, None]).astype(jnp.bfloat16)
        grouped = slot_in.reshape(batch_size, local_experts, slot_per, model_dim)
        hidden = jnp.einsum("besd,edf->besf", grouped, w_in, preferred_element_type=jnp.float32)
        hidden = jax.nn.gelu(hidden, approximate=False).astype(jnp.bfloat16)
        out_part = jnp.einsum("besf,efd->besd", hidden, w_out, preferred_element_type=jnp.float32)
        slot_out = lax.psum(out_part, "model").astype(jnp.bfloat16).reshape(batch_size, local_slots, model_dim)
        all_slots = lax.all_gather(slot_out, "seq", axis=1, tiled=True)
        mix_weights = jax.nn.softmax(logits, axis=-1).astype(jnp.bfloat16)
        mixed = jnp.einsum("bmn,bnd->bmd", mix_weights, all_slots, preferred_element_type=jnp.float32)
        return jnp.where(is_valid[:, :, None], mixed, 0.0).astype(jnp.bfloat16)

    return jax.shard_map(local_layer, mesh=mesh, in_specs=(P("data", "seq", None), P("data"), P(), P(), P("seq", None, "model"), P("seq", "model", None)), out_specs=P("data", "seq", None), check_vma=False)
```

profile of v0, /device:TPU:0, one launch (start us, length us, event | category | flops | bytes accessed | tf_op | source)
XLA Modules:
  0.0 809.5 jit_solution(8969118530094861299)
XLA Ops:
  6.5 0.0 reduce-scatter.7.cloned.1.call-start
  7.2 1.2 fusion.45
  8.4 0.0 copy-start.3
  8.4 0.0 copy-start.2
  8.4 27.2 %fusion.1 = f32[64,512]{1,0:T(8,128)S(1)} fusion(bf16[64,512,1280]{2,1,0:T(8,128)(2,1)} %param.6), kind=kLoop, calls=%fused_computation.3 | loop fusion | flops 125796352 | bytes 84017152 | tf_op jit(solution)/shard_map/reduce_sum | solution.py:11
  35.6 0.0 copy-done.3
  35.6 0.1 broadcast_compare_fusion
  35.7 0.0 copy-done.2
  35.8 0.0 copy-start
  35.8 40.0 %select_reduce_fusion = (f32[64,128]{1,0:T(8,128)S(1)}, f32[64,512,128]{2,1,0:T(8,128)}) fusion(f32[]{:T(128)S(6)} %copy.21, pred[64,512]{1,0:T(8,128)(4,1)S(1)} %broadcast_compare_fusion, bf16[1280,128]{1,0:T(8,128)(2,1)S(1)} %copy-done.2, f32[128]{0:T(128)S(1)} %add_rsqrt_fusion.1, bf16[64,512,1280]{2,1,0:T(8,128)(2,1)} %param.6, ...), kind=kOutput, calls=%fused_computation.40 | convolution fusion | flops 10876313600 | bytes 101188096 | tf_op jit(solution)/shard_map/bmd,dn->bmn/dot_general | solution.py:25
  75.7 13.3 %pmax.7 = f32[64,128]{1,0:T(8,128)S(1)} all-reduce(f32[64,128]{1,0:T(8,128)S(1)} %get-tuple-element.5), channel_id=1, replica_groups=mesh['data'=1,'model'=2,'seq'=4] {'seq'}, use_global_device_ids=true, to_apply=%region_5.6 | all-reduce | flops 8192 | bytes 65536 | tf_op jit(solution)/shard_map/pmax | solution.py:27
  89.0 7.3 fusion.30
  96.3 0.7 copy.17
  97.0 0.0 reduce-scatter.7.cloned.1.call-update
  97.0 0.0 reduce-scatter.5.cloned.1.call-start
  97.1 0.0 copy-done
  97.1 39.5 %convolution_convert_fusion = bf16[64,128,1280]{2,1,0:T(8,128)(2,1)} fusion(bf16[64,512,1280]{2,1,0:T(8,128)(2,1)} %param.6, f32[64,512,128]{2,1,0:T(8,128)} %get-tuple-element.6, f32[64,128]{1,0:T(8,128)S(1)} %pmax.7, f32[]{:T(128)S(6)} %copy.21, pred[64,512]{1,0:T(8,128)(4,1)S(1)} %broadcast_compare_fusion), kind=kOutput, calls=%fused_computation.36 | convolution fusion | flops 10764681216 | bytes 121700352 | tf_op jit(solution)/shard_map/bmn,bmd->bnd/dot_general | solution.py:30
  136.6 0.0 reduce-scatter.5.cloned.1.call-update
  136.6 0.0 all-gather.2.cloned.1.call-start
  136.7 0.0 reduce-scatter.7.cloned.1.call-done
  136.7 0.8 copy.18
  137.5 143.3 %reduce-scatter.5.cloned.1.call-done = bf16[64,32,1280]{2,1,0:T(8,128)(2,1)} async-done(((bf16[64,128,1280]{2,1,0:T(8,128)(2,1)}), bf16[64,32,1280]{2,1,0:T(8,128)(2,1)}) %reduce-scatter.5.cloned.1.call-update) | async-done | bytes 5242896 | tf_op jit(solution)/shard_map/reduce_scatter | solution.py:31
  280.8 4.6 divide_convert_fusion.1
  285.4 2.9 copy.16
  288.3 59.8 %fusion.12.clone.4 = bf16[64,8,4,2560]{3,0,2,1:T(8,128)(2,1)} fusion(bf16[64,8,4,1280]{3,0,2,1:T(8,128)(2,1)S(1)} %bitcast.117, bf16[8,1280,2560]{2,1,0:T(8,128)(2,1)} %param.10), kind=kOutput, calls=%fused_computation.15.clone.clone.clone.1 | convolution fusion | flops 13762560000 | bytes 68157440 | tf_op jit(solution)/shard_map/besd,edf->besf/dot_general | solution.py:34
  348.1 28.2 %fusion.42 = f32[64,8,4,1280]{3,0,2,1:T(8,128)} fusion(bf16[8,2560,1280]{2,1,0:T(8,128)(2,1)} %param.11, bf16[64,8,4,2560]{3,0,2,1:T(8,128)(2,1)} %fusion.12.clone.4), kind=kOutput, calls=%fused_computation.52 | convolution fusion | flops 13421772800 | bytes 73400320 | tf_op jit(solution)/shard_map/besf,efd->besd/dot_general | solution.py:36
  376.2 241.6 %all-reduce.1 = bf16[64,8,4,1280]{3,0,2,1:T(8,128)(2,1)} all-reduce(f32[64,8,4,1280]{3,0,2,1:T(8,128)} %fusion.42), channel_id=1, replica_groups=mesh['data'=1,'model'=2,'seq'=4] {'model'}, use_global_device_ids=true, to_apply=%region_9.10 | all-reduce | flops 2621440 | bytes 15728640 | tf_op jit(solution)/shard_map/psum | solution.py:37
  617.9 7.7 copy.12
  625.6 0.0 copy-start.1
  625.6 0.0 all-gather.2.cloned.1.call-update
  625.6 22.9 %fusion.83 = (f32[64,512]{1,0:T(8,128)S(1)}, f32[64,512,128]{2,1,0:T(8,128)}) fusion(f32[64,512,128]{2,1,0:T(8,128)} %get-tuple-element.6, f32[]{:T(128)S(6)} %copy.21), kind=kOutput, calls=%fused_computation.94 | output fusion | flops 16777344 | bytes 33685508 | tf_op jit(solution)/shard_map/sub | solution.py:39
  648.5 106.2 %all-gather.2.cloned.1.call-done = bf16[64,128,1280]{2,1,0:T(8,128)(2,1)} async-done(((bf16[64,32,1280]{2,1,0:T(8,128)(2,1)}), bf16[64,128,1280]{2,1,0:T(8,128)(2,1)}) %all-gather.2.cloned.1.call-update) | async-done | bytes 20971536 | tf_op jit(solution)/shard_map/all_gather | solution.py:38
  754.7 0.0 copy-done.1
  754.7 48.2 %select_convert_fusion = bf16[64,512,1280]{2,1,0:T(8,128)(2,1)} fusion(bf16[64,128,1280]{2,1,0:T(8,128)(2,1)} %all-gather.2.cloned.1.call-done, pred[64,512]{1,0:T(8,128)(4,1)S(1)} %copy-done.1, f32[64,512,128]{2,1,0:T(8,128)} %get-tuple-element.8, f32[64,512]{1,0:T(8,128)S(1)} %get-tuple-element.7), kind=kOutput, calls=%fused_computation.5 | convolution fusion | flops 10829692928 | bytes 121798656 | tf_op jit(solution)/shard_map/bmn,bnd->bmd/dot_general | solution.py:40
  (3 shorter events, 0.0 us)
Async XLA Ops:
  6.5 130.2 %reduce-scatter.7.cloned.1.call-start = ((), (), s32[]{:S(2)}) async-start(), calls=%async_computation.4 | async-start | bytes 81920
  8.4 27.3 %copy-start.3 = (s32[64]{0:T(128)S(1)}, s32[64]{0:T(128)}, u32[]{:S(2)}) copy-start(s32[64]{0:T(128)} %param.7) | copy-start | bytes 772
  8.4 27.4 %copy-start.2 = (bf16[1280,128]{1,0:T(8,128)(2,1)S(1)}, bf16[1280,128]{1,0:T(8,128)(2,1)}, u32[]{:S(2)}) copy-start(bf16[1280,128]{1,0:T(8,128)(2,1)} %param.8) | copy-start | bytes 983044
  35.8 61.3 %copy-start = (pred[64,512]{1,0:T(8,128)(4,1)}, pred[64,512]{1,0:T(8,128)(4,1)S(1)}, u32[]{:S(2)}) copy-start(pred[64,512]{1,0:T(8,128)(4,1)S(1)} %broadcast_compare_fusion) | copy-start | bytes 98308
  97.0 183.8 %reduce-scatter.5.cloned.1.call-start = ((), (), s32[]{:S(2)}) async-start(), calls=%async_computation.2 | async-start | bytes 26214400 | tf_op jit(solution)/shard_map/reduce_scatter | solution.py:31
  136.6 618.1 %all-gather.2.cloned.1.call-start = ((), (), s32[]{:S(2)}) async-start(), calls=%async_computation.3 | async-start | bytes 26214400 | tf_op jit(solution)/shard_map/all_gather | solution.py:38
  625.6 129.2 %copy-start.1 = (pred[64,512]{1,0:T(8,128)(4,1)S(1)}, pred[64,512]{1,0:T(8,128)(4,1)}, u32[]{:S(2)}) copy-start(pred[64,512]{1,0:T(8,128)(4,1)} %copy-done) | copy-start | bytes 98308
Sparse Core Ops, SparseCore 0:
  97.1 14.0 reduce-scatter.6
  136.8 144.0 reduce-scatter.4
  625.7 128.9 all-gather.1
where the time goes:
time: 810 us; the launch traced here: 809 us
  blocking collectives  255 us (31%)
  waiting for transfers between devices  250 us (31%)
  matrix products  216 us (27%)
  other arithmetic  63.3 us (8%)
  between operations  13.9 us (2%)
  local copies, waits for them, and re-layouts  12.1 us (1%)
    psum x1, blocking collectives, local_layer(): lax.psum(out_part, 'model').astype(jnp.bfloat16)  242 us
    reduce_scatter x1, waiting for transfers between devices, local_layer(): lax.psum_scatter(part_sum.astype(jnp.bfloat16), 'seq', scatter_dimension=...  143 us
    all_gather x1, waiting for transfers between devices, local_layer(): all_slots = lax.all_gather(slot_out, 'seq', axis=1, tiled=True)  106 us
    dot_general x1, matrix products, local_layer(): jnp.einsum('besd,edf->besf', grouped, w_in, preferred_element_type=jnp.fl...  59.8 us
    dot_general x1, matrix products, local_layer(): jnp.einsum('bmn,bnd->bmd', mix_weights, all_slots, preferred_element_type...  48.2 us
    dot_general x1, matrix products, local_layer(): jnp.einsum('bmd,dn->bmn', unit_vectors(tokens, 2), unit_vectors(slot_para...  40 us
    dot_general x1, matrix products, local_layer(): jnp.einsum('bmn,bmd->bnd', weights.astype(jnp.bfloat16), tokens, preferre...  39.5 us
    reduce_sum x2, other arithmetic, unit_vectors(): jnp.sum(v32 * v32, axis=axis, keepdims=True) + NORM_EPS  28.4 us
  transfers between devices with their start and end apart: 3, of which 2 were waited for; matrix products, arithmetic and copies ran while one was open for 8% of the time, Pallas kernels for 0%

commit v1 on v0

v1 whole, which is shorter than its diff:
```python
import functools

import jax
import jax.numpy as jnp
from jax import lax
from jax.experimental import pallas as pl
from jax.experimental.pallas import tpu as pltpu
from jax.sharding import PartitionSpec as P


NORM_EPS = 1e-6
NEG = -1e30
MESH = pl.DeviceIdType.MESH
CHUNK_SEQS = 4
X_SLOTS = 6
C_SLOTS = 8
ROW_BLOCK = 256
HIDDEN_TILE = 2560
SUB_TILE = 256
LANES = 128
GROUPS = 2
BATCH_CHUNKS = 4
COMBINE_SEQS = 4


def dispatch_kernel(n_half, n_tok, dim, n_slots, per_dev, phi_ref, len_ref, g_ref, x_hbm, xs_hbm, c_hbm,
                    v_ref, xbuf, lbuf, cbuf, sbuf, lse1, r1, lr1, m0, s2, lse2, r2, lr2, xso,
                    xsem, csem, osem, s1_sem, r1_sem, s2_sem, r2_sem, s3_sem, r3_sem):
    s = lax.axis_index("seq")
    m = lax.axis_index("model")
    core_peer = {"seq": s + 1 - 2 * lax.rem(s, 2)}
    x_peer = {"seq": lax.rem(s + 2, 4)}
    y_peer = {"model": 1 - m}
    cs = CHUNK_SEQS
    n = n_half // cs

    barrier = pltpu.get_barrier_semaphore()
    for peer in (core_peer, x_peer, y_peer):
        pl.semaphore_signal(barrier, inc=1, device_id=peer, device_id_type=MESH)

    def batch_of(t):
        return lax.rem(m * n_half + t, 2 * n_half)

    def x_copy(t):
        slot = lax.rem(t, X_SLOTS)
        return pltpu.make_async_copy(x_hbm.at[batch_of(t)], xbuf.at[slot], xsem.at[slot])

    def c_copy(t):
        slot = lax.rem(t, C_SLOTS)
        return pltpu.make_async_copy(cbuf.at[slot], c_hbm.at[batch_of(t)], csem.at[slot])

    for t in range(X_SLOTS - 1):
        x_copy(t).start()

    phi = phi_ref[...].astype(jnp.float32)
    unit = (phi * lax.rsqrt(jnp.sum(phi * phi, axis=0, keepdims=True) + NORM_EPS)).astype(jnp.bfloat16)
    row = lax.broadcasted_iota(jnp.int32, (n_slots, n_slots), 0)
    col = lax.broadcasted_iota(jnp.int32, (n_slots, n_slots), 1)
    target = jnp.bitwise_xor(col, s * per_dev)
    pick = jnp.where(row == target, 1.0, 0.0).astype(jnp.bfloat16)
    v_ref[...] = jnp.dot(unit, pick, preferred_element_type=jnp.float32).astype(jnp.bfloat16)
    lse1[...] = jnp.zeros_like(lse1)
    g = g_ref[0]

    pl.semaphore_wait(barrier, 3)

    def logits_and_mix(t):
        xslot = lax.rem(t, X_SLOTS)
        cslot = lax.rem(t, C_SLOTS)
        length = len_ref[batch_of(t)]

        @pl.when(t + X_SLOTS - 1 < 2 * n_half)
        def _():
            x_copy(t + X_SLOTS - 1).start()

        x_copy(t).wait()

        @pl.when(t >= C_SLOTS)
        def _():
            c_copy(t - C_SLOTS).wait()

        dots = jnp.dot(xbuf[xslot], v_ref[...], preferred_element_type=jnp.float32)
        for r in range(n_tok // ROW_BLOCK):
            rows = pl.ds(r * ROW_BLOCK, ROW_BLOCK)
            square = jnp.zeros((ROW_BLOCK, LANES), jnp.float32)
            for c in range(dim // LANES):
                x32 = xbuf[xslot, rows, c * LANES:(c + 1) * LANES].astype(jnp.float32)
                square += x32 * x32
            scale = lax.rsqrt(jnp.sum(square, axis=1, keepdims=True) + NORM_EPS)
            block = dots[r * ROW_BLOCK:(r + 1) * ROW_BLOCK]
            lg = jnp.where(scale > 0.0, block * (g * scale), 0.0)
            lbuf[rows, :] = lg
            e = jnp.exp(lg - jnp.max(lg, axis=1, keepdims=True))
            mix = e * (1.0 / jnp.sum(e, axis=1, keepdims=True))
            pos = s * n_tok + r * ROW_BLOCK + lax.broadcasted_iota(jnp.int32, (ROW_BLOCK, 1), 0)
            cbuf[cslot, rows, :] = jnp.where(pos < length, mix, 0.0).astype(jnp.bfloat16)
        c_copy(t).start()
        return xslot, length

    def own(k, j):
        t = k * cs + j
        xslot, length = logits_and_mix(t)
        ok = s * n_tok + lax.broadcasted_iota(jnp.int32, (n_tok, 1), 0) < length
        lg = jnp.where(ok, lbuf[...], NEG)
        mx = jnp.max(lg, axis=0, keepdims=True)
        w = jnp.where(ok, jnp.exp(lg - mx), 0.0)
        z = jnp.sum(w, axis=0, keepdims=True)
        z = jnp.where(z > 0.0, z, 1.0)
        lse1[k, pl.ds(j, 1), :] = mx + jnp.log(z)
        rz = jnp.transpose(jnp.broadcast_to(1.0 / z, (8, n_slots)))[:, :1]
        part = lax.dot_general(w.astype(jnp.bfloat16), xbuf[xslot], (((0,), (0,)), ((), ())), preferred_element_type=jnp.float32)
        sbuf[t] = (part * rz).astype(jnp.bfloat16)

    def remote(src, dst, send, recv, peer):
        return pltpu.make_async_remote_copy(src, dst, send, recv, device_id=peer, device_id_type=MESH)

    def d1(k):
        seqs = pl.ds(k * cs, cs)
        p = per_dev
        return (
            remote(sbuf.at[seqs, pl.ds(p, p)], r1.at[seqs, pl.ds(0, p)], s1_sem.at[k, 0], r1_sem.at[k, 0], core_peer),
            remote(sbuf.at[seqs, pl.ds(3 * p, p)], r1.at[seqs, pl.ds(p, p)], s1_sem.at[k, 1], r1_sem.at[k, 1], core_peer),
            remote(lse1.at[k], lr1.at[k], s1_sem.at[k, 2], r1_sem.at[k, 2], core_peer),
        )

    def d2(k):
        seqs = pl.ds(k * cs, cs)
        return (
            remote(s2.at[seqs], r2.at[seqs], s2_sem.at[k, 0], r2_sem.at[k, 0], x_peer),
            remote(lse2.at[k], lr2.at[k], s2_sem.at[k, 1], r2_sem.at[k, 1], x_peer),
        )

    def d3(k):
        seqs = pl.ds(k * cs, cs)
        return remote(xso.at[seqs], xs_hbm.at[pl.ds(m * n_half + k * cs, cs)], s3_sem.at[k], r3_sem.at[k], y_peer)

    def keep(k):
        seqs = pl.ds(k * cs, cs)
        return pltpu.make_async_copy(xso.at[seqs], xs_hbm.at[pl.ds(m * n_half + k * cs, cs)], osem.at[k])

    def weights(a, b):
        top = jnp.maximum(a, b)
        ea, eb = jnp.exp(a - top), jnp.exp(b - top)
        tot = ea + eb
        return jnp.transpose(ea / tot), jnp.transpose(eb / tot), top + jnp.log(tot)

    def merge1(k):
        for c in d1(k):
            c.wait_recv()
        p = per_dev
        wa, wb, joint = weights(lse1[k], pltpu.roll(lr1[k], n_slots - p, 1))
        lse2[k] = joint
        for j in range(cs):
            t = k * cs + j
            m0[t] = wa[:p, j:j + 1] * sbuf[t, 0:p, :].astype(jnp.float32) + wb[:p, j:j + 1] * r1[t, 0:p, :].astype(jnp.float32)
            s2[t] = (wa[2 * p:3 * p, j:j + 1] * sbuf[t, 2 * p:3 * p, :].astype(jnp.float32)
                     + wb[2 * p:3 * p, j:j + 1] * r1[t, p:2 * p, :].astype(jnp.float32)).astype(jnp.bfloat16)
        for c in d2(k):
            c.start()

    def merge2(k):
        for c in d2(k):
            c.wait_recv()
        p = per_dev
        wa, wb, _ = weights(lse2[k], pltpu.roll(lr2[k], n_slots - 2 * p, 1))
        for j in range(cs):
            t = k * cs + j
            xso[t] = (wa[:p, j:j + 1] * m0[t] + wb[:p, j:j + 1] * r2[t].astype(jnp.float32)).astype(jnp.bfloat16)
        d3(k).start()
        keep(k).start()

    lead = 4
    early = n - lead
    late = n // 2 - 1

    @pl.loop(0, 2 * n)
    def _(k):
        @pl.when(k < n)
        def _():
            @pl.loop(0, cs)
            def _(j):
                own(k, j)

            for c in d1(k):
                c.start()

        @pl.when(k >= n)
        def _():
            @pl.loop(0, cs)
            def _(j):
                logits_and_mix(k * cs + j)

        @pl.when((k >= 1) & (k <= n))
        def _():
            merge1(k - 1)

        @pl.when((k >= lead) & (k < n))
        def _():
            merge2(k - lead)

        @pl.when((k > n) & (lax.rem(k - n, 2) == 1) & ((k - n) // 2 < late))
        def _():
            merge2(early + (k - n) // 2)

    @pl.loop(early + late, n)
    def _(k):
        merge2(k)

    @pl.loop(2 * n_half - C_SLOTS, 2 * n_half)
    def _(t):
        c_copy(t).wait()

    @pl.loop(0, n)
    def _(k):
        for c in d1(k):
            c.wait_send()
        for c in d2(k):
            c.wait_send()
        d3(k).wait()
        keep(k).wait()


def dispatch(tokens, lengths, phi, scale, per_dev):
    batch, n_tok, dim = tokens.shape
    n_slots = phi.shape[1]
    half = batch // 2
    n = half // CHUNK_SEQS
    bf, f32 = jnp.bfloat16, jnp.float32
    return pl.pallas_call(
        functools.partial(dispatch_kernel, half, n_tok, dim, n_slots, per_dev),
        out_shape=(jax.ShapeDtypeStruct((batch, per_dev, dim), bf), jax.ShapeDtypeStruct((batch, n_tok, n_slots), bf)),
        in_specs=[
            pl.BlockSpec(memory_space=pltpu.VMEM),
            pl.BlockSpec(memory_space=pltpu.SMEM),
            pl.BlockSpec(memory_space=pltpu.SMEM),
            pl.BlockSpec(memory_space=pl.ANY),
        ],
        out_specs=[pl.BlockSpec(memory_space=pl.ANY)] * 2,
        scratch_shapes=[
            pltpu.VMEM((dim, n_slots), bf),
            pltpu.VMEM((X_SLOTS, n_tok, dim), bf),
            pltpu.VMEM((n_tok, n_slots), f32),
            pltpu.VMEM((C_SLOTS, n_tok, n_slots), bf),
            pltpu.VMEM((half, n_slots, dim), bf),
            pltpu.VMEM((n, 8, n_slots), f32),
            pltpu.VMEM((half, 2 * per_dev, dim), bf),
            pltpu.VMEM((n, 8, n_slots), f32),
            pltpu.VMEM((half, per_dev, dim), f32),
            pltpu.VMEM((half, per_dev, dim), bf),
            pltpu.VMEM((n, 8, n_slots), f32),
            pltpu.VMEM((half, per_dev, dim), bf),
            pltpu.VMEM((n, 8, n_slots), f32),
            pltpu.VMEM((half, per_dev, dim), bf),
            pltpu.SemaphoreType.DMA((X_SLOTS,)),
            pltpu.SemaphoreType.DMA((C_SLOTS,)),
            pltpu.SemaphoreType.DMA((n,)),
            pltpu.SemaphoreType.DMA((n, 3)),
            pltpu.SemaphoreType.DMA((n, 3)),
            pltpu.SemaphoreType.DMA((n, 2)),
            pltpu.SemaphoreType.DMA((n, 2)),
            pltpu.SemaphoreType.DMA((n,)),
            pltpu.SemaphoreType.DMA((n,)),
        ],
        compiler_params=pltpu.CompilerParams(collective_id=0, has_side_effects=True, vmem_limit_bytes=58 * 1024 * 1024),
        name="dispatch",
    )(phi, lengths, scale, tokens)


def ffn_kernel(first, batch, slot_per, per_dev, grp, x_ref, wi_ref, wo_ref, *rest):
    outs, (xf, xe, acc, og) = rest[:BATCH_CHUNKS], rest[BATCH_CHUNKS:]
    e, h = pl.program_id(0), pl.program_id(1)
    last_e, last_h = pl.num_programs(0) - 1, pl.num_programs(1) - 1
    tiles = x_ref.shape[2] // LANES

    @pl.when((e == 0) & (h == 0))
    def _():
        @pl.loop(0, batch)
        def _(b):
            rows = pl.ds(pl.multiple_of(b * per_dev, per_dev), per_dev)
            for c in range(tiles):
                xf[c, rows, :] = x_ref[b, :, c * LANES:(c + 1) * LANES].astype(jnp.float32)

    @pl.when(h == 0)
    def _():
        for q in range(slot_per):
            for c in range(tiles):
                rows = xf[c, pl.ds((first + e) * slot_per + q, batch, stride=per_dev), :]
                xe[q * batch:(q + 1) * batch, c * LANES:(c + 1) * LANES] = rows.astype(jnp.bfloat16)

    acts = []
    for i in range(wi_ref.shape[2] // SUB_TILE):
        hid = jnp.dot(xe[...], wi_ref[0, :, i * SUB_TILE:(i + 1) * SUB_TILE], preferred_element_type=jnp.float32)
        acts.append((0.5 * hid * (1.0 + lax.erf(hid * 0.7071067811865476))).astype(jnp.bfloat16))
    part = jnp.dot(jnp.concatenate(acts, axis=1), wo_ref[0], preferred_element_type=jnp.float32)

    @pl.when(h == 0)
    def _():
        acc[...] = part

    @pl.when(h > 0)
    def _():
        acc[...] += part

    @pl.when(h == last_h)
    def _():
        for q in range(slot_per):
            for c in range(tiles):
                og[c, pl.ds(e * slot_per + q, batch, stride=grp), :] = acc[q * batch:(q + 1) * batch, c * LANES:(c + 1) * LANES]

    @pl.when((e == last_e) & (h == last_h))
    def _():
        step = batch // BATCH_CHUNKS
        for i, out in enumerate(outs):
            for b in range(step):
                rows = slice((i * step + b) * grp, (i * step + b + 1) * grp)
                for c in range(tiles):
                    out[b, :, c * LANES:(c + 1) * LANES] = og[c, rows, :].astype(jnp.bfloat16)


def ffn(group, xs, w_in, w_out, slot_per):
    batch, per_dev, dim = xs.shape
    experts, _, hidden = w_in.shape
    ge = experts // GROUPS
    grp = ge * slot_per
    first = group * ge
    step = batch // BATCH_CHUNKS
    rows = batch * slot_per
    return pl.pallas_call(
        functools.partial(ffn_kernel, first, batch, slot_per, per_dev, grp),
        grid=(ge, hidden // HIDDEN_TILE),
        out_shape=[jax.ShapeDtypeStruct((step, grp, dim), jnp.bfloat16)] * BATCH_CHUNKS,
        in_specs=[
            pl.BlockSpec((batch, per_dev, dim), lambda e, h: (0, 0, 0)),
            pl.BlockSpec((1, dim, HIDDEN_TILE), lambda e, h: (first + e, 0, h)),
            pl.BlockSpec((1, HIDDEN_TILE, dim), lambda e, h: (first + e, h, 0)),
        ],
        out_specs=[pl.BlockSpec((step, grp, dim), lambda e, h: (0, 0, 0))] * BATCH_CHUNKS,
        scratch_shapes=[
            pltpu.VMEM((dim // LANES, batch * per_dev, LANES), jnp.float32),
            pltpu.VMEM((rows, dim), jnp.bfloat16),
            pltpu.VMEM((rows, dim), jnp.float32),
            pltpu.VMEM((dim // LANES, batch * grp, LANES), jnp.float32),
        ],
        compiler_params=pltpu.CompilerParams(dimension_semantics=("arbitrary", "arbitrary"), vmem_limit_bytes=58 * 1024 * 1024),
        cost_estimate=pl.CostEstimate(flops=4 * ge * rows * dim * hidden, bytes_accessed=4 * ge * dim * hidden, transcendentals=0),
        name="ffn",
    )(xs, w_in, w_out)


def combine_kernel(first, n_tok, n_pieces, len_ref, off_ref, c_ref, *rest):
    pieces, out_ref = rest[:n_pieces], rest[-1]
    pos = off_ref[0] + lax.broadcasted_iota(jnp.int32, (n_tok, 1), 0)
    for i in range(COMBINE_SEQS):
        slots = jnp.concatenate([p[i] for p in pieces], axis=0)
        mixed = jnp.dot(c_ref[i], slots, preferred_element_type=jnp.float32)
        ok = pos < len_ref[first + pl.program_id(0) * COMBINE_SEQS + i]
        out_ref[i] = jnp.where(ok, mixed, 0.0).astype(jnp.bfloat16)


def combine(chunk, mix, pieces, lengths, offset, y):
    batch, n_tok, n_slots = mix.shape
    step, grp, dim = pieces[0].shape
    first = chunk * step
    n_p = len(pieces)
    cs = COMBINE_SEQS
    base = first // cs
    in_specs = [
        pl.BlockSpec((cs, n_tok, n_slots), lambda b, *_: (base + b, 0, 0)),
        *[pl.BlockSpec((cs, grp, dim), lambda b, *_: (b, 0, 0))] * n_p,
    ]
    args = [lengths, offset, mix, *pieces]
    alias = {}
    if y is not None:
        in_specs.append(pl.BlockSpec(memory_space=pl.ANY))
        args.append(y)
        alias = {len(args) - 1: 0}
    return pl.pallas_call(
        functools.partial(combine_kernel, first, n_tok, n_p),
        grid_spec=pltpu.PrefetchScalarGridSpec(
            num_scalar_prefetch=2,
            grid=(step // cs,),
            in_specs=in_specs,
            out_specs=pl.BlockSpec((cs, n_tok, dim), lambda b, *_: (base + b, 0, 0)),
        ),
        out_shape=jax.ShapeDtypeStruct((batch, n_tok, dim), jnp.bfloat16),
        input_output_aliases=alias,
        compiler_params=pltpu.CompilerParams(dimension_semantics=("arbitrary",), vmem_limit_bytes=32 * 1024 * 1024),
        cost_estimate=pl.CostEstimate(flops=2 * 2 * step * n_tok * n_slots * dim, bytes_accessed=2 * step * n_tok * (dim + n_slots), transcendentals=0),
        name="combine",
    )(*args)


def solution(mesh):
    seq_size = mesh.shape["seq"]
    swap_y = [(0, 1), (1, 0)]
    swap_x = [(i, i ^ 2) for i in range(seq_size)]
    swap_c = [(i, i ^ 1) for i in range(seq_size)]

    def local_layer(tokens, lengths, slot_params, logit_scale, w_in, w_out):
        n_tok = tokens.shape[1]
        per_dev = slot_params.shape[1] // seq_size
        slot_per = per_dev // w_in.shape[0]
        offset = (lax.axis_index("seq") * n_tok).reshape(1).astype(jnp.int32)
        xs, mix = dispatch(tokens, lengths, slot_params, logit_scale.reshape(1), per_dev)
        table = {}
        for group in range(GROUPS):
            parts = ffn(group, xs, w_in, w_out, slot_per)
            for k, part in enumerate(parts):
                other = lax.ppermute(part, "model", swap_y)
                own = (part.astype(jnp.float32) + other.astype(jnp.float32)).astype(jnp.bfloat16)
                across = lax.ppermute(own, "seq", swap_x)
                table[k, group, 0] = own
                table[k, group, 1] = lax.ppermute(own, "seq", swap_c)
                table[k, group, 2] = across
                table[k, group, 3] = lax.ppermute(across, "seq", swap_c)
        y = None
        for k in range(BATCH_CHUNKS):
            pieces = [table[k, group, q] for q in range(seq_size) for group in range(GROUPS)]
            y = combine(k, mix, pieces, lengths, offset, y)
        return y

    return jax.shard_map(local_layer, mesh=mesh, in_specs=(P("data", "seq", None), P("data"), P(), P(), P("seq", None, "model"), P("seq", "model", None)), out_specs=P("data", "seq", None), check_vma=False)
```

time: 810 us -> 383 us (0.47)
  blocking collectives: 255 us -> 0 us
  matrix products: 216 us -> 0 us
  Pallas kernels: 0 us -> 197 us
  waiting for transfers between devices: 250 us -> 148 us
  other arithmetic: 63.3 us -> 2.12 us
  starting transfers between devices: 0.09 us -> 22.8 us
  between operations: 13.9 us -> 0.94 us
    psum x1 -> x0, blocking collectives: 242 us -> none  [local_layer(): lax.psum(out_part, 'model').astype(jnp.bfloat16)]
    dot_general x5 -> x0, matrix products: 216 us -> none  [the longest x1 59.8 us: local_layer(): jnp.einsum('besd,edf->besf', grouped, w_in, preferred_element_type=jnp.fl...]
    pallas_call x0 -> x7, Pallas kernels: none -> 197 us  [the longest x1 92.8 us: dispatch(): pl.pallas_call(functools.partial(dispatch_kernel, half, n_tok, dim, n_slo...]
    ppermute x0 -> x32, waiting for transfers between devices: none -> 148 us  [the longest x8 87.9 us: local_layer(): other = lax.ppermute(part, 'model', swap_y)]
    reduce_scatter x1 -> x0, waiting for transfers between devices: 143 us -> none  [local_layer(): lax.psum_scatter(part_sum.astype(jnp.bfloat16), 'seq', scatter_dimension=...]
    all_gather x1 -> x0, waiting for transfers between devices: 106 us -> none  [local_layer(): all_slots = lax.all_gather(slot_out, 'seq', axis=1, tiled=True)]
    reduce_sum x3 -> x0, other arithmetic: 35.6 us -> none  [the longest x2 28.4 us: unit_vectors(): jnp.sum(v32 * v32, axis=axis, keepdims=True) + NORM_EPS]
    sub x1 -> x0, other arithmetic: 22.9 us -> none  [local_layer(): mix_weights = jax.nn.softmax(logits, axis=-1).astype(jnp.bfloat16)]
  transfers between devices with their start and end apart: 3 -> 32, of which waited for: 2 -> 12; matrix products, arithmetic and copies ran while one was open for 8% -> 1% of each run, Pallas kernels for 0% -> 17%
where the time goes in v1:
time: 383 us; the launch traced here: 382 us
  Pallas kernels  197 us (51%)
  waiting for transfers between devices  148 us (39%)
  starting transfers between devices  22.8 us (6%)
  local copies, waits for them, and re-layouts  11.3 us (3%)
    pallas_call x1, Pallas kernels, dispatch(): pl.pallas_call(functools.partial(dispatch_kernel, half, n_tok, dim, n_slo...  92.8 us
    ppermute x8, waiting for transfers between devices, local_layer(): other = lax.ppermute(part, 'model', swap_y)  87.9 us
    ppermute x8, waiting for transfers between devices, local_layer(): across = lax.ppermute(own, 'seq', swap_x)  60.2 us
    pallas_call x2, Pallas kernels, ffn(): pl.pallas_call(functools.partial(ffn_kernel, first, batch, slot_per, per_...  59.3 us
    pallas_call x4, Pallas kernels, combine(): pl.pallas_call(functools.partial(combine_kernel, first, n_tok, n_p), grid...  44.7 us
    ppermute x8, starting transfers between devices, local_layer(): across = lax.ppermute(own, 'seq', swap_x)  11.4 us
    unnamed x68, local copies, waits for them, and re-layouts  11.3 us
    ppermute x8, starting transfers between devices, local_layer(): other = lax.ppermute(part, 'model', swap_y)  8.95 us
  transfers between devices with their start and end apart: 32, of which 12 were waited for; matrix products, arithmetic and copies ran while one was open for 1% of the time, Pallas kernels for 17%

profile of v1, /device:TPU:0, one launch (start us, length us, event | category | flops | bytes accessed | tf_op | source)
XLA Modules:
  0.0 382.1 jit_solution(6431048390308375964)
XLA Ops:
  0.7 92.8 %dispatch.1 = (bf16[64,32,1280]{2,1,0:T(8,128)(2,1)}, bf16[64,512,128]{2,1,0:T(8,128)(2,1)}) custom-call(bf16[1280,128]{1,0:T(8,128)(2,1)} %phi_ref.1, s32[64]{0:T(128)} %len_ref.9, f32[1]{0:T(128)} %bitcast.2.g_ref, bf16[64,512,1280]{2,1,0:T(8,128)(2,1)} %x_hbm.1), custom_call_target="tpu_custom_call" | custom-call | tf_op jit(solution)/shard_map/dispatch/pallas_call | solution.py:229
  93.4 29.5 %ffn.2 = (bf16[16,16,1280]{2,1,0:T(8,128)(2,1)}, bf16[16,16,1280]{2,1,0:T(8,128)(2,1)}, bf16[16,16,1280]{2,1,0:T(8,128)(2,1)}, bf16[16,16,1280]{2,1,0:T(8,128)(2,1)}) custom-call(bf16[64,32,1280]{2,1,0:T(8,128)(2,1)} %get-tuple-element.16.x_ref, bf16[8,1280,2560]{2,1,0:T(8,128)(2,1)} %wi_ref.3, bf16[8,2560,1280]{2,1,0:T(8,128)(2,1)} %wo_ref.3), custom_call_target="tpu_custom_call" | custom-call | flops 13421772800 | bytes 52428800 | tf_op jit(solution)/shard_map/ffn/pallas_call | solution.py:328
  123.0 0.4 collective-permute-start.24
  123.4 29.7 %ffn.3 = (bf16[16,16,1280]{2,1,0:T(8,128)(2,1)}, bf16[16,16,1280]{2,1,0:T(8,128)(2,1)}, bf16[16,16,1280]{2,1,0:T(8,128)(2,1)}, bf16[16,16,1280]{2,1,0:T(8,128)(2,1)}) custom-call(bf16[64,32,1280]{2,1,0:T(8,128)(2,1)} %get-tuple-element.16.x_ref, bf16[8,1280,2560]{2,1,0:T(8,128)(2,1)} %wi_ref.3, bf16[8,2560,1280]{2,1,0:T(8,128)(2,1)} %wo_ref.3), custom_call_target="tpu_custom_call" | custom-call | flops 13421772800 | bytes 52428800 | tf_op jit(solution)/shard_map/ffn/pallas_call | solution.py:328
  153.2 1.5 collective-permute-start.25
  154.7 0.5 collective-permute-start.17
  155.2 1.5 collective-permute-start.16
  156.7 0.5 collective-permute-start.9
  157.3 0.0 collective-permute-done.24
  157.3 1.5 collective-permute-start.8
  158.8 0.2 add_convert_fusion.1.rest_0_
  158.9 12.1 %collective-permute-done.25 = bf16[16,16,1280]{2,1,0:T(8,128)(2,1)S(1)} collective-permute-done((bf16[16,16,1280]{2,1,0:T(8,128)(2,1)}, bf16[16,16,1280]{2,1,0:T(8,128)(2,1)S(1)}, u32[]{:S(2)}, u32[]{:S(2)}) %collective-permute-start.25) | collective-permute-done | bytes 655392 | tf_op jit(solution)/shard_map/ppermute | solution.py:409
  171.0 1.5 collective-permute-start.1
  172.5 0.2 add_convert_fusion.rest_1_
  172.7 12.4 %collective-permute-done.17 = bf16[16,16,1280]{2,1,0:T(8,128)(2,1)S(1)} collective-permute-done((bf16[16,16,1280]{2,1,0:T(8,128)(2,1)}, bf16[16,16,1280]{2,1,0:T(8,128)(2,1)S(1)}, u32[]{:S(2)}, u32[]{:S(2)}) %collective-permute-start.17) | collective-permute-done | bytes 655392 | tf_op jit(solution)/shard_map/ppermute | solution.py:409
  185.1 1.5 collective-permute-start
  186.6 0.2 add_convert_fusion.2.rest_1_
  186.7 12.4 %collective-permute-done.16 = bf16[16,16,1280]{2,1,0:T(8,128)(2,1)S(1)} collective-permute-done((bf16[16,16,1280]{2,1,0:T(8,128)(2,1)S(1)}, bf16[16,16,1280]{2,1,0:T(8,128)(2,1)S(1)}, u32[]{:S(2)}, u32[]{:S(2)}) %collective-permute-start.16) | collective-permute-done | bytes 655392 | tf_op jit(solution)/shard_map/ppermute | solution.py:409
  199.1 1.5 collective-permute-start.28
  200.6 12.6 %collective-permute-done.9 = bf16[16,16,1280]{2,1,0:T(8,128)(2,1)S(1)} collective-permute-done((bf16[16,16,1280]{2,1,0:T(8,128)(2,1)}, bf16[16,16,1280]{2,1,0:T(8,128)(2,1)S(1)}, u32[]{:S(2)}, u32[]{:S(2)}) %collective-permute-start.9) | collective-permute-done | bytes 655392 | tf_op jit(solution)/shard_map/ppermute | solution.py:409
  213.2 14.0 %collective-permute-done.8 = bf16[16,16,1280]{2,1,0:T(8,128)(2,1)S(1)} collective-permute-done((bf16[16,16,1280]{2,1,0:T(8,128)(2,1)S(1)}, bf16[16,16,1280]{2,1,0:T(8,128)(2,1)S(1)}, u32[]{:S(2)}, u32[]{:S(2)}) %collective-permute-start.8) | collective-permute-done | bytes 655392 | tf_op jit(solution)/shard_map/ppermute | solution.py:409
  227.2 1.5 collective-permute-start.29
  228.7 12.6 %collective-permute-done.1 = bf16[16,16,1280]{2,1,0:T(8,128)(2,1)S(1)} collective-permute-done((bf16[16,16,1280]{2,1,0:T(8,128)(2,1)S(1)}, bf16[16,16,1280]{2,1,0:T(8,128)(2,1)S(1)}, u32[]{:S(2)}, u32[]{:S(2)}) %collective-permute-start.1) | collective-permute-done | bytes 655392 | tf_op jit(solution)/shard_map/ppermute | solution.py:409
  241.2 0.2 add_convert_fusion.3.rest_0_
  241.4 11.9 %collective-permute-done = bf16[16,16,1280]{2,1,0:T(8,128)(2,1)S(1)} collective-permute-done((bf16[16,16,1280]{2,1,0:T(8,128)(2,1)S(1)}, bf16[16,16,1280]{2,1,0:T(8,128)(2,1)S(1)}, u32[]{:S(2)}, u32[]{:S(2)}) %collective-permute-start) | collective-permute-done | bytes 655392 | tf_op jit(solution)/shard_map/ppermute | solution.py:409
  253.3 1.6 collective-permute-start.21
  254.9 0.2 add_convert_fusion.4.rest_1_
  255.0 0.0 collective-permute-start.19
  255.1 0.5 collective-permute-start.20
  255.6 0.2 collective-permute-start.18
  255.8 0.9 copy-done.13
  256.6 1.6 collective-permute-start.13
  258.2 0.2 add_convert_fusion.5.rest_0_
  258.4 12.6 %collective-permute-done.21.rest_5_ = bf16[16,16,1280]{2,1,0:T(8,128)(2,1)} collective-permute-done((bf16[16,16,1280]{2,1,0:T(8,128)(2,1)S(1)}, bf16[16,16,1280]{2,1,0:T(8,128)(2,1)}, u32[]{:S(2)}, u32[]{:S(2)}) %collective-permute-start.21) | collective-permute-done | bytes 655392 | tf_op jit(solution)/shard_map/ppermute | solution.py:411
  271.0 1.6 collective-permute-start.12
  272.6 0.2 add_convert_fusion.6.rest_1_
  272.7 0.0 copy-start.25
  272.8 12.3 %collective-permute-done.20.rest_4_ = bf16[16,16,1280]{2,1,0:T(8,128)(2,1)} collective-permute-done((bf16[16,16,1280]{2,1,0:T(8,128)(2,1)S(1)}, bf16[16,16,1280]{2,1,0:T(8,128)(2,1)}, u32[]{:S(2)}, u32[]{:S(2)}) %collective-permute-start.20) | collective-permute-done | bytes 655392 | tf_op jit(solution)/shard_map/ppermute | solution.py:411
  285.0 0.5 collective-permute-start.10
  285.6 1.6 collective-permute-start.5
  287.1 11.9 %collective-permute-done.13.rest_5_ = bf16[16,16,1280]{2,1,0:T(8,128)(2,1)} collective-permute-done((bf16[16,16,1280]{2,1,0:T(8,128)(2,1)S(1)}, bf16[16,16,1280]{2,1,0:T(8,128)(2,1)}, u32[]{:S(2)}, u32[]{:S(2)}) %collective-permute-start.13) | collective-permute-done | bytes 655392 | tf_op jit(solution)/shard_map/ppermute | solution.py:411
  299.1 13.9 %collective-permute-done.12.rest_4_ = bf16[16,16,1280]{2,1,0:T(8,128)(2,1)S(1)} collective-permute-done((bf16[16,16,1280]{2,1,0:T(8,128)(2,1)S(1)}, bf16[16,16,1280]{2,1,0:T(8,128)(2,1)S(1)}, u32[]{:S(2)}, u32[]{:S(2)}) %collective-permute-start.12) | collective-permute-done | bytes 655392 | tf_op jit(solution)/shard_map/ppermute | solution.py:411
  313.0 1.0 add_convert_fusion.7.rest_0_
  314.1 0.8 copy-done.19
  314.9 1.6 collective-permute-start.4
  316.5 0.9 copy-done.21
  317.4 0.2 collective-permute-start.23
  317.6 9.5 %collective-permute-done.5.rest_5_ = bf16[16,16,1280]{2,1,0:T(8,128)(2,1)S(1)} collective-permute-done((bf16[16,16,1280]{2,1,0:T(8,128)(2,1)S(1)}, bf16[16,16,1280]{2,1,0:T(8,128)(2,1)S(1)}, u32[]{:S(2)}, u32[]{:S(2)}) %collective-permute-start.5) | collective-permute-done | bytes 655392 | tf_op jit(solution)/shard_map/ppermute | solution.py:411
  327.1 0.9 copy-done.23
  328.0 0.5 collective-permute-start.15
  328.4 0.1 collective-permute-start.14
  328.5 3.4 copy-done
  331.9 1.1 copy-done.6
  333.0 1.1 copy-done.10
  334.1 1.1 copy-done.14
  335.2 1.1 copy-done.24
  336.3 11.2 %combine.4.rest_8_ = bf16[64,512,1280]{2,1,0:T(8,128)(2,1)} custom-call(s32[64]{0:T(128)S(1)} %copy-done.25, s32[1]{0:T(128)} %bitcast.off_ref, bf16[64,512,128]{2,1,0:T(8,128)(2,1)S(1)} %copy-done, bf16[16,16,1280]{2,1,0:T(8,128)(2,1)S(1)} %add_convert_fusion.1.rest_0_, bf16[16,16,1280]{2,1,0:T(8,128)(2,1)S(1)} %add_convert_fusion.rest_1_, ...), custom_call_target="tpu_custom_call" | custom-call | flops 5368709120 | bytes 23068672 | tf_op jit(solution)/shard_map/combine/pallas_call | solution.py:377
  347.5 0.5 collective-permute-start.3
  348.0 0.0 collective-permute-start.2
  348.1 0.5 collective-permute-start.7
  348.6 0.0 collective-permute-start.6
  348.6 11.3 %combine.5.rest_8_ = bf16[64,512,1280]{2,1,0:T(8,128)(2,1)} custom-call(s32[64]{0:T(128)S(1)} %copy-done.25, s32[1]{0:T(128)} %bitcast.off_ref, bf16[64,512,128]{2,1,0:T(8,128)(2,1)S(1)} %copy-done, bf16[16,16,1280]{2,1,0:T(8,128)(2,1)S(1)} %add_convert_fusion.3.rest_0_, ...), custom_call_target="tpu_custom_call", output_to_operand_aliasing={{}: (11, {})} | custom-call | flops 5368709120 | bytes 23068672 | tf_op jit(solution)/shard_map/combine/pallas_call | solution.py:377
  360.0 11.1 %combine.6.rest_8_ = bf16[64,512,1280]{2,1,0:T(8,128)(2,1)} custom-call(s32[64]{0:T(128)S(1)} %copy-done.25, s32[1]{0:T(128)} %bitcast.off_ref, bf16[64,512,128]{2,1,0:T(8,128)(2,1)S(1)} %copy-done, bf16[16,16,1280]{2,1,0:T(8,128)(2,1)S(1)} %copy-done.4, bf16[16,16,1280]{2,1,0:T(8,128)(2,1)S(1)} %add_convert_fusion.4.rest_1_, ...), custom_call_target="tpu_custom_call", output_to_operand_aliasing={{}: (11, {})} | custom-call | flops 5368709120 | bytes 23068672 | tf_op jit(solution)/shard_map/combine/pallas_call | solution.py:377
  371.1 11.1 %combine.7 = bf16[64,512,1280]{2,1,0:T(8,128)(2,1)} custom-call(s32[64]{0:T(128)S(1)} %copy-done.25, s32[1]{0:T(128)} %bitcast.off_ref, bf16[64,512,128]{2,1,0:T(8,128)(2,1)S(1)} %copy-done, bf16[16,16,1280]{2,1,0:T(8,128)(2,1)} %add_convert_fusion.7.rest_0_, bf16[16,16,1280]{2,1,0:T(8,128)(2,1)S(1)} %copy-done.2, ...), custom_call_target="tpu_custom_call", output_to_operand_aliasing={{}: (11, {})} | custom-call | flops 5368709120 | bytes 23068672 | tf_op jit(solution)/shard_map/combine/pallas_call | solution.py:377
  (83 shorter events, 0.2 us)
Async XLA Ops:
  123.0 32.3 %copy-start.29 = (bf16[16,16,1280]{2,1,0:T(8,128)(2,1)S(1)}, bf16[16,16,1280]{2,1,0:T(8,128)(2,1)}, u32[]{:S(2)}) copy-start(bf16[16,16,1280]{2,1,0:T(8,128)(2,1)} %get-tuple-element.21) | copy-start | bytes 1966084
  123.0 34.3 %copy-start.27 = (bf16[16,16,1280]{2,1,0:T(8,128)(2,1)S(1)}, bf16[16,16,1280]{2,1,0:T(8,128)(2,1)}, u32[]{:S(2)}) copy-start(bf16[16,16,1280]{2,1,0:T(8,128)(2,1)} %get-tuple-element.19) | copy-start | bytes 1966084
  123.0 35.8 %copy-start.33 = (bf16[16,16,1280]{2,1,0:T(8,128)(2,1)S(1)}, bf16[16,16,1280]{2,1,0:T(8,128)(2,1)}, u32[]{:S(2)}) copy-start(bf16[16,16,1280]{2,1,0:T(8,128)(2,1)} %get-tuple-element.23) | copy-start | bytes 1966084
  123.0 34.3 %collective-permute-start.24 = (bf16[16,16,1280]{2,1,0:T(8,128)(2,1)}, bf16[16,16,1280]{2,1,0:T(8,128)(2,1)S(1)}, u32[]{:S(2)}, u32[]{:S(2)}) collective-permute-start(bf16[16,16,1280]{2,1,0:T(8,128)(2,1)} %get-tuple-element.23), channel_id=1, source_target_pairs={{0,4},{4,0},{1,5},{5,1},{2,6},{6,2},{3,7},{7,3}} | collective-permute-start | bytes 1966088 | tf_op jit(solution)/shard_map/ppermute | solution.py:409
  153.2 17.8 %copy-start.28 = (bf16[16,16,1280]{2,1,0:T(8,128)(2,1)S(1)}, bf16[16,16,1280]{2,1,0:T(8,128)(2,1)}, u32[]{:S(2)}) copy-start(bf16[16,16,1280]{2,1,0:T(8,128)(2,1)} %get-tuple-element.18) | copy-start | bytes 1966084
  153.2 19.3 %copy-start.32 = (bf16[16,16,1280]{2,1,0:T(8,128)(2,1)S(1)}, bf16[16,16,1280]{2,1,0:T(8,128)(2,1)}, u32[]{:S(2)}) copy-start(bf16[16,16,1280]{2,1,0:T(8,128)(2,1)} %get-tuple-element.24) | copy-start | bytes 1966084
  153.2 17.8 %collective-permute-start.25 = (bf16[16,16,1280]{2,1,0:T(8,128)(2,1)}, bf16[16,16,1280]{2,1,0:T(8,128)(2,1)S(1)}, u32[]{:S(2)}, u32[]{:S(2)}) collective-permute-start(bf16[16,16,1280]{2,1,0:T(8,128)(2,1)} %get-tuple-element.24), channel_id=1, source_target_pairs={{0,4},{4,0},{1,5},{5,1},{2,6},{6,2},{3,7},{7,3}} | collective-permute-start | bytes 1966088 | tf_op jit(solution)/shard_map/ppermute | solution.py:409
  154.7 30.4 %collective-permute-start.17 = (bf16[16,16,1280]{2,1,0:T(8,128)(2,1)}, bf16[16,16,1280]{2,1,0:T(8,128)(2,1)S(1)}, u32[]{:S(2)}, u32[]{:S(2)}) collective-permute-start(bf16[16,16,1280]{2,1,0:T(8,128)(2,1)} %get-tuple-element.22), channel_id=1, source_target_pairs={{0,4},{4,0},{1,5},{5,1},{2,6},{6,2},{3,7},{7,3}} | collective-permute-start | bytes 1966088 | tf_op jit(solution)/shard_map/ppermute | solution.py:409
  155.2 43.9 %collective-permute-start.16 = (bf16[16,16,1280]{2,1,0:T(8,128)(2,1)S(1)}, bf16[16,16,1280]{2,1,0:T(8,128)(2,1)S(1)}, u32[]{:S(2)}, u32[]{:S(2)}) collective-permute-start(bf16[16,16,1280]{2,1,0:T(8,128)(2,1)S(1)} %copy-done.29), channel_id=1, source_target_pairs={{0,4},{4,0},{1,5},{5,1},{2,6},{6,2},{3,7},{7,3}} | collective-permute-start | bytes 1966088 | tf_op jit(solution)/shard_map/ppermute | solution.py:409
  156.7 56.4 %collective-permute-start.9 = (bf16[16,16,1280]{2,1,0:T(8,128)(2,1)}, bf16[16,16,1280]{2,1,0:T(8,128)(2,1)S(1)}, u32[]{:S(2)}, u32[]{:S(2)}) collective-permute-start(bf16[16,16,1280]{2,1,0:T(8,128)(2,1)} %get-tuple-element.20), channel_id=1, source_target_pairs={{0,4},{4,0},{1,5},{5,1},{2,6},{6,2},{3,7},{7,3}} | collective-permute-start | bytes 1966088 | tf_op jit(solution)/shard_map/ppermute | solution.py:409
  157.3 69.9 %collective-permute-start.8 = (bf16[16,16,1280]{2,1,0:T(8,128)(2,1)S(1)}, bf16[16,16,1280]{2,1,0:T(8,128)(2,1)S(1)}, u32[]{:S(2)}, u32[]{:S(2)}) collective-permute-start(bf16[16,16,1280]{2,1,0:T(8,128)(2,1)S(1)} %copy-done.27), channel_id=1, source_target_pairs={{0,4},{4,0},{1,5},{5,1},{2,6},{6,2},{3,7},{7,3}} | collective-permute-start | bytes 1966088 | tf_op jit(solution)/shard_map/ppermute | solution.py:409
  158.9 26.2 %copy-start.26 = (bf16[16,16,1280]{2,1,0:T(8,128)(2,1)S(1)}, bf16[16,16,1280]{2,1,0:T(8,128)(2,1)}, u32[]{:S(2)}) copy-start(bf16[16,16,1280]{2,1,0:T(8,128)(2,1)} %get-tuple-element.17) | copy-start | bytes 1966084
  158.9 27.6 %copy-start.31 = (bf16[16,16,1280]{2,1,0:T(8,128)(2,1)S(1)}, bf16[16,16,1280]{2,1,0:T(8,128)(2,1)}, u32[]{:S(2)}) copy-start(bf16[16,16,1280]{2,1,0:T(8,128)(2,1)} %get-tuple-element.22) | copy-start | bytes 1966084
  171.0 70.2 %collective-permute-start.1 = (bf16[16,16,1280]{2,1,0:T(8,128)(2,1)S(1)}, bf16[16,16,1280]{2,1,0:T(8,128)(2,1)S(1)}, u32[]{:S(2)}, u32[]{:S(2)}) collective-permute-start(bf16[16,16,1280]{2,1,0:T(8,128)(2,1)S(1)} %copy-done.28), channel_id=1, source_target_pairs={{0,4},{4,0},{1,5},{5,1},{2,6},{6,2},{3,7},{7,3}} | collective-permute-start | bytes 1966088 | tf_op jit(solution)/shard_map/ppermute | solution.py:409
  185.1 68.2 %collective-permute-start = (bf16[16,16,1280]{2,1,0:T(8,128)(2,1)S(1)}, bf16[16,16,1280]{2,1,0:T(8,128)(2,1)S(1)}, u32[]{:S(2)}, u32[]{:S(2)}) collective-permute-start(bf16[16,16,1280]{2,1,0:T(8,128)(2,1)S(1)} %copy-done.26), channel_id=1, source_target_pairs={{0,4},{4,0},{1,5},{5,1},{2,6},{6,2},{3,7},{7,3}} | collective-permute-start | bytes 1966088 | tf_op jit(solution)/shard_map/ppermute | solution.py:409
  186.7 68.2 %copy-start.30 = (bf16[16,16,1280]{2,1,0:T(8,128)(2,1)S(1)}, bf16[16,16,1280]{2,1,0:T(8,128)(2,1)}, u32[]{:S(2)}) copy-start(bf16[16,16,1280]{2,1,0:T(8,128)(2,1)} %get-tuple-element.20) | copy-start | bytes 1966084
  199.1 55.9 %collective-permute-start.28 = (bf16[16,16,1280]{2,1,0:T(8,128)(2,1)S(1)}, bf16[16,16,1280]{2,1,0:T(8,128)(2,1)S(1)}, u32[]{:S(2)}, u32[]{:S(2)}) collective-permute-start(bf16[16,16,1280]{2,1,0:T(8,128)(2,1)S(1)} %add_convert_fusion.1.rest_0_), channel_id=1, source_target_pairs={{0,2},{1,3},{2,0},{3,1},{4,6},{5,7},{6,4},{7,5}} | collective-permute-start | bytes 1966088 | tf_op jit(solution)/shard_map/ppermute | solution.py:411
  213.2 42.4 %collective-permute-start.26 = (bf16[16,16,1280]{2,1,0:T(8,128)(2,1)S(1)}, bf16[16,16,1280]{2,1,0:T(8,128)(2,1)S(1)}, u32[]{:S(2)}, u32[]{:S(2)}) collective-permute-start(bf16[16,16,1280]{2,1,0:T(8,128)(2,1)S(1)} %add_convert_fusion.1.rest_0_), channel_id=1, source_target_pairs={{0,1},{1,0},{2,3},{3,2},{4,5},{5,4},{6,7},{7,6}} | collective-permute-start | bytes 1966088 | tf_op jit(solution)/shard_map/ppermute | solution.py:413
  227.2 27.9 %collective-permute-start.29 = (bf16[16,16,1280]{2,1,0:T(8,128)(2,1)S(1)}, bf16[16,16,1280]{2,1,0:T(8,128)(2,1)}, u32[]{:S(2)}, u32[]{:S(2)}) collective-permute-start(bf16[16,16,1280]{2,1,0:T(8,128)(2,1)S(1)} %add_convert_fusion.rest_1_), channel_id=1, source_target_pairs={{0,2},{1,3},{2,0},{3,1},{4,6},{5,7},{6,4},{7,5}} | collective-permute-start | bytes 1966088 | tf_op jit(solution)/shard_map/ppermute | solution.py:411
  241.2 14.5 %collective-permute-start.27 = (bf16[16,16,1280]{2,1,0:T(8,128)(2,1)S(1)}, bf16[16,16,1280]{2,1,0:T(8,128)(2,1)S(1)}, u32[]{:S(2)}, u32[]{:S(2)}) collective-permute-start(bf16[16,16,1280]{2,1,0:T(8,128)(2,1)S(1)} %add_convert_fusion.rest_1_), channel_id=1, source_target_pairs={{0,1},{1,0},{2,3},{3,2},{4,5},{5,4},{6,7},{7,6}} | collective-permute-start | bytes 1966088 | tf_op jit(solution)/shard_map/ppermute | solution.py:413
  253.3 17.7 %collective-permute-start.21 = (bf16[16,16,1280]{2,1,0:T(8,128)(2,1)S(1)}, bf16[16,16,1280]{2,1,0:T(8,128)(2,1)}, u32[]{:S(2)}, u32[]{:S(2)}) collective-permute-start(bf16[16,16,1280]{2,1,0:T(8,128)(2,1)S(1)} %add_convert_fusion.2.rest_1_), channel_id=1, source_target_pairs={{0,2},{1,3},{2,0},{3,1},{4,6},{5,7},{6,4},{7,5}} | collective-permute-start | bytes 1966088 | tf_op jit(solution)/shard_map/ppermute | solution.py:411
  255.0 44.0 %copy-start.5 = (bf16[16,16,1280]{2,1,0:T(8,128)(2,1)}, bf16[16,16,1280]{2,1,0:T(8,128)(2,1)S(1)}, u32[]{:S(2)}) copy-start(bf16[16,16,1280]{2,1,0:T(8,128)(2,1)S(1)} %collective-permute-done.28.rest_4_) | copy-start | bytes 1966084
  255.0 30.0 %collective-permute-start.19 = (bf16[16,16,1280]{2,1,0:T(8,128)(2,1)S(1)}, bf16[16,16,1280]{2,1,0:T(8,128)(2,1)S(1)}, u32[]{:S(2)}, u32[]{:S(2)}) collective-permute-start(bf16[16,16,1280]{2,1,0:T(8,128)(2,1)S(1)} %add_convert_fusion.2.rest_1_), channel_id=1, source_target_pairs={{0,1},{1,0},{2,3},{3,2},{4,5},{5,4},{6,7},{7,6}} | collective-permute-start | bytes 1966088 | tf_op jit(solution)/shard_map/ppermute | solution.py:413
  255.1 29.9 %collective-permute-start.20 = (bf16[16,16,1280]{2,1,0:T(8,128)(2,1)S(1)}, bf16[16,16,1280]{2,1,0:T(8,128)(2,1)}, u32[]{:S(2)}, u32[]{:S(2)}) collective-permute-start(bf16[16,16,1280]{2,1,0:T(8,128)(2,1)S(1)} %add_convert_fusion.3.rest_0_), channel_id=1, source_target_pairs={{0,2},{1,3},{2,0},{3,1},{4,6},{5,7},{6,4},{7,5}} | collective-permute-start | bytes 1966088 | tf_op jit(solution)/shard_map/ppermute | solution.py:411
  255.6 15.4 %copy-start.9 = (bf16[16,16,1280]{2,1,0:T(8,128)(2,1)}, bf16[16,16,1280]{2,1,0:T(8,128)(2,1)S(1)}, u32[]{:S(2)}) copy-start(bf16[16,16,1280]{2,1,0:T(8,128)(2,1)S(1)} %collective-permute-done.26.rest_2_) | copy-start | bytes 1966084
  255.6 30.0 %collective-permute-start.18 = (bf16[16,16,1280]{2,1,0:T(8,128)(2,1)S(1)}, bf16[16,16,1280]{2,1,0:T(8,128)(2,1)S(1)}, u32[]{:S(2)}, u32[]{:S(2)}) collective-permute-start(bf16[16,16,1280]{2,1,0:T(8,128)(2,1)S(1)} %add_convert_fusion.3.rest_0_), channel_id=1, source_target_pairs={{0,1},{1,0},{2,3},{3,2},{4,5},{5,4},{6,7},{7,6}} | collective-permute-start | bytes 1966088 | tf_op jit(solution)/shard_map/ppermute | solution.py:413
  255.7 0.9 copy-start.13
  256.6 42.4 %collective-permute-start.13 = (bf16[16,16,1280]{2,1,0:T(8,128)(2,1)S(1)}, bf16[16,16,1280]{2,1,0:T(8,128)(2,1)}, u32[]{:S(2)}, u32[]{:S(2)}) collective-permute-start(bf16[16,16,1280]{2,1,0:T(8,128)(2,1)S(1)} %add_convert_fusion.4.rest_1_), channel_id=1, source_target_pairs={{0,2},{1,3},{2,0},{3,1},{4,6},{5,7},{6,4},{7,5}} | collective-permute-start | bytes 1966088 | tf_op jit(solution)/shard_map/ppermute | solution.py:411
  258.4 55.7 %copy-start.3 = (bf16[16,16,1280]{2,1,0:T(8,128)(2,1)}, bf16[16,16,1280]{2,1,0:T(8,128)(2,1)S(1)}, u32[]{:S(2)}) copy-start(bf16[16,16,1280]{2,1,0:T(8,128)(2,1)S(1)} %add_convert_fusion.5.rest_0_) | copy-start | bytes 1966084
  271.0 42.0 %collective-permute-start.12 = (bf16[16,16,1280]{2,1,0:T(8,128)(2,1)S(1)}, bf16[16,16,1280]{2,1,0:T(8,128)(2,1)S(1)}, u32[]{:S(2)}, u32[]{:S(2)}) collective-permute-start(bf16[16,16,1280]{2,1,0:T(8,128)(2,1)S(1)} %add_convert_fusion.5.rest_0_), channel_id=1, source_target_pairs={{0,2},{1,3},{2,0},{3,1},{4,6},{5,7},{6,4},{7,5}} | collective-permute-start | bytes 1966088 | tf_op jit(solution)/shard_map/ppermute | solution.py:411
  272.7 41.3 %copy-start.1 = (bf16[16,16,1280]{2,1,0:T(8,128)(2,1)}, bf16[16,16,1280]{2,1,0:T(8,128)(2,1)S(1)}, u32[]{:S(2)}) copy-start(bf16[16,16,1280]{2,1,0:T(8,128)(2,1)S(1)} %add_convert_fusion.6.rest_1_) | copy-start | bytes 1966084
  272.7 55.8 %copy-start.25 = (s32[64]{0:T(128)S(1)}, s32[64]{0:T(128)}, u32[]{:S(2)}) copy-start(s32[64]{0:T(128)} %len_ref.9) | copy-start | bytes 772
  285.0 29.0 %collective-permute-start.11 = (bf16[16,16,1280]{2,1,0:T(8,128)(2,1)S(1)}, bf16[16,16,1280]{2,1,0:T(8,128)(2,1)S(1)}, u32[]{:S(2)}, u32[]{:S(2)}) collective-permute-start(bf16[16,16,1280]{2,1,0:T(8,128)(2,1)S(1)} %add_convert_fusion.4.rest_1_), channel_id=1, source_target_pairs={{0,1},{1,0},{2,3},{3,2},{4,5},{5,4},{6,7},{7,6}} | collective-permute-start | bytes 1966088 | tf_op jit(solution)/shard_map/ppermute | solution.py:413
  285.0 42.0 %copy-start.7 = (bf16[16,16,1280]{2,1,0:T(8,128)(2,1)}, bf16[16,16,1280]{2,1,0:T(8,128)(2,1)S(1)}, u32[]{:S(2)}) copy-start(bf16[16,16,1280]{2,1,0:T(8,128)(2,1)S(1)} %collective-permute-done.19.rest_3_) | copy-start | bytes 1966084
  285.0 31.5 %collective-permute-start.10 = (bf16[16,16,1280]{2,1,0:T(8,128)(2,1)S(1)}, bf16[16,16,1280]{2,1,0:T(8,128)(2,1)S(1)}, u32[]{:S(2)}, u32[]{:S(2)}) collective-permute-start(bf16[16,16,1280]{2,1,0:T(8,128)(2,1)S(1)} %add_convert_fusion.5.rest_0_), channel_id=1, source_target_pairs={{0,1},{1,0},{2,3},{3,2},{4,5},{5,4},{6,7},{7,6}} | collective-permute-start | bytes 1966088 | tf_op jit(solution)/shard_map/ppermute | solution.py:413
  285.5 42.9 %copy-start.11 = (bf16[16,16,1280]{2,1,0:T(8,128)(2,1)}, bf16[16,16,1280]{2,1,0:T(8,128)(2,1)S(1)}, u32[]{:S(2)}) copy-start(bf16[16,16,1280]{2,1,0:T(8,128)(2,1)S(1)} %collective-permute-done.18.rest_2_) | copy-start | bytes 1966084
  285.6 41.5 %collective-permute-start.5 = (bf16[16,16,1280]{2,1,0:T(8,128)(2,1)S(1)}, bf16[16,16,1280]{2,1,0:T(8,128)(2,1)S(1)}, u32[]{:S(2)}, u32[]{:S(2)}) collective-permute-start(bf16[16,16,1280]{2,1,0:T(8,128)(2,1)S(1)} %add_convert_fusion.6.rest_1_), channel_id=1, source_target_pairs={{0,2},{1,3},{2,0},{3,1},{4,6},{5,7},{6,4},{7,5}} | collective-permute-start | bytes 1966088 | tf_op jit(solution)/shard_map/ppermute | solution.py:411
  299.1 28.0 %collective-permute-start.30 = (bf16[16,16,1280]{2,1,0:T(8,128)(2,1)S(1)}, bf16[16,16,1280]{2,1,0:T(8,128)(2,1)S(1)}, u32[]{:S(2)}, u32[]{:S(2)}) collective-permute-start(bf16[16,16,1280]{2,1,0:T(8,128)(2,1)S(1)} %collective-permute-done.28.rest_4_), channel_id=1, source_target_pairs={{0,1},{1,0},{2,3},{3,2},{4,5},{5,4},{6,7},{7,6}} | collective-permute-start | bytes 1966088 | tf_op jit(solution)/shard_map/ppermute | solution.py:415
  313.0 15.4 %copy-start.15 = (bf16[16,16,1280]{2,1,0:T(8,128)(2,1)}, bf16[16,16,1280]{2,1,0:T(8,128)(2,1)S(1)}, u32[]{:S(2)}) copy-start(bf16[16,16,1280]{2,1,0:T(8,128)(2,1)S(1)} %collective-permute-done.12.rest_4_) | copy-start | bytes 1966084
  313.0 15.4 %collective-permute-start.31 = (bf16[16,16,1280]{2,1,0:T(8,128)(2,1)}, bf16[16,16,1280]{2,1,0:T(8,128)(2,1)}, u32[]{:S(2)}, u32[]{:S(2)}) collective-permute-start(bf16[16,16,1280]{2,1,0:T(8,128)(2,1)} %collective-permute-done.29.rest_5_), channel_id=1, source_target_pairs={{0,1},{1,0},{2,3},{3,2},{4,5},{5,4},{6,7},{7,6}} | collective-permute-start | bytes 1966088 | tf_op jit(solution)/shard_map/ppermute | solution.py:415
  314.9 32.6 %collective-permute-start.4 = (bf16[16,16,1280]{2,1,0:T(8,128)(2,1)}, bf16[16,16,1280]{2,1,0:T(8,128)(2,1)}, u32[]{:S(2)}, u32[]{:S(2)}) collective-permute-start(bf16[16,16,1280]{2,1,0:T(8,128)(2,1)} %add_convert_fusion.7.rest_0_), channel_id=1, source_target_pairs={{0,2},{1,3},{2,0},{3,1},{4,6},{5,7},{6,4},{7,5}} | collective-permute-start | bytes 1966088 | tf_op jit(solution)/shard_map/ppermute | solution.py:411
  317.4 30.7 %collective-permute-start.23 = (bf16[16,16,1280]{2,1,0:T(8,128)(2,1)}, bf16[16,16,1280]{2,1,0:T(8,128)(2,1)}, u32[]{:S(2)}, u32[]{:S(2)}) collective-permute-start(bf16[16,16,1280]{2,1,0:T(8,128)(2,1)} %collective-permute-done.21.rest_5_), channel_id=1, source_target_pairs={{0,1},{1,0},{2,3},{3,2},{4,5},{5,4},{6,7},{7,6}} | collective-permute-start | bytes 1966088 | tf_op jit(solution)/shard_map/ppermute | solution.py:415
  327.1 1.4 copy-start.17
  327.1 21.0 %collective-permute-start.22 = (bf16[16,16,1280]{2,1,0:T(8,128)(2,1)}, bf16[16,16,1280]{2,1,0:T(8,128)(2,1)}, u32[]{:S(2)}, u32[]{:S(2)}) collective-permute-start(bf16[16,16,1280]{2,1,0:T(8,128)(2,1)} %collective-permute-done.20.rest_4_), channel_id=1, source_target_pairs={{0,1},{1,0},{2,3},{3,2},{4,5},{5,4},{6,7},{7,6}} | collective-permute-start | bytes 1966088 | tf_op jit(solution)/shard_map/ppermute | solution.py:415
  327.1 0.9 copy-start.23
  328.0 20.6 %collective-permute-start.15 = (bf16[16,16,1280]{2,1,0:T(8,128)(2,1)}, bf16[16,16,1280]{2,1,0:T(8,128)(2,1)}, u32[]{:S(2)}, u32[]{:S(2)}) collective-permute-start(bf16[16,16,1280]{2,1,0:T(8,128)(2,1)} %collective-permute-done.13.rest_5_), channel_id=1, source_target_pairs={{0,1},{1,0},{2,3},{3,2},{4,5},{5,4},{6,7},{7,6}} | collective-permute-start | bytes 1966088 | tf_op jit(solution)/shard_map/ppermute | solution.py:415
  328.4 31.5 %collective-permute-start.14 = (bf16[16,16,1280]{2,1,0:T(8,128)(2,1)}, bf16[16,16,1280]{2,1,0:T(8,128)(2,1)S(1)}, u32[]{:S(2)}, u32[]{:S(2)}) collective-permute-start(bf16[16,16,1280]{2,1,0:T(8,128)(2,1)} %copy-done.15), channel_id=1, source_target_pairs={{0,1},{1,0},{2,3},{3,2},{4,5},{5,4},{6,7},{7,6}} | collective-permute-start | bytes 1966088 | tf_op jit(solution)/shard_map/ppermute | solution.py:415
  328.5 3.4 copy-start
  331.9 1.1 copy-start.6
  333.0 1.1 copy-start.10
  334.1 1.1 copy-start.14
  335.2 1.1 copy-start.24
  336.2 11.3 %copy-start.2 = (bf16[16,16,1280]{2,1,0:T(8,128)(2,1)S(1)}, bf16[16,16,1280]{2,1,0:T(8,128)(2,1)}, u32[]{:S(2)}) copy-start(bf16[16,16,1280]{2,1,0:T(8,128)(2,1)} %copy-done.1) | copy-start | bytes 1966084
  336.2 11.8 %copy-start.18 = (bf16[16,16,1280]{2,1,0:T(8,128)(2,1)S(1)}, bf16[16,16,1280]{2,1,0:T(8,128)(2,1)}, u32[]{:S(2)}) copy-start(bf16[16,16,1280]{2,1,0:T(8,128)(2,1)} %copy-done.17) | copy-start | bytes 1966084
  336.2 12.4 %copy-start.8 = (bf16[16,16,1280]{2,1,0:T(8,128)(2,1)S(1)}, bf16[16,16,1280]{2,1,0:T(8,128)(2,1)}, u32[]{:S(2)}) copy-start(bf16[16,16,1280]{2,1,0:T(8,128)(2,1)} %copy-done.7) | copy-start | bytes 1966084
  336.2 12.4 %copy-start.12 = (bf16[16,16,1280]{2,1,0:T(8,128)(2,1)S(1)}, bf16[16,16,1280]{2,1,0:T(8,128)(2,1)}, u32[]{:S(2)}) copy-start(bf16[16,16,1280]{2,1,0:T(8,128)(2,1)} %copy-done.11) | copy-start | bytes 1966084
  347.5 12.4 %copy-start.4 = (bf16[16,16,1280]{2,1,0:T(8,128)(2,1)S(1)}, bf16[16,16,1280]{2,1,0:T(8,128)(2,1)}, u32[]{:S(2)}) copy-start(bf16[16,16,1280]{2,1,0:T(8,128)(2,1)} %copy-done.3) | copy-start | bytes 1966084
  347.5 12.4 %copy-start.16 = (bf16[16,16,1280]{2,1,0:T(8,128)(2,1)S(1)}, bf16[16,16,1280]{2,1,0:T(8,128)(2,1)}, u32[]{:S(2)}) copy-start(bf16[16,16,1280]{2,1,0:T(8,128)(2,1)} %copy-done.15) | copy-start | bytes 1966084
  347.5 12.5 %copy-start.20 = (bf16[16,16,1280]{2,1,0:T(8,128)(2,1)S(1)}, bf16[16,16,1280]{2,1,0:T(8,128)(2,1)}, u32[]{:S(2)}) copy-start(bf16[16,16,1280]{2,1,0:T(8,128)(2,1)} %copy-done.19) | copy-start | bytes 1966084
  347.5 12.5 %copy-start.22 = (bf16[16,16,1280]{2,1,0:T(8,128)(2,1)S(1)}, bf16[16,16,1280]{2,1,0:T(8,128)(2,1)}, u32[]{:S(2)}) copy-start(bf16[16,16,1280]{2,1,0:T(8,128)(2,1)} %copy-done.21) | copy-start | bytes 1966084
  347.5 23.5 %collective-permute-start.3 = (bf16[16,16,1280]{2,1,0:T(8,128)(2,1)S(1)}, bf16[16,16,1280]{2,1,0:T(8,128)(2,1)S(1)}, u32[]{:S(2)}, u32[]{:S(2)}) collective-permute-start(bf16[16,16,1280]{2,1,0:T(8,128)(2,1)S(1)} %copy-done.2), channel_id=1, source_target_pairs={{0,1},{1,0},{2,3},{3,2},{4,5},{5,4},{6,7},{7,6}} | collective-permute-start | bytes 1966088 | tf_op jit(solution)/shard_map/ppermute | solution.py:413
  348.0 23.0 %collective-permute-start.2 = (bf16[16,16,1280]{2,1,0:T(8,128)(2,1)}, bf16[16,16,1280]{2,1,0:T(8,128)(2,1)S(1)}, u32[]{:S(2)}, u32[]{:S(2)}) collective-permute-start(bf16[16,16,1280]{2,1,0:T(8,128)(2,1)} %add_convert_fusion.7.rest_0_), channel_id=1, source_target_pairs={{0,1},{1,0},{2,3},{3,2},{4,5},{5,4},{6,7},{7,6}} | collective-permute-start | bytes 1966088 | tf_op jit(solution)/shard_map/ppermute | solution.py:413
  348.1 23.0 %collective-permute-start.7 = (bf16[16,16,1280]{2,1,0:T(8,128)(2,1)S(1)}, bf16[16,16,1280]{2,1,0:T(8,128)(2,1)S(1)}, u32[]{:S(2)}, u32[]{:S(2)}) collective-permute-start(bf16[16,16,1280]{2,1,0:T(8,128)(2,1)S(1)} %copy-done.18), channel_id=1, source_target_pairs={{0,1},{1,0},{2,3},{3,2},{4,5},{5,4},{6,7},{7,6}} | collective-permute-start | bytes 1966088 | tf_op jit(solution)/shard_map/ppermute | solution.py:415
  348.6 22.5 %collective-permute-start.6 = (bf16[16,16,1280]{2,1,0:T(8,128)(2,1)}, bf16[16,16,1280]{2,1,0:T(8,128)(2,1)S(1)}, u32[]{:S(2)}, u32[]{:S(2)}) collective-permute-start(bf16[16,16,1280]{2,1,0:T(8,128)(2,1)} %collective-permute-done.4.rest_4_), channel_id=1, source_target_pairs={{0,1},{1,0},{2,3},{3,2},{4,5},{5,4},{6,7},{7,6}} | collective-permute-start | bytes 1966088 | tf_op jit(solution)/shard_map/ppermute | solution.py:415
  (2 other events, 1.7 us)

commit v2 on v1

--- a/solution.py
+++ b/solution.py
@@ -11,19 +11,98 @@
 NORM_EPS = 1e-6
 NEG = -1e30
 MESH = pl.DeviceIdType.MESH
-CHUNK_SEQS = 4
+CHUNK_SEQS = 2
+LEAD = 4
+LATE_EVERY = 1
+IN_DISPATCH = 16
+MIX_CALLS = 2
+MIX_SEQS = 2
 X_SLOTS = 6
 C_SLOTS = 8
 ROW_BLOCK = 256
-HIDDEN_TILE = 2560
-SUB_TILE = 256
+HIDDEN_TILE = 1280
 LANES = 128
-GROUPS = 2
-BATCH_CHUNKS = 4
+GROUPS = 4
+CHUNKS = (2, 2, 2, 4)
+MIX_CHUNKS = 4
 COMBINE_SEQS = 4
 
 
-def dispatch_kernel(n_half, n_tok, dim, n_slots, per_dev, phi_ref, len_ref, g_ref, x_hbm, xs_hbm, c_hbm,
+def slot_units(phi, s, per_dev):
+    n_slots = phi.shape[1]
+    p32 = phi.astype(jnp.float32)
+    unit = (p32 * lax.rsqrt(jnp.sum(p32 * p32, axis=0, keepdims=True) + NORM_EPS)).astype(jnp.bfloat16)
+    row = lax.broadcasted_iota(jnp.int32, (n_slots, n_slots), 0)
+    col = lax.broadcasted_iota(jnp.int32, (n_slots, n_slots), 1)
+    pick = jnp.where(row == jnp.bitwise_xor(col, s * per_dev), 1.0, 0.0).astype(jnp.bfloat16)
+    return jnp.dot(unit, pick, preferred_element_type=jnp.float32).astype(jnp.bfloat16)
+
+
+def logit_block(x_ref, dots, g, r):
+    rows = pl.ds(r * ROW_BLOCK, ROW_BLOCK)
+    square = jnp.zeros((ROW_BLOCK, LANES), jnp.float32)
+    for c in range(x_ref.shape[1] // LANES):
+        x32 = x_ref[rows, c * LANES:(c + 1) * LANES].astype(jnp.float32)
+        square += x32 * x32
+    scale = lax.rsqrt(jnp.sum(square, axis=1, keepdims=True) + NORM_EPS)
+    return jnp.where(scale > 0.0, dots[r * ROW_BLOCK:(r + 1) * ROW_BLOCK] * (g * scale), 0.0)
+
+
+def mix_block(lg, first_pos, length):
+    e = jnp.exp(lg - jnp.max(lg, axis=1, keepdims=True))
+    mix = e * (1.0 / jnp.sum(e, axis=1, keepdims=True))
+    pos = first_pos + lax.broadcasted_iota(jnp.int32, (lg.shape[0], 1), 0)
+    return jnp.where(pos < length, mix, 0.0).astype(jnp.bfloat16)
+
+
+def mix_kernel(per_dev, seqs, idx_ref, len_ref, phi_ref, g_ref, x_ref, _, c_ref, v_ref):
+    s = idx_ref[0]
+    i = pl.program_id(0)
+
+    @pl.when(i == 0)
+    def _():
+        v_ref[...] = slot_units(phi_ref[...], s, per_dev)
+
+    n_tok = x_ref.shape[1]
+    for j in range(seqs):
+        length = len_ref[(idx_ref[1] + i) * seqs + j]
+        dots = jnp.dot(x_ref[j], v_ref[...], preferred_element_type=jnp.float32)
+        for r in range(n_tok // ROW_BLOCK):
+            lg = logit_block(x_ref.at[j], dots, g_ref[0], r)
+            c_ref[j, r * ROW_BLOCK:(r + 1) * ROW_BLOCK, :] = mix_block(lg, s * n_tok + r * ROW_BLOCK, length)
+
+
+def mix_weights(part, tokens, lengths, phi, scale, per_dev, mix):
+    batch, n_tok, dim = tokens.shape
+    n_slots = phi.shape[1]
+    count = (batch // 2 - IN_DISPATCH) // MIX_CALLS
+    seqs = MIX_SEQS
+    start = lax.rem(lax.axis_index("model") * (batch // 2) + batch // 2 + IN_DISPATCH + part * count, batch)
+    index = jnp.stack([lax.axis_index("seq"), start // seqs]).astype(jnp.int32)
+    block = lambda i, idx, _: (idx[1] + i, 0, 0)
+    return pl.pallas_call(
+        functools.partial(mix_kernel, per_dev, seqs),
+        grid_spec=pltpu.PrefetchScalarGridSpec(
+            num_scalar_prefetch=2,
+            grid=(count // seqs,),
+            in_specs=[
+                pl.BlockSpec((dim, n_slots), lambda i, *_: (0, 0)),
+                pl.BlockSpec(memory_space=pltpu.SMEM),
+                pl.BlockSpec((seqs, n_tok, dim), block),
+                pl.BlockSpec(memory_space=pl.ANY),
+            ],
+            out_specs=pl.BlockSpec((seqs, n_tok, n_slots), block),
+            scratch_shapes=[pltpu.VMEM((dim, n_slots), jnp.bfloat16)],
+        ),
+        out_shape=jax.ShapeDtypeStruct(mix.shape, mix.dtype),
+        input_output_aliases={5: 0},
+        compiler_params=pltpu.CompilerParams(dimension_semantics=("arbitrary",), vmem_limit_bytes=32 * 1024 * 1024),
+        cost_estimate=pl.CostEstimate(flops=4 * count * n_tok * n_slots * dim, bytes_accessed=2 * count * n_tok * dim, transcendentals=0),
+        name="mix",
+    )(index, lengths, phi, scale, tokens, mix)
+
+
+def dispatch_kernel(n_half, n_tok, n_slots, per_dev, phi_ref, len_ref, g_ref, x_hbm, xs_hbm, c_hbm,
                     v_ref, xbuf, lbuf, cbuf, sbuf, lse1, r1, lr1, m0, s2, lse2, r2, lr2, xso,
                     xsem, csem, osem, s1_sem, r1_sem, s2_sem, r2_sem, s3_sem, r3_sem):
     s = lax.axis_index("seq")
@@ -33,6 +112,8 @@
     y_peer = {"model": 1 - m}
     cs = CHUNK_SEQS
     n = n_half // cs
+    total = n_half + IN_DISPATCH
+    steps = total // cs
 
     barrier = pltpu.get_barrier_semaphore()
     for peer in (core_peer, x_peer, y_peer):
@@ -52,13 +133,7 @@
     for t in range(X_SLOTS - 1):
         x_copy(t).start()
 
-    phi = phi_ref[...].astype(jnp.float32)
-    unit = (phi * lax.rsqrt(jnp.sum(phi * phi, axis=0, keepdims=True) + NORM_EPS)).astype(jnp.bfloat16)
-    row = lax.broadcasted_iota(jnp.int32, (n_slots, n_slots), 0)
-    col = lax.broadcasted_iota(jnp.int32, (n_slots, n_slots), 1)
-    target = jnp.bitwise_xor(col, s * per_dev)
-    pick = jnp.where(row == target, 1.0, 0.0).astype(jnp.bfloat16)
-    v_ref[...] = jnp.dot(unit, pick, preferred_element_type=jnp.float32).astype(jnp.bfloat16)
+    v_ref[...] = slot_units(phi_ref[...], s, per_dev)
     lse1[...] = jnp.zeros_like(lse1)
     g = g_ref[0]
 
@@ -69,7 +144,7 @@
         cslot = lax.rem(t, C_SLOTS)
         length = len_ref[batch_of(t)]
 
-        @pl.when(t + X_SLOTS - 1 < 2 * n_half)
+        @pl.when(t + X_SLOTS - 1 < total)
         def _():
             x_copy(t + X_SLOTS - 1).start()
 
@@ -82,18 +157,9 @@
         dots = jnp.dot(xbuf[xslot], v_ref[...], preferred_element_type=jnp.float32)
         for r in range(n_tok // ROW_BLOCK):
             rows = pl.ds(r * ROW_BLOCK, ROW_BLOCK)
-            square = jnp.zeros((ROW_BLOCK, LANES), jnp.float32)
-            for c in range(dim // LANES):
-                x32 = xbuf[xslot, rows, c * LANES:(c + 1) * LANES].astype(jnp.float32)
-                square += x32 * x32
-            scale = lax.rsqrt(jnp.sum(square, axis=1, keepdims=True) + NORM_EPS)
-            block = dots[r * ROW_BLOCK:(r + 1) * ROW_BLOCK]
-            lg = jnp.where(scale > 0.0, block * (g * scale), 0.0)
+            lg = logit_block(xbuf.at[xslot], dots, g, r)
             lbuf[rows, :] = lg
-            e = jnp.exp(lg - jnp.max(lg, axis=1, keepdims=True))
-            mix = e * (1.0 / jnp.sum(e, axis=1, keepdims=True))
-            pos = s * n_tok + r * ROW_BLOCK + lax.broadcasted_iota(jnp.int32, (ROW_BLOCK, 1), 0)
-            cbuf[cslot, rows, :] = jnp.where(pos < length, mix, 0.0).astype(jnp.bfloat16)
+            cbuf[cslot, rows, :] = mix_block(lg, s * n_tok + r * ROW_BLOCK, length)
         c_copy(t).start()
         return xslot, length
 
@@ -169,11 +235,10 @@
         d3(k).start()
         keep(k).start()
 
-    lead = 4
-    early = n - lead
-    late = n // 2 - 1
-
-    @pl.loop(0, 2 * n)
+    early = n - LEAD
+    late = min(LEAD, (steps - n) // LATE_EVERY)
+
+    @pl.loop(0, steps)
     def _(k):
         @pl.when(k < n)
         def _():
@@ -194,19 +259,19 @@
         def _():
             merge1(k - 1)
 
-        @pl.when((k >= lead) & (k < n))
-        def _():
-            merge2(k - lead)
-
-        @pl.when((k > n) & (lax.rem(k - n, 2) == 1) & ((k - n) // 2 < late))
-        def _():
-            merge2(early + (k - n) // 2)
+        @pl.when((k >= LEAD) & (k < n))
+        def _():
+            merge2(k - LEAD)
+
+        @pl.when((k >= n) & (lax.rem(k - n, LATE_EVERY) == 0) & ((k - n) // LATE_EVERY < late))
+        def _():
+            merge2(early + (k - n) // LATE_EVERY)
 
     @pl.loop(early + late, n)
     def _(k):
         merge2(k)
 
-    @pl.loop(2 * n_half - C_SLOTS, 2 * n_half)
+    @pl.loop(total - C_SLOTS, total)
     def _(t):
         c_copy(t).wait()
 
@@ -227,7 +292,7 @@
     n = half // CHUNK_SEQS
     bf, f32 = jnp.bfloat16, jnp.float32
     return pl.pallas_call(
-        functools.partial(dispatch_kernel, half, n_tok, dim, n_slots, per_dev),
+        functools.partial(dispatch_kernel, half, n_tok, n_slots, per_dev),
         out_shape=(jax.ShapeDtypeStruct((batch, per_dev, dim), bf), jax.ShapeDtypeStruct((batch, n_tok, n_slots), bf)),
         in_specs=[
             pl.BlockSpec(memory_space=pltpu.VMEM),
@@ -266,17 +331,18 @@
     )(phi, lengths, scale, tokens)
 
 
-def ffn_kernel(first, batch, slot_per, per_dev, grp, x_ref, wi_ref, wo_ref, *rest):
-    outs, (xf, xe, acc, og) = rest[:BATCH_CHUNKS], rest[BATCH_CHUNKS:]
+def ffn_kernel(batch, slot_per, n_out, x_ref, wi_ref, wo_ref, *rest):
+    outs, (xf, xe, acc, og, act) = rest[:n_out], rest[n_out:]
     e, h = pl.program_id(0), pl.program_id(1)
     last_e, last_h = pl.num_programs(0) - 1, pl.num_programs(1) - 1
-    tiles = x_ref.shape[2] // LANES
+    grp, dim = x_ref.shape[1:]
+    tiles = dim // LANES
 
     @pl.when((e == 0) & (h == 0))
     def _():
-        @pl.loop(0, batch)
+        @pl.loop(0, batch, unroll=4)
         def _(b):
-            rows = pl.ds(pl.multiple_of(b * per_dev, per_dev), per_dev)
+            rows = pl.ds(pl.multiple_of(b * grp, grp), grp)
             for c in range(tiles):
                 xf[c, rows, :] = x_ref[b, :, c * LANES:(c + 1) * LANES].astype(jnp.float32)
 
@@ -284,22 +350,15 @@
     def _():
         for q in range(slot_per):
             for c in range(tiles):
-                rows = xf[c, pl.ds((first + e) * slot_per + q, batch, stride=per_dev), :]
+                rows = xf[c, pl.ds(e * slot_per + q, batch, stride=grp), :]
                 xe[q * batch:(q + 1) * batch, c * LANES:(c + 1) * LANES] = rows.astype(jnp.bfloat16)
 
-    acts = []
-    for i in range(wi_ref.shape[2] // SUB_TILE):
-        hid = jnp.dot(xe[...], wi_ref[0, :, i * SUB_TILE:(i + 1) * SUB_TILE], preferred_element_type=jnp.float32)
-        acts.append((0.5 * hid * (1.0 + lax.erf(hid * 0.7071067811865476))).astype(jnp.bfloat16))
-    part = jnp.dot(jnp.concatenate(acts, axis=1), wo_ref[0], preferred_element_type=jnp.float32)
-
-    @pl.when(h == 0)
-    def _():
-        acc[...] = part
-
-    @pl.when(h > 0)
-    def _():
-        acc[...] += part
+    hidden = wi_ref.shape[2]
+    for i in range(0, hidden, 256):
+        hid = jnp.dot(xe[...], wi_ref[0, :, i:i + 256], preferred_element_type=jnp.float32)
+        act[:, i:i + 256] = (0.5 * hid * (1.0 + lax.erf(hid * 0.7071067811865476))).astype(jnp.bfloat16)
+    for i in range(0, dim, 256):
+        acc[:, i:i + 256] = jnp.where(h == 0, 0.0, acc[:, i:i + 256]) + jnp.dot(act[...], wo_ref[0, :, i:i + 256], preferred_element_type=jnp.float32)
 
     @pl.when(h == last_h)
     def _():
@@ -309,37 +368,40 @@
 
     @pl.when((e == last_e) & (h == last_h))
     def _():
-        step = batch // BATCH_CHUNKS
+        step = batch // n_out
         for i, out in enumerate(outs):
-            for b in range(step):
-                rows = slice((i * step + b) * grp, (i * step + b + 1) * grp)
+            @pl.loop(0, step, unroll=4)
+            def _(b):
+                rows = pl.ds(pl.multiple_of((i * step + b) * grp, grp), grp)
                 for c in range(tiles):
                     out[b, :, c * LANES:(c + 1) * LANES] = og[c, rows, :].astype(jnp.bfloat16)
 
 
 def ffn(group, xs, w_in, w_out, slot_per):
-    batch, per_dev, dim = xs.shape
+    batch, _, dim = xs.shape
     experts, _, hidden = w_in.shape
     ge = experts // GROUPS
     grp = ge * slot_per
     first = group * ge
-    step = batch // BATCH_CHUNKS
+    n_out = CHUNKS[group]
+    step = batch // n_out
     rows = batch * slot_per
     return pl.pallas_call(
-        functools.partial(ffn_kernel, first, batch, slot_per, per_dev, grp),
+        functools.partial(ffn_kernel, batch, slot_per, n_out),
         grid=(ge, hidden // HIDDEN_TILE),
-        out_shape=[jax.ShapeDtypeStruct((step, grp, dim), jnp.bfloat16)] * BATCH_CHUNKS,
+        out_shape=[jax.ShapeDtypeStruct((step, grp, dim), jnp.bfloat16)] * n_out,
         in_specs=[
-            pl.BlockSpec((batch, per_dev, dim), lambda e, h: (0, 0, 0)),
+            pl.BlockSpec((batch, grp, dim), lambda e, h: (0, group, 0)),
             pl.BlockSpec((1, dim, HIDDEN_TILE), lambda e, h: (first + e, 0, h)),
             pl.BlockSpec((1, HIDDEN_TILE, dim), lambda e, h: (first + e, h, 0)),
         ],
-        out_specs=[pl.BlockSpec((step, grp, dim), lambda e, h: (0, 0, 0))] * BATCH_CHUNKS,
+        out_specs=[pl.BlockSpec((step, grp, dim), lambda e, h: (0, 0, 0))] * n_out,
         scratch_shapes=[
-            pltpu.VMEM((dim // LANES, batch * per_dev, LANES), jnp.float32),
+            pltpu.VMEM((dim // LANES, batch * grp, LANES), jnp.float32),
             pltpu.VMEM((rows, dim), jnp.bfloat16),
             pltpu.VMEM((rows, dim), jnp.float32),
             pltpu.VMEM((dim // LANES, batch * grp, LANES), jnp.float32),
+            pltpu.VMEM((rows, HIDDEN_TILE), jnp.bfloat16),
         ],
         compiler_params=pltpu.CompilerParams(dimension_semantics=("arbitrary", "arbitrary"), vmem_limit_bytes=58 * 1024 * 1024),
         cost_estimate=pl.CostEstimate(flops=4 * ge * rows * dim * hidden, bytes_accessed=4 * ge * dim * hidden, transcendentals=0),
@@ -359,15 +421,17 @@
 
 def combine(chunk, mix, pieces, lengths, offset, y):
     batch, n_tok, n_slots = mix.shape
-    step, grp, dim = pieces[0].shape
+    _, grp, dim = pieces[0][0].shape
+    cs = COMBINE_SEQS
+    step = batch // MIX_CHUNKS
     first = chunk * step
     n_p = len(pieces)
-    cs = COMBINE_SEQS
     base = first // cs
     in_specs = [
         pl.BlockSpec((cs, n_tok, n_slots), lambda b, *_: (base + b, 0, 0)),
-        *[pl.BlockSpec((cs, grp, dim), lambda b, *_: (b, 0, 0))] * n_p,
+        *[pl.BlockSpec((cs, grp, dim), functools.partial(lambda at, b, *_: (at // cs + b, 0, 0), at)) for _, at in pieces],
     ]
+    pieces = [p for p, _ in pieces]
     args = [lengths, offset, mix, *pieces]
     alias = {}
     if y is not None:
@@ -413,10 +477,17 @@
                 table[k, group, 1] = lax.ppermute(own, "seq", swap_c)
                 table[k, group, 2] = across
                 table[k, group, 3] = lax.ppermute(across, "seq", swap_c)
+        for part in range(MIX_CALLS):
+            mix = mix_weights(part, tokens, lengths, slot_params, logit_scale.reshape(1), per_dev, mix)
         y = None
-        for k in range(BATCH_CHUNKS):
-            pieces = [table[k, group, q] for q in range(seq_size) for group in range(GROUPS)]
+        for k in range(MIX_CHUNKS):
+            pieces = []
+            for q in range(seq_size):
+                for group in range(GROUPS):
+                    per = MIX_CHUNKS // CHUNKS[group]
+                    pieces.append((table[k // per, group, q], k % per * (tokens.shape[0] // MIX_CHUNKS)))
             y = combine(k, mix, pieces, lengths, offset, y)
         return y
 
+
     return jax.shard_map(local_layer, mesh=mesh, in_specs=(P("data", "seq", None), P("data"), P(), P(), P("seq", None, "model"), P("seq", "model", None)), out_specs=P("data", "seq", None), check_vma=False)

time: 383 us -> 380 us (level)
  waiting for transfers between devices: 148 us -> 134 us
  Pallas kernels: 197 us -> 202 us
    ppermute x8 -> x10, waiting for transfers between devices: 87.9 us -> 49.3 us  [local_layer(): other = lax.ppermute(part, 'model', swap_y)]
    ppermute x8 -> x10, waiting for transfers between devices: 60.2 us -> 83.5 us  [local_layer(): across = lax.ppermute(own, 'seq', swap_x)]
    pallas_call x3 -> x7, Pallas kernels: 152 us -> 157 us  [the longest x1 79.9 us: dispatch(): pl.pallas_call(functools.partial(dispatch_kernel, half, n_tok, n_slots, p...]
    unnamed x68 -> x88, local copies, waits for them, and re-layouts: 11.3 us -> 14 us
    ppermute x8 -> x10, starting transfers between devices: 8.95 us -> 10.4 us  [local_layer(): other = lax.ppermute(part, 'model', swap_y)]
    ppermute x8 -> x10, starting transfers between devices: 11.4 us -> 10.8 us  [local_layer(): across = lax.ppermute(own, 'seq', swap_x)]
  transfers between devices with their start and end apart: 32 -> 40, of which waited for: 12 -> 15; matrix products, arithmetic and copies ran while one was open for 1% -> 1% of each run, Pallas kernels for 17% -> 25%
where the time goes in v2:
time: 380 us; the launch traced here: 379 us
  Pallas kernels  202 us (53%)
  waiting for transfers between devices  134 us (35%)
  starting transfers between devices  24.3 us (6%)
  local copies, waits for them, and re-layouts  14 us (4%)
    ppermute x10, waiting for transfers between devices, local_layer(): across = lax.ppermute(own, 'seq', swap_x)  83.5 us
    pallas_call x1, Pallas kernels, dispatch(): pl.pallas_call(functools.partial(dispatch_kernel, half, n_tok, n_slots, p...  79.9 us
    pallas_call x4, Pallas kernels, ffn(): pl.pallas_call(functools.partial(ffn_kernel, batch, slot_per, n_out), gri...  59.6 us
    ppermute x10, waiting for transfers between devices, local_layer(): other = lax.ppermute(part, 'model', swap_y)  49.3 us
    pallas_call x4, Pallas kernels, combine(): pl.pallas_call(functools.partial(combine_kernel, first, n_tok, n_p), grid...  45.2 us
    pallas_call x2, Pallas kernels, mix_weights(): pl.pallas_call(functools.partial(mix_kernel, per_dev, seqs), grid_spec=pl...  17.1 us
    unnamed x88, local copies, waits for them, and re-layouts  14 us
    ppermute x10, starting transfers between devices, local_layer(): across = lax.ppermute(own, 'seq', swap_x)  10.8 us
  transfers between devices with their start and end apart: 40, of which 15 were waited for; matrix products, arithmetic and copies ran while one was open for 1% of the time, Pallas kernels for 25%

profile of v2, /device:TPU:0, one launch (start us, length us, event | category | flops | bytes accessed | tf_op | source)
XLA Modules:
  0.0 378.8 jit_solution(6311734640733590904)
XLA Ops:
  0.7 79.9 %dispatch.1 = (bf16[64,32,1280]{2,1,0:T(8,128)(2,1)}, bf16[64,512,128]{2,1,0:T(8,128)(2,1)}) custom-call(bf16[1280,128]{1,0:T(8,128)(2,1)} %phi_ref.5, s32[64]{0:T(128)} %len_ref.13, f32[1]{0:T(128)} %bitcast.5.g_ref, bf16[64,512,1280]{2,1,0:T(8,128)(2,1)} %x_ref.3), custom_call_target="tpu_custom_call" | custom-call | tf_op jit(solution)/shard_map/dispatch/pallas_call | solution.py:294
  80.6 14.9 %ffn.7 = (bf16[16,8,1280]{2,1,0:T(8,128)(2,1)}, bf16[16,8,1280]{2,1,0:T(8,128)(2,1)}, bf16[16,8,1280]{2,1,0:T(8,128)(2,1)}, bf16[16,8,1280]{2,1,0:T(8,128)(2,1)}) custom-call(bf16[64,32,1280]{2,1,0:T(8,128)(2,1)} %get-tuple-element.18.x_ref, bf16[8,1280,2560]{2,1,0:T(8,128)(2,1)} %wi_ref.7, bf16[8,2560,1280]{2,1,0:T(8,128)(2,1)} %wo_ref.7), custom_call_target="tpu_custom_call" | custom-call | flops 6710886400 | bytes 26214400 | tf_op jit(solution)/shard_map/ffn/pallas_call | solution.py:389
  95.5 0.9 collective-permute-start.36
  96.4 14.9 %ffn.4 = (bf16[32,8,1280]{2,1,0:T(8,128)(2,1)}, bf16[32,8,1280]{2,1,0:T(8,128)(2,1)}) custom-call(bf16[64,32,1280]{2,1,0:T(8,128)(2,1)} %get-tuple-element.18.x_ref, bf16[8,1280,2560]{2,1,0:T(8,128)(2,1)} %wi_ref.7, bf16[8,2560,1280]{2,1,0:T(8,128)(2,1)} %wo_ref.7), custom_call_target="tpu_custom_call" | custom-call | flops 6710886400 | bytes 26214400 | tf_op jit(solution)/shard_map/ffn/pallas_call | solution.py:389
  111.3 1.1 collective-permute-start.20
  112.4 14.9 %ffn.5 = (bf16[32,8,1280]{2,1,0:T(8,128)(2,1)}, bf16[32,8,1280]{2,1,0:T(8,128)(2,1)}) custom-call(bf16[64,32,1280]{2,1,0:T(8,128)(2,1)} %get-tuple-element.18.x_ref, bf16[8,1280,2560]{2,1,0:T(8,128)(2,1)} %wi_ref.7, bf16[8,2560,1280]{2,1,0:T(8,128)(2,1)} %wo_ref.7), custom_call_target="tpu_custom_call" | custom-call | flops 6710886400 | bytes 26214400 | tf_op jit(solution)/shard_map/ffn/pallas_call | solution.py:389
  127.3 0.9 collective-permute-start.21
  128.2 14.9 %ffn.6 = (bf16[32,8,1280]{2,1,0:T(8,128)(2,1)}, bf16[32,8,1280]{2,1,0:T(8,128)(2,1)}) custom-call(bf16[64,32,1280]{2,1,0:T(8,128)(2,1)} %get-tuple-element.18.x_ref, bf16[8,1280,2560]{2,1,0:T(8,128)(2,1)} %wi_ref.7, bf16[8,2560,1280]{2,1,0:T(8,128)(2,1)} %wo_ref.7), custom_call_target="tpu_custom_call" | custom-call | flops 6710886400 | bytes 26214400 | tf_op jit(solution)/shard_map/ffn/pallas_call | solution.py:389
  143.1 1.1 collective-permute-start.22
  144.3 0.9 collective-permute-start.23
  145.1 1.1 collective-permute-start.16
  146.4 21.6 %collective-permute-done.23 = bf16[16,8,1280]{2,1,0:T(8,128)(2,1)S(1)} collective-permute-done((bf16[16,8,1280]{2,1,0:T(8,128)(2,1)S(1)}, bf16[16,8,1280]{2,1,0:T(8,128)(2,1)S(1)}, u32[]{:S(2)}, u32[]{:S(2)}) %collective-permute-start.23) | collective-permute-done | bytes 327712 | tf_op jit(solution)/shard_map/ppermute | solution.py:473
  167.9 1.1 collective-permute-start
  169.2 5.8 %collective-permute-done.16 = bf16[16,8,1280]{2,1,0:T(8,128)(2,1)S(1)} collective-permute-done((bf16[16,8,1280]{2,1,0:T(8,128)(2,1)S(1)}, bf16[16,8,1280]{2,1,0:T(8,128)(2,1)S(1)}, u32[]{:S(2)}, u32[]{:S(2)}) %collective-permute-start.16) | collective-permute-done | bytes 327712 | tf_op jit(solution)/shard_map/ppermute | solution.py:473
  175.0 1.1 collective-permute-start.3
  176.2 17.7 %collective-permute-done.3 = bf16[16,8,1280]{2,1,0:T(8,128)(2,1)S(1)} collective-permute-done((bf16[16,8,1280]{2,1,0:T(8,128)(2,1)S(1)}, bf16[16,8,1280]{2,1,0:T(8,128)(2,1)S(1)}, u32[]{:S(2)}, u32[]{:S(2)}) %collective-permute-start.3) | collective-permute-done | bytes 327712 | tf_op jit(solution)/shard_map/ppermute | solution.py:473
  193.9 1.1 collective-permute-start.38
  195.2 0.2 add_convert_fusion.2.rest_0_
  195.4 6.2 %collective-permute-done.38.rest_11_ = bf16[16,8,1280]{2,1,0:T(8,128)(2,1)S(1)} collective-permute-done((bf16[16,8,1280]{2,1,0:T(8,128)(2,1)S(1)}, bf16[16,8,1280]{2,1,0:T(8,128)(2,1)S(1)}, u32[]{:S(2)}, u32[]{:S(2)}) %collective-permute-start.38) | collective-permute-done | bytes 327712 | tf_op jit(solution)/shard_map/ppermute | solution.py:475
  201.5 0.9 collective-permute-start.1
  202.5 1.1 collective-permute-start.2
  203.6 1.1 collective-permute-start.31
  204.8 0.2 add_convert_fusion.1.rest_1_
  204.9 0.5 copy-done.28
  205.4 6.9 %collective-permute-done.31.rest_11_ = bf16[16,8,1280]{2,1,0:T(8,128)(2,1)S(1)} collective-permute-done((bf16[16,8,1280]{2,1,0:T(8,128)(2,1)S(1)}, bf16[16,8,1280]{2,1,0:T(8,128)(2,1)S(1)}, u32[]{:S(2)}, u32[]{:S(2)}) %collective-permute-start.31) | collective-permute-done | bytes 327712 | tf_op jit(solution)/shard_map/ppermute | solution.py:475
  212.3 1.1 collective-permute-start.18
  213.7 8.3 %collective-permute-done.18.rest_11_ = bf16[16,8,1280]{2,1,0:T(8,128)(2,1)S(1)} collective-permute-done((bf16[16,8,1280]{2,1,0:T(8,128)(2,1)S(1)}, bf16[16,8,1280]{2,1,0:T(8,128)(2,1)S(1)}, u32[]{:S(2)}, u32[]{:S(2)}) %collective-permute-start.18) | collective-permute-done | bytes 327712 | tf_op jit(solution)/shard_map/ppermute | solution.py:475
  221.9 1.1 collective-permute-start.11
  223.1 0.9 collective-permute-start.28
  224.0 1.1 collective-permute-start.29
  225.1 4.3 %collective-permute-done.2 = bf16[32,8,1280]{2,1,0:T(8,128)(2,1)S(1)} collective-permute-done((bf16[32,8,1280]{2,1,0:T(8,128)(2,1)S(1)}, bf16[32,8,1280]{2,1,0:T(8,128)(2,1)S(1)}, u32[]{:S(2)}, u32[]{:S(2)}) %collective-permute-start.2) | collective-permute-done | bytes 655392 | tf_op jit(solution)/shard_map/ppermute | solution.py:473
  229.4 1.1 collective-permute-start.30
  230.5 0.7 copy-done.16
  231.4 1.1 collective-permute-done.11.rest_11_
  232.5 0.3 collective-permute-done.39.rest_15_
  232.9 0.2 collective-permute-start.19
  233.2 0.9 collective-permute-done.35.rest_15_
  234.2 0.7 copy-done.24
  235.0 0.7 copy-done.22
  235.7 0.4 collective-permute-start.25
  236.1 10.6 %collective-permute-done.28.rest_8_ = bf16[32,8,1280]{2,1,0:T(8,128)(2,1)} collective-permute-done((bf16[32,8,1280]{2,1,0:T(8,128)(2,1)S(1)}, bf16[32,8,1280]{2,1,0:T(8,128)(2,1)}, u32[]{:S(2)}, u32[]{:S(2)}) %collective-permute-start.28) | collective-permute-done | bytes 655392 | tf_op jit(solution)/shard_map/ppermute | solution.py:475
  246.7 14.0 %collective-permute-done.29.rest_9_ = bf16[32,8,1280]{2,1,0:T(8,128)(2,1)} collective-permute-done((bf16[32,8,1280]{2,1,0:T(8,128)(2,1)S(1)}, bf16[32,8,1280]{2,1,0:T(8,128)(2,1)}, u32[]{:S(2)}, u32[]{:S(2)}) %collective-permute-start.29) | collective-permute-done | bytes 655392 | tf_op jit(solution)/shard_map/ppermute | solution.py:475
  260.7 1.1 collective-permute-start.8
  261.8 12.9 %collective-permute-done.30.rest_10_ = bf16[32,8,1280]{2,1,0:T(8,128)(2,1)} collective-permute-done((bf16[32,8,1280]{2,1,0:T(8,128)(2,1)S(1)}, bf16[32,8,1280]{2,1,0:T(8,128)(2,1)}, u32[]{:S(2)}, u32[]{:S(2)}) %collective-permute-start.30) | collective-permute-done | bytes 655392 | tf_op jit(solution)/shard_map/ppermute | solution.py:475
  274.8 1.1 collective-permute-start.9
  275.9 2.3 add_convert_fusion.3.rest_2_
  278.2 0.9 collective-permute-start.10
  279.1 0.2 collective-permute-start.32
  279.3 9.5 %collective-permute-done.8.rest_8_ = bf16[32,8,1280]{2,1,0:T(8,128)(2,1)} collective-permute-done((bf16[32,8,1280]{2,1,0:T(8,128)(2,1)S(1)}, bf16[32,8,1280]{2,1,0:T(8,128)(2,1)}, u32[]{:S(2)}, u32[]{:S(2)}) %collective-permute-start.8) | collective-permute-done | bytes 655392 | tf_op jit(solution)/shard_map/ppermute | solution.py:475
  288.8 14.0 %collective-permute-done.9.rest_9_ = bf16[32,8,1280]{2,1,0:T(8,128)(2,1)} collective-permute-done((bf16[32,8,1280]{2,1,0:T(8,128)(2,1)S(1)}, bf16[32,8,1280]{2,1,0:T(8,128)(2,1)}, u32[]{:S(2)}, u32[]{:S(2)}) %collective-permute-start.9) | collective-permute-done | bytes 655392 | tf_op jit(solution)/shard_map/ppermute | solution.py:475
  303.0 3.4 copy-done
  306.4 1.0 copy-done.3
  307.4 8.6 %mix.2._ = bf16[64,512,128]{2,1,0:T(8,128)(2,1)S(1)} custom-call(s32[2]{0:T(128)S(1)} %pad_add_fusion.1.idx_ref, s32[64]{0:T(128)S(1)} %copy-done.32, bf16[1280,128]{1,0:T(8,128)(2,1)S(1)} %copy-done.3, f32[1]{0:T(128)} %bitcast.6.g_ref, bf16[64,512,1280]{2,1,0:T(8,128)(2,1)} %x_ref.3, bf16[64,512,128]{2,1,0:T(8,128)(2,1)S(1)} %copy-done), custom_call_target="tpu_custom_call", output_to_operand_aliasing={{}: (5, {})} | custom-call | flops 2684354560 | bytes 10485760 | tf_op jit(solution)/shard_map/mix/pallas_call | solution.py:83
  316.0 8.6 %mix.3.c_ref = bf16[64,512,128]{2,1,0:T(8,128)(2,1)S(1)} custom-call(s32[2]{0:T(128)S(1)} %pad_add_fusion.idx_ref, s32[64]{0:T(128)S(1)} %copy-done.32, bf16[1280,128]{1,0:T(8,128)(2,1)S(1)} %copy-done.3, f32[1]{0:T(128)} %bitcast.7.g_ref, bf16[64,512,1280]{2,1,0:T(8,128)(2,1)} %x_ref.3, bf16[64,512,128]{2,1,0:T(8,128)(2,1)S(1)} %mix.2._), custom_call_target="tpu_custom_call", output_to_operand_aliasing={{}: (5, {})} | custom-call | flops 2684354560 | bytes 10485760 | tf_op jit(solution)/shard_map/mix/pallas_call | solution.py:83
  324.6 3.4 copy-done.1
  328.0 0.5 collective-permute-start.5
  328.5 0.5 collective-permute-start.12
  329.0 0.5 collective-permute-start.14
  329.5 3.4 copy-done.2
  332.9 11.5 %combine.4.rest_16_ = bf16[64,512,1280]{2,1,0:T(8,128)(2,1)} custom-call(s32[64]{0:T(128)S(1)} %copy-done.32, s32[1]{0:T(128)} %bitcast.off_ref, bf16[64,512,128]{2,1,0:T(8,128)(2,1)S(1)} %copy-done.2, bf16[32,8,1280]{2,1,0:T(8,128)(2,1)S(1)} %add_convert_fusion.2.rest_0_, bf16[32,8,1280]{2,1,0:T(8,128)(2,1)S(1)} %add_convert_fusion.1.rest_1_, ...), custom_call_target="tpu_custom_call" | custom-call | flops 5368709120 | bytes 23068672 | tf_op jit(solution)/shard_map/combine/pallas_call | solution.py:441
  344.5 11.5 %combine.5.rest_16_ = bf16[64,512,1280]{2,1,0:T(8,128)(2,1)} custom-call(s32[64]{0:T(128)S(1)} %copy-done.32, s32[1]{0:T(128)} %bitcast.off_ref, bf16[64,512,128]{2,1,0:T(8,128)(2,1)S(1)} %copy-done.2, bf16[32,8,1280]{2,1,0:T(8,128)(2,1)S(1)} %add_convert_fusion.2.rest_0_, ...), custom_call_target="tpu_custom_call", output_to_operand_aliasing={{}: (19, {})} | custom-call | flops 5368709120 | bytes 23068672 | tf_op jit(solution)/shard_map/combine/pallas_call | solution.py:441
  356.0 0.5 collective-permute-start.15
  356.5 11.1 %combine.6.rest_16_ = bf16[64,512,1280]{2,1,0:T(8,128)(2,1)} custom-call(s32[64]{0:T(128)S(1)} %copy-done.32, s32[1]{0:T(128)} %bitcast.off_ref, bf16[64,512,128]{2,1,0:T(8,128)(2,1)S(1)} %copy-done.2, bf16[32,8,1280]{2,1,0:T(8,128)(2,1)S(1)} %add_convert_fusion.5.rest_0_, ...), custom_call_target="tpu_custom_call", output_to_operand_aliasing={{}: (19, {})} | custom-call | flops 5368709120 | bytes 23068672 | tf_op jit(solution)/shard_map/combine/pallas_call | solution.py:441
  367.7 11.1 %combine.7 = bf16[64,512,1280]{2,1,0:T(8,128)(2,1)} custom-call(s32[64]{0:T(128)S(1)} %copy-done.32, s32[1]{0:T(128)} %bitcast.off_ref, bf16[64,512,128]{2,1,0:T(8,128)(2,1)S(1)} %copy-done.2, bf16[32,8,1280]{2,1,0:T(8,128)(2,1)S(1)} %add_convert_fusion.5.rest_0_, ...), custom_call_target="tpu_custom_call", output_to_operand_aliasing={{}: (19, {})} | custom-call | flops 5368709120 | bytes 23068672 | tf_op jit(solution)/shard_map/combine/pallas_call | solution.py:441
  (127 shorter events, 1.5 us)
Async XLA Ops:
  95.5 49.6 %collective-permute-start.36 = (bf16[16,8,1280]{2,1,0:T(8,128)(2,1)}, bf16[16,8,1280]{2,1,0:T(8,128)(2,1)S(1)}, u32[]{:S(2)}, u32[]{:S(2)}) collective-permute-start(bf16[16,8,1280]{2,1,0:T(8,128)(2,1)} %get-tuple-element.28), channel_id=1, source_target_pairs={{0,4},{4,0},{1,5},{5,1},{2,6},{6,2},{3,7},{7,3}} | collective-permute-start | bytes 983048 | tf_op jit(solution)/shard_map/ppermute | solution.py:473
  111.3 83.9 %collective-permute-start.20 = (bf16[32,8,1280]{2,1,0:T(8,128)(2,1)}, bf16[32,8,1280]{2,1,0:T(8,128)(2,1)S(1)}, u32[]{:S(2)}, u32[]{:S(2)}) collective-permute-start(bf16[32,8,1280]{2,1,0:T(8,128)(2,1)} %get-tuple-element.24), channel_id=1, source_target_pairs={{0,4},{4,0},{1,5},{5,1},{2,6},{6,2},{3,7},{7,3}} | collective-permute-start | bytes 1966088 | tf_op jit(solution)/shard_map/ppermute | solution.py:473
  127.3 16.9 %copy-start.42 = (bf16[16,8,1280]{2,1,0:T(8,128)(2,1)S(1)}, bf16[16,8,1280]{2,1,0:T(8,128)(2,1)}, u32[]{:S(2)}) copy-start(bf16[16,8,1280]{2,1,0:T(8,128)(2,1)} %get-tuple-element.27) | copy-start | bytes 983044
  127.3 17.8 %copy-start.41 = (bf16[16,8,1280]{2,1,0:T(8,128)(2,1)S(1)}, bf16[16,8,1280]{2,1,0:T(8,128)(2,1)}, u32[]{:S(2)}) copy-start(bf16[16,8,1280]{2,1,0:T(8,128)(2,1)} %get-tuple-element.23) | copy-start | bytes 983044
  127.3 19.0 %copy-start.43 = (bf16[16,8,1280]{2,1,0:T(8,128)(2,1)S(1)}, bf16[16,8,1280]{2,1,0:T(8,128)(2,1)}, u32[]{:S(2)}) copy-start(bf16[16,8,1280]{2,1,0:T(8,128)(2,1)} %get-tuple-element.28) | copy-start | bytes 983044
  127.3 40.6 %copy-start.36 = (bf16[32,8,1280]{2,1,0:T(8,128)(2,1)S(1)}, bf16[32,8,1280]{2,1,0:T(8,128)(2,1)}, u32[]{:S(2)}) copy-start(bf16[32,8,1280]{2,1,0:T(8,128)(2,1)} %get-tuple-element.19) | copy-start | bytes 1966084
  127.3 75.2 %collective-permute-start.21 = (bf16[32,8,1280]{2,1,0:T(8,128)(2,1)}, bf16[32,8,1280]{2,1,0:T(8,128)(2,1)S(1)}, u32[]{:S(2)}, u32[]{:S(2)}) collective-permute-start(bf16[32,8,1280]{2,1,0:T(8,128)(2,1)} %get-tuple-element.25), channel_id=1, source_target_pairs={{0,4},{4,0},{1,5},{5,1},{2,6},{6,2},{3,7},{7,3}} | collective-permute-start | bytes 1966088 | tf_op jit(solution)/shard_map/ppermute | solution.py:473
  143.1 31.9 %copy-start.40 = (bf16[16,8,1280]{2,1,0:T(8,128)(2,1)S(1)}, bf16[16,8,1280]{2,1,0:T(8,128)(2,1)}, u32[]{:S(2)}) copy-start(bf16[16,8,1280]{2,1,0:T(8,128)(2,1)} %get-tuple-element.22) | copy-start | bytes 983044
  143.1 60.5 %collective-permute-start.22 = (bf16[32,8,1280]{2,1,0:T(8,128)(2,1)}, bf16[32,8,1280]{2,1,0:T(8,128)(2,1)S(1)}, u32[]{:S(2)}, u32[]{:S(2)}) collective-permute-start(bf16[32,8,1280]{2,1,0:T(8,128)(2,1)} %get-tuple-element.26), channel_id=1, source_target_pairs={{0,4},{4,0},{1,5},{5,1},{2,6},{6,2},{3,7},{7,3}} | collective-permute-start | bytes 1966088 | tf_op jit(solution)/shard_map/ppermute | solution.py:473
  144.3 23.7 %collective-permute-start.23 = (bf16[16,8,1280]{2,1,0:T(8,128)(2,1)S(1)}, bf16[16,8,1280]{2,1,0:T(8,128)(2,1)S(1)}, u32[]{:S(2)}, u32[]{:S(2)}) collective-permute-start(bf16[16,8,1280]{2,1,0:T(8,128)(2,1)S(1)} %copy-done.42), channel_id=1, source_target_pairs={{0,4},{4,0},{1,5},{5,1},{2,6},{6,2},{3,7},{7,3}} | collective-permute-start | bytes 983048 | tf_op jit(solution)/shard_map/ppermute | solution.py:473
  145.1 29.8 %collective-permute-start.16 = (bf16[16,8,1280]{2,1,0:T(8,128)(2,1)S(1)}, bf16[16,8,1280]{2,1,0:T(8,128)(2,1)S(1)}, u32[]{:S(2)}, u32[]{:S(2)}) collective-permute-start(bf16[16,8,1280]{2,1,0:T(8,128)(2,1)S(1)} %copy-done.41), channel_id=1, source_target_pairs={{0,4},{4,0},{1,5},{5,1},{2,6},{6,2},{3,7},{7,3}} | collective-permute-start | bytes 983048 | tf_op jit(solution)/shard_map/ppermute | solution.py:473
  146.4 48.8 %copy-start.10 = (bf16[16,8,1280]{2,1,0:T(8,128)(2,1)}, bf16[16,8,1280]{2,1,0:T(8,128)(2,1)S(1)}, u32[]{:S(2)}) copy-start(bf16[16,8,1280]{2,1,0:T(8,128)(2,1)S(1)} %add_convert_fusion.6.rest_3_) | copy-start | bytes 983044
  167.9 27.2 %copy-start.39 = (bf16[32,8,1280]{2,1,0:T(8,128)(2,1)S(1)}, bf16[32,8,1280]{2,1,0:T(8,128)(2,1)}, u32[]{:S(2)}) copy-start(bf16[32,8,1280]{2,1,0:T(8,128)(2,1)} %get-tuple-element.24) | copy-start | bytes 1966084
  167.9 55.1 %collective-permute-start = (bf16[32,8,1280]{2,1,0:T(8,128)(2,1)S(1)}, bf16[32,8,1280]{2,1,0:T(8,128)(2,1)S(1)}, u32[]{:S(2)}, u32[]{:S(2)}) collective-permute-start(bf16[32,8,1280]{2,1,0:T(8,128)(2,1)S(1)} %copy-done.36), channel_id=1, source_target_pairs={{0,4},{4,0},{1,5},{5,1},{2,6},{6,2},{3,7},{7,3}} | collective-permute-start | bytes 1966088 | tf_op jit(solution)/shard_map/ppermute | solution.py:473
  169.2 35.5 %copy-start.8 = (bf16[16,8,1280]{2,1,0:T(8,128)(2,1)}, bf16[16,8,1280]{2,1,0:T(8,128)(2,1)S(1)}, u32[]{:S(2)}) copy-start(bf16[16,8,1280]{2,1,0:T(8,128)(2,1)S(1)} %add_convert_fusion.7.rest_3_) | copy-start | bytes 983044
  175.0 19.0 %collective-permute-start.3 = (bf16[16,8,1280]{2,1,0:T(8,128)(2,1)S(1)}, bf16[16,8,1280]{2,1,0:T(8,128)(2,1)S(1)}, u32[]{:S(2)}, u32[]{:S(2)}) collective-permute-start(bf16[16,8,1280]{2,1,0:T(8,128)(2,1)S(1)} %copy-done.40), channel_id=1, source_target_pairs={{0,4},{4,0},{1,5},{5,1},{2,6},{6,2},{3,7},{7,3}} | collective-permute-start | bytes 983048 | tf_op jit(solution)/shard_map/ppermute | solution.py:473
  176.2 37.3 %copy-start.6 = (bf16[16,8,1280]{2,1,0:T(8,128)(2,1)}, bf16[16,8,1280]{2,1,0:T(8,128)(2,1)S(1)}, u32[]{:S(2)}) copy-start(bf16[16,8,1280]{2,1,0:T(8,128)(2,1)S(1)} %add_convert_fusion.8.rest_3_) | copy-start | bytes 983044
  176.2 25.3 %copy-start.35 = (bf16[32,8,1280]{2,1,0:T(8,128)(2,1)S(1)}, bf16[32,8,1280]{2,1,0:T(8,128)(2,1)}, u32[]{:S(2)}) copy-start(bf16[32,8,1280]{2,1,0:T(8,128)(2,1)} %get-tuple-element.20) | copy-start | bytes 1966084
  176.2 26.3 %copy-start.33 = (bf16[32,8,1280]{2,1,0:T(8,128)(2,1)S(1)}, bf16[32,8,1280]{2,1,0:T(8,128)(2,1)}, u32[]{:S(2)}) copy-start(bf16[32,8,1280]{2,1,0:T(8,128)(2,1)} %get-tuple-element.21) | copy-start | bytes 1966084
  176.2 28.5 %copy-start.38 = (bf16[32,8,1280]{2,1,0:T(8,128)(2,1)S(1)}, bf16[32,8,1280]{2,1,0:T(8,128)(2,1)}, u32[]{:S(2)}) copy-start(bf16[32,8,1280]{2,1,0:T(8,128)(2,1)} %get-tuple-element.25) | copy-start | bytes 1966084
  193.9 7.6 %collective-permute-start.38 = (bf16[16,8,1280]{2,1,0:T(8,128)(2,1)S(1)}, bf16[16,8,1280]{2,1,0:T(8,128)(2,1)S(1)}, u32[]{:S(2)}, u32[]{:S(2)}) collective-permute-start(bf16[16,8,1280]{2,1,0:T(8,128)(2,1)S(1)} %add_convert_fusion.6.rest_3_), channel_id=1, source_target_pairs={{0,2},{1,3},{2,0},{3,1},{4,6},{5,7},{6,4},{7,5}} | collective-permute-start | bytes 983048 | tf_op jit(solution)/shard_map/ppermute | solution.py:475
  195.1 26.8 %copy-start.4 = (bf16[16,8,1280]{2,1,0:T(8,128)(2,1)}, bf16[16,8,1280]{2,1,0:T(8,128)(2,1)S(1)}, u32[]{:S(2)}) copy-start(bf16[16,8,1280]{2,1,0:T(8,128)(2,1)S(1)} %add_convert_fusion.9.rest_3_) | copy-start | bytes 983044
  195.2 9.6 %collective-permute-start.37 = (bf16[16,8,1280]{2,1,0:T(8,128)(2,1)S(1)}, bf16[16,8,1280]{2,1,0:T(8,128)(2,1)S(1)}, u32[]{:S(2)}, u32[]{:S(2)}) collective-permute-start(bf16[16,8,1280]{2,1,0:T(8,128)(2,1)S(1)} %add_convert_fusion.6.rest_3_), channel_id=1, source_target_pairs={{0,1},{1,0},{2,3},{3,2},{4,5},{5,4},{6,7},{7,6}} | collective-permute-start | bytes 983048 | tf_op jit(solution)/shard_map/ppermute | solution.py:477
  195.4 18.1 %copy-start.37 = (bf16[32,8,1280]{2,1,0:T(8,128)(2,1)S(1)}, bf16[32,8,1280]{2,1,0:T(8,128)(2,1)}, u32[]{:S(2)}) copy-start(bf16[32,8,1280]{2,1,0:T(8,128)(2,1)} %get-tuple-element.26) | copy-start | bytes 1966084
  201.5 29.0 %copy-start.26 = (bf16[16,8,1280]{2,1,0:T(8,128)(2,1)}, bf16[16,8,1280]{2,1,0:T(8,128)(2,1)S(1)}, u32[]{:S(2)}) copy-start(bf16[16,8,1280]{2,1,0:T(8,128)(2,1)S(1)} %collective-permute-done.38.rest_11_) | copy-start | bytes 983044
  201.5 22.4 %collective-permute-start.1 = (bf16[32,8,1280]{2,1,0:T(8,128)(2,1)S(1)}, bf16[32,8,1280]{2,1,0:T(8,128)(2,1)S(1)}, u32[]{:S(2)}, u32[]{:S(2)}) collective-permute-start(bf16[32,8,1280]{2,1,0:T(8,128)(2,1)S(1)} %copy-done.35), channel_id=1, source_target_pairs={{0,4},{4,0},{1,5},{5,1},{2,6},{6,2},{3,7},{7,3}} | collective-permute-start | bytes 1966088 | tf_op jit(solution)/shard_map/ppermute | solution.py:473
  202.5 26.9 %collective-permute-start.2 = (bf16[32,8,1280]{2,1,0:T(8,128)(2,1)S(1)}, bf16[32,8,1280]{2,1,0:T(8,128)(2,1)S(1)}, u32[]{:S(2)}, u32[]{:S(2)}) collective-permute-start(bf16[32,8,1280]{2,1,0:T(8,128)(2,1)S(1)} %copy-done.33), channel_id=1, source_target_pairs={{0,4},{4,0},{1,5},{5,1},{2,6},{6,2},{3,7},{7,3}} | collective-permute-start | bytes 1966088 | tf_op jit(solution)/shard_map/ppermute | solution.py:473
  203.6 8.7 %collective-permute-start.31 = (bf16[16,8,1280]{2,1,0:T(8,128)(2,1)S(1)}, bf16[16,8,1280]{2,1,0:T(8,128)(2,1)S(1)}, u32[]{:S(2)}, u32[]{:S(2)}) collective-permute-start(bf16[16,8,1280]{2,1,0:T(8,128)(2,1)S(1)} %add_convert_fusion.7.rest_3_), channel_id=1, source_target_pairs={{0,2},{1,3},{2,0},{3,1},{4,6},{5,7},{6,4},{7,5}} | collective-permute-start | bytes 983048 | tf_op jit(solution)/shard_map/ppermute | solution.py:475
  204.7 8.7 %collective-permute-start.27 = (bf16[16,8,1280]{2,1,0:T(8,128)(2,1)S(1)}, bf16[16,8,1280]{2,1,0:T(8,128)(2,1)S(1)}, u32[]{:S(2)}, u32[]{:S(2)}) collective-permute-start(bf16[16,8,1280]{2,1,0:T(8,128)(2,1)S(1)} %add_convert_fusion.7.rest_3_), channel_id=1, source_target_pairs={{0,1},{1,0},{2,3},{3,2},{4,5},{5,4},{6,7},{7,6}} | collective-permute-start | bytes 983048 | tf_op jit(solution)/shard_map/ppermute | solution.py:477
  212.3 20.2 %copy-start.18 = (bf16[16,8,1280]{2,1,0:T(8,128)(2,1)}, bf16[16,8,1280]{2,1,0:T(8,128)(2,1)S(1)}, u32[]{:S(2)}) copy-start(bf16[16,8,1280]{2,1,0:T(8,128)(2,1)S(1)} %collective-permute-done.31.rest_11_) | copy-start | bytes 983044
  212.3 9.6 %collective-permute-start.18 = (bf16[16,8,1280]{2,1,0:T(8,128)(2,1)S(1)}, bf16[16,8,1280]{2,1,0:T(8,128)(2,1)S(1)}, u32[]{:S(2)}, u32[]{:S(2)}) collective-permute-start(bf16[16,8,1280]{2,1,0:T(8,128)(2,1)S(1)} %add_convert_fusion.8.rest_3_), channel_id=1, source_target_pairs={{0,2},{1,3},{2,0},{3,1},{4,6},{5,7},{6,4},{7,5}} | collective-permute-start | bytes 983048 | tf_op jit(solution)/shard_map/ppermute | solution.py:475
  213.5 17.9 %copy-start.20 = (bf16[16,8,1280]{2,1,0:T(8,128)(2,1)}, bf16[16,8,1280]{2,1,0:T(8,128)(2,1)S(1)}, u32[]{:S(2)}) copy-start(bf16[16,8,1280]{2,1,0:T(8,128)(2,1)S(1)} %collective-permute-done.27.rest_7_) | copy-start | bytes 983044
  213.5 17.0 %collective-permute-start.17 = (bf16[16,8,1280]{2,1,0:T(8,128)(2,1)S(1)}, bf16[16,8,1280]{2,1,0:T(8,128)(2,1)S(1)}, u32[]{:S(2)}, u32[]{:S(2)}) collective-permute-start(bf16[16,8,1280]{2,1,0:T(8,128)(2,1)S(1)} %add_convert_fusion.8.rest_3_), channel_id=1, source_target_pairs={{0,1},{1,0},{2,3},{3,2},{4,5},{5,4},{6,7},{7,6}} | collective-permute-start | bytes 983048 | tf_op jit(solution)/shard_map/ppermute | solution.py:477
  221.9 10.6 %collective-permute-start.11 = (bf16[16,8,1280]{2,1,0:T(8,128)(2,1)S(1)}, bf16[16,8,1280]{2,1,0:T(8,128)(2,1)S(1)}, u32[]{:S(2)}, u32[]{:S(2)}) collective-permute-start(bf16[16,8,1280]{2,1,0:T(8,128)(2,1)S(1)} %add_convert_fusion.9.rest_3_), channel_id=1, source_target_pairs={{0,2},{1,3},{2,0},{3,1},{4,6},{5,7},{6,4},{7,5}} | collective-permute-start | bytes 983048 | tf_op jit(solution)/shard_map/ppermute | solution.py:475
  223.1 23.6 %collective-permute-start.28 = (bf16[32,8,1280]{2,1,0:T(8,128)(2,1)S(1)}, bf16[32,8,1280]{2,1,0:T(8,128)(2,1)}, u32[]{:S(2)}, u32[]{:S(2)}) collective-permute-start(bf16[32,8,1280]{2,1,0:T(8,128)(2,1)S(1)} %add_convert_fusion.2.rest_0_), channel_id=1, source_target_pairs={{0,2},{1,3},{2,0},{3,1},{4,6},{5,7},{6,4},{7,5}} | collective-permute-start | bytes 1966088 | tf_op jit(solution)/shard_map/ppermute | solution.py:475
  224.0 36.7 %collective-permute-start.29 = (bf16[32,8,1280]{2,1,0:T(8,128)(2,1)S(1)}, bf16[32,8,1280]{2,1,0:T(8,128)(2,1)}, u32[]{:S(2)}, u32[]{:S(2)}) collective-permute-start(bf16[32,8,1280]{2,1,0:T(8,128)(2,1)S(1)} %add_convert_fusion.1.rest_1_), channel_id=1, source_target_pairs={{0,2},{1,3},{2,0},{3,1},{4,6},{5,7},{6,4},{7,5}} | collective-permute-start | bytes 1966088 | tf_op jit(solution)/shard_map/ppermute | solution.py:475
  229.4 46.5 %copy-start.34 = (bf16[32,8,1280]{2,1,0:T(8,128)(2,1)}, bf16[32,8,1280]{2,1,0:T(8,128)(2,1)S(1)}, u32[]{:S(2)}) copy-start(bf16[32,8,1280]{2,1,0:T(8,128)(2,1)S(1)} %collective-permute-done.2) | copy-start | bytes 1966084
  229.4 45.4 %collective-permute-start.30 = (bf16[32,8,1280]{2,1,0:T(8,128)(2,1)S(1)}, bf16[32,8,1280]{2,1,0:T(8,128)(2,1)}, u32[]{:S(2)}, u32[]{:S(2)}) collective-permute-start(bf16[32,8,1280]{2,1,0:T(8,128)(2,1)S(1)} %add_convert_fusion.rest_2_), channel_id=1, source_target_pairs={{0,2},{1,3},{2,0},{3,1},{4,6},{5,7},{6,4},{7,5}} | collective-permute-start | bytes 1966088 | tf_op jit(solution)/shard_map/ppermute | solution.py:475
  231.2 1.6 collective-permute-start.39
  232.5 42.2 %copy-start.14 = (bf16[16,8,1280]{2,1,0:T(8,128)(2,1)}, bf16[16,8,1280]{2,1,0:T(8,128)(2,1)S(1)}, u32[]{:S(2)}) copy-start(bf16[16,8,1280]{2,1,0:T(8,128)(2,1)S(1)} %collective-permute-done.11.rest_11_) | copy-start | bytes 983044
  232.5 1.6 collective-permute-start.35
  232.9 43.0 %copy-start.30 = (bf16[16,8,1280]{2,1,0:T(8,128)(2,1)}, bf16[16,8,1280]{2,1,0:T(8,128)(2,1)S(1)}, u32[]{:S(2)}) copy-start(bf16[16,8,1280]{2,1,0:T(8,128)(2,1)S(1)} %collective-permute-done.39.rest_15_) | copy-start | bytes 983044
  232.9 2.1 collective-permute-start.19
  233.2 69.8 %copy-start.32 = (s32[64]{0:T(128)S(1)}, s32[64]{0:T(128)}, u32[]{:S(2)}) copy-start(s32[64]{0:T(128)} %len_ref.13) | copy-start | bytes 772
  234.9 43.3 %collective-permute-start.24 = (bf16[32,8,1280]{2,1,0:T(8,128)(2,1)S(1)}, bf16[32,8,1280]{2,1,0:T(8,128)(2,1)}, u32[]{:S(2)}, u32[]{:S(2)}) collective-permute-start(bf16[32,8,1280]{2,1,0:T(8,128)(2,1)S(1)} %add_convert_fusion.2.rest_0_), channel_id=1, source_target_pairs={{0,1},{1,0},{2,3},{3,2},{4,5},{5,4},{6,7},{7,6}} | collective-permute-start | bytes 1966088 | tf_op jit(solution)/shard_map/ppermute | solution.py:477
  235.7 42.4 %collective-permute-start.25 = (bf16[32,8,1280]{2,1,0:T(8,128)(2,1)S(1)}, bf16[32,8,1280]{2,1,0:T(8,128)(2,1)}, u32[]{:S(2)}, u32[]{:S(2)}) collective-permute-start(bf16[32,8,1280]{2,1,0:T(8,128)(2,1)S(1)} %add_convert_fusion.1.rest_1_), channel_id=1, source_target_pairs={{0,1},{1,0},{2,3},{3,2},{4,5},{5,4},{6,7},{7,6}} | collective-permute-start | bytes 1966088 | tf_op jit(solution)/shard_map/ppermute | solution.py:477
  246.7 32.4 %collective-permute-start.26 = (bf16[32,8,1280]{2,1,0:T(8,128)(2,1)S(1)}, bf16[32,8,1280]{2,1,0:T(8,128)(2,1)}, u32[]{:S(2)}, u32[]{:S(2)}) collective-permute-start(bf16[32,8,1280]{2,1,0:T(8,128)(2,1)S(1)} %add_convert_fusion.rest_2_), channel_id=1, source_target_pairs={{0,1},{1,0},{2,3},{3,2},{4,5},{5,4},{6,7},{7,6}} | collective-permute-start | bytes 1966088 | tf_op jit(solution)/shard_map/ppermute | solution.py:477
  260.7 28.1 %collective-permute-start.8 = (bf16[32,8,1280]{2,1,0:T(8,128)(2,1)S(1)}, bf16[32,8,1280]{2,1,0:T(8,128)(2,1)}, u32[]{:S(2)}, u32[]{:S(2)}) collective-permute-start(bf16[32,8,1280]{2,1,0:T(8,128)(2,1)S(1)} %add_convert_fusion.5.rest_0_), channel_id=1, source_target_pairs={{0,2},{1,3},{2,0},{3,1},{4,6},{5,7},{6,4},{7,5}} | collective-permute-start | bytes 1966088 | tf_op jit(solution)/shard_map/ppermute | solution.py:475
  274.8 28.1 %collective-permute-start.9 = (bf16[32,8,1280]{2,1,0:T(8,128)(2,1)S(1)}, bf16[32,8,1280]{2,1,0:T(8,128)(2,1)}, u32[]{:S(2)}, u32[]{:S(2)}) collective-permute-start(bf16[32,8,1280]{2,1,0:T(8,128)(2,1)S(1)} %add_convert_fusion.4.rest_1_), channel_id=1, source_target_pairs={{0,2},{1,3},{2,0},{3,1},{4,6},{5,7},{6,4},{7,5}} | collective-permute-start | bytes 1966088 | tf_op jit(solution)/shard_map/ppermute | solution.py:475
  278.2 50.3 %collective-permute-start.4 = (bf16[32,8,1280]{2,1,0:T(8,128)(2,1)S(1)}, bf16[32,8,1280]{2,1,0:T(8,128)(2,1)}, u32[]{:S(2)}, u32[]{:S(2)}) collective-permute-start(bf16[32,8,1280]{2,1,0:T(8,128)(2,1)S(1)} %add_convert_fusion.5.rest_0_), channel_id=1, source_target_pairs={{0,1},{1,0},{2,3},{3,2},{4,5},{5,4},{6,7},{7,6}} | collective-permute-start | bytes 1966088 | tf_op jit(solution)/shard_map/ppermute | solution.py:477
  278.2 49.8 %collective-permute-start.10 = (bf16[32,8,1280]{2,1,0:T(8,128)(2,1)}, bf16[32,8,1280]{2,1,0:T(8,128)(2,1)}, u32[]{:S(2)}, u32[]{:S(2)}) collective-permute-start(bf16[32,8,1280]{2,1,0:T(8,128)(2,1)} %add_convert_fusion.3.rest_2_), channel_id=1, source_target_pairs={{0,2},{1,3},{2,0},{3,1},{4,6},{5,7},{6,4},{7,5}} | collective-permute-start | bytes 1966088 | tf_op jit(solution)/shard_map/ppermute | solution.py:475
  279.1 49.4 %collective-permute-start.32 = (bf16[32,8,1280]{2,1,0:T(8,128)(2,1)}, bf16[32,8,1280]{2,1,0:T(8,128)(2,1)}, u32[]{:S(2)}, u32[]{:S(2)}) collective-permute-start(bf16[32,8,1280]{2,1,0:T(8,128)(2,1)} %collective-permute-done.28.rest_8_), channel_id=1, source_target_pairs={{0,1},{1,0},{2,3},{3,2},{4,5},{5,4},{6,7},{7,6}} | collective-permute-start | bytes 1966088 | tf_op jit(solution)/shard_map/ppermute | solution.py:479
  288.8 40.2 %collective-permute-start.33 = (bf16[32,8,1280]{2,1,0:T(8,128)(2,1)}, bf16[32,8,1280]{2,1,0:T(8,128)(2,1)}, u32[]{:S(2)}, u32[]{:S(2)}) collective-permute-start(bf16[32,8,1280]{2,1,0:T(8,128)(2,1)} %collective-permute-done.29.rest_9_), channel_id=1, source_target_pairs={{0,1},{1,0},{2,3},{3,2},{4,5},{5,4},{6,7},{7,6}} | collective-permute-start | bytes 1966088 | tf_op jit(solution)/shard_map/ppermute | solution.py:479
  302.8 26.2 %collective-permute-start.34 = (bf16[32,8,1280]{2,1,0:T(8,128)(2,1)}, bf16[32,8,1280]{2,1,0:T(8,128)(2,1)}, u32[]{:S(2)}, u32[]{:S(2)}) collective-permute-start(bf16[32,8,1280]{2,1,0:T(8,128)(2,1)} %collective-permute-done.30.rest_10_), channel_id=1, source_target_pairs={{0,1},{1,0},{2,3},{3,2},{4,5},{5,4},{6,7},{7,6}} | collective-permute-start | bytes 1966088 | tf_op jit(solution)/shard_map/ppermute | solution.py:479
  315.9 13.6 %copy-start.11 = (bf16[16,8,1280]{2,1,0:T(8,128)(2,1)S(1)}, bf16[16,8,1280]{2,1,0:T(8,128)(2,1)}, u32[]{:S(2)}) copy-start(bf16[16,8,1280]{2,1,0:T(8,128)(2,1)} %copy-done.10) | copy-start | bytes 983044
  315.9 13.6 %copy-start.27 = (bf16[16,8,1280]{2,1,0:T(8,128)(2,1)S(1)}, bf16[16,8,1280]{2,1,0:T(8,128)(2,1)}, u32[]{:S(2)}) copy-start(bf16[16,8,1280]{2,1,0:T(8,128)(2,1)} %copy-done.26) | copy-start | bytes 983044
  316.0 13.6 %copy-start.29 = (bf16[16,8,1280]{2,1,0:T(8,128)(2,1)S(1)}, bf16[16,8,1280]{2,1,0:T(8,128)(2,1)}, u32[]{:S(2)}) copy-start(bf16[16,8,1280]{2,1,0:T(8,128)(2,1)} %copy-done.28) | copy-start | bytes 983044
  328.0 28.0 %collective-permute-start.5 = (bf16[32,8,1280]{2,1,0:T(8,128)(2,1)S(1)}, bf16[32,8,1280]{2,1,0:T(8,128)(2,1)S(1)}, u32[]{:S(2)}, u32[]{:S(2)}) collective-permute-start(bf16[32,8,1280]{2,1,0:T(8,128)(2,1)S(1)} %add_convert_fusion.4.rest_1_), channel_id=1, source_target_pairs={{0,1},{1,0},{2,3},{3,2},{4,5},{5,4},{6,7},{7,6}} | collective-permute-start | bytes 1966088 | tf_op jit(solution)/shard_map/ppermute | solution.py:477
  328.5 27.5 %collective-permute-start.6 = (bf16[32,8,1280]{2,1,0:T(8,128)(2,1)}, bf16[32,8,1280]{2,1,0:T(8,128)(2,1)S(1)}, u32[]{:S(2)}, u32[]{:S(2)}) collective-permute-start(bf16[32,8,1280]{2,1,0:T(8,128)(2,1)} %add_convert_fusion.3.rest_2_), channel_id=1, source_target_pairs={{0,1},{1,0},{2,3},{3,2},{4,5},{5,4},{6,7},{7,6}} | collective-permute-start | bytes 1966088 | tf_op jit(solution)/shard_map/ppermute | solution.py:477
  328.5 28.0 %collective-permute-start.12 = (bf16[32,8,1280]{2,1,0:T(8,128)(2,1)}, bf16[32,8,1280]{2,1,0:T(8,128)(2,1)S(1)}, u32[]{:S(2)}, u32[]{:S(2)}) collective-permute-start(bf16[32,8,1280]{2,1,0:T(8,128)(2,1)} %collective-permute-done.8.rest_8_), channel_id=1, source_target_pairs={{0,1},{1,0},{2,3},{3,2},{4,5},{5,4},{6,7},{7,6}} | collective-permute-start | bytes 1966088 | tf_op jit(solution)/shard_map/ppermute | solution.py:479
  329.0 27.5 %collective-permute-start.13 = (bf16[32,8,1280]{2,1,0:T(8,128)(2,1)}, bf16[32,8,1280]{2,1,0:T(8,128)(2,1)S(1)}, u32[]{:S(2)}, u32[]{:S(2)}) collective-permute-start(bf16[32,8,1280]{2,1,0:T(8,128)(2,1)} %collective-permute-done.9.rest_9_), channel_id=1, source_target_pairs={{0,1},{1,0},{2,3},{3,2},{4,5},{5,4},{6,7},{7,6}} | collective-permute-start | bytes 1966088 | tf_op jit(solution)/shard_map/ppermute | solution.py:479
  329.0 27.5 %collective-permute-start.14 = (bf16[32,8,1280]{2,1,0:T(8,128)(2,1)}, bf16[32,8,1280]{2,1,0:T(8,128)(2,1)S(1)}, u32[]{:S(2)}, u32[]{:S(2)}) collective-permute-start(bf16[32,8,1280]{2,1,0:T(8,128)(2,1)} %collective-permute-done.10.rest_10_), channel_id=1, source_target_pairs={{0,1},{1,0},{2,3},{3,2},{4,5},{5,4},{6,7},{7,6}} | collective-permute-start | bytes 1966088 | tf_op jit(solution)/shard_map/ppermute | solution.py:479
  355.9 11.7 %collective-permute-start.7 = (bf16[16,8,1280]{2,1,0:T(8,128)(2,1)S(1)}, bf16[16,8,1280]{2,1,0:T(8,128)(2,1)S(1)}, u32[]{:S(2)}, u32[]{:S(2)}) collective-permute-start(bf16[16,8,1280]{2,1,0:T(8,128)(2,1)S(1)} %copy-done.5), channel_id=1, source_target_pairs={{0,1},{1,0},{2,3},{3,2},{4,5},{5,4},{6,7},{7,6}} | collective-permute-start | bytes 983048 | tf_op jit(solution)/shard_map/ppermute | solution.py:477
  356.0 11.7 %collective-permute-start.15 = (bf16[16,8,1280]{2,1,0:T(8,128)(2,1)S(1)}, bf16[16,8,1280]{2,1,0:T(8,128)(2,1)S(1)}, u32[]{:S(2)}, u32[]{:S(2)}) collective-permute-start(bf16[16,8,1280]{2,1,0:T(8,128)(2,1)S(1)} %copy-done.15), channel_id=1, source_target_pairs={{0,1},{1,0},{2,3},{3,2},{4,5},{5,4},{6,7},{7,6}} | collective-permute-start | bytes 983048 | tf_op jit(solution)/shard_map/ppermute | solution.py:479
  (20 other events, 156.2 us)

commit v3 on v2

--- a/solution.py
+++ b/solution.py
@@ -17,10 +17,12 @@
 IN_DISPATCH = 16
 MIX_CALLS = 2
 MIX_SEQS = 2
+MIX_VMEM = 32
+COMBINE_VMEM = 32
 X_SLOTS = 6
 C_SLOTS = 8
 ROW_BLOCK = 256
-HIDDEN_TILE = 1280
+HIDDEN_TILE = 2560
 LANES = 128
 GROUPS = 4
 CHUNKS = (2, 2, 2, 4)
@@ -55,7 +57,8 @@
     return jnp.where(pos < length, mix, 0.0).astype(jnp.bfloat16)
 
 
-def mix_kernel(per_dev, seqs, idx_ref, len_ref, phi_ref, g_ref, x_ref, _, c_ref, v_ref):
+def mix_kernel(per_dev, seqs, idx_ref, len_ref, phi_ref, g_ref, x_ref, *rest):
+    c_ref, v_ref = rest[-2:]
     s = idx_ref[0]
     i = pl.program_id(0)
 
@@ -75,11 +78,13 @@
 def mix_weights(part, tokens, lengths, phi, scale, per_dev, mix):
     batch, n_tok, dim = tokens.shape
     n_slots = phi.shape[1]
-    count = (batch // 2 - IN_DISPATCH) // MIX_CALLS
+    left = batch // 2 - IN_DISPATCH
+    count = left // MIX_CALLS
     seqs = MIX_SEQS
     start = lax.rem(lax.axis_index("model") * (batch // 2) + batch // 2 + IN_DISPATCH + part * count, batch)
     index = jnp.stack([lax.axis_index("seq"), start // seqs]).astype(jnp.int32)
-    block = lambda i, idx, _: (idx[1] + i, 0, 0)
+    first = part * count // seqs
+    args = [index, lengths, phi, scale, tokens] + ([] if mix is None else [mix])
     return pl.pallas_call(
         functools.partial(mix_kernel, per_dev, seqs),
         grid_spec=pltpu.PrefetchScalarGridSpec(
@@ -88,18 +93,17 @@
             in_specs=[
                 pl.BlockSpec((dim, n_slots), lambda i, *_: (0, 0)),
                 pl.BlockSpec(memory_space=pltpu.SMEM),
-                pl.BlockSpec((seqs, n_tok, dim), block),
-                pl.BlockSpec(memory_space=pl.ANY),
-            ],
-            out_specs=pl.BlockSpec((seqs, n_tok, n_slots), block),
+                pl.BlockSpec((seqs, n_tok, dim), lambda i, idx, _: (idx[1] + i, 0, 0)),
+            ] + ([] if mix is None else [pl.BlockSpec(memory_space=pl.ANY)]),
+            out_specs=pl.BlockSpec((seqs, n_tok, n_slots), lambda i, *_: (first + i, 0, 0)),
             scratch_shapes=[pltpu.VMEM((dim, n_slots), jnp.bfloat16)],
         ),
-        out_shape=jax.ShapeDtypeStruct(mix.shape, mix.dtype),
-        input_output_aliases={5: 0},
-        compiler_params=pltpu.CompilerParams(dimension_semantics=("arbitrary",), vmem_limit_bytes=32 * 1024 * 1024),
+        out_shape=jax.ShapeDtypeStruct((left, n_tok, n_slots), jnp.bfloat16),
+        input_output_aliases={} if mix is None else {5: 0},
+        compiler_params=pltpu.CompilerParams(dimension_semantics=("arbitrary",), vmem_limit_bytes=MIX_VMEM * 1024 * 1024),
         cost_estimate=pl.CostEstimate(flops=4 * count * n_tok * n_slots * dim, bytes_accessed=2 * count * n_tok * dim, transcendentals=0),
         name="mix",
-    )(index, lengths, phi, scale, tokens, mix)
+    )(*args)
 
 
 def dispatch_kernel(n_half, n_tok, n_slots, per_dev, phi_ref, len_ref, g_ref, x_hbm, xs_hbm, c_hbm,
@@ -409,17 +413,18 @@
     )(xs, w_in, w_out)
 
 
-def combine_kernel(first, n_tok, n_pieces, len_ref, off_ref, c_ref, *rest):
-    pieces, out_ref = rest[:n_pieces], rest[-1]
+def combine_kernel(first, n_tok, n_pieces, extra, len_ref, off_ref, c_ref, *rest):
+    pieces, out_ref = rest[extra:extra + n_pieces], rest[-1]
     pos = off_ref[0] + lax.broadcasted_iota(jnp.int32, (n_tok, 1), 0)
     for i in range(COMBINE_SEQS):
         slots = jnp.concatenate([p[i] for p in pieces], axis=0)
-        mixed = jnp.dot(c_ref[i], slots, preferred_element_type=jnp.float32)
+        mix = jnp.where(off_ref[1] == first, rest[0][i], c_ref[i]) if extra else c_ref[i]
+        mixed = jnp.dot(mix, slots, preferred_element_type=jnp.float32)
         ok = pos < len_ref[first + pl.program_id(0) * COMBINE_SEQS + i]
         out_ref[i] = jnp.where(ok, mixed, 0.0).astype(jnp.bfloat16)
 
 
-def combine(chunk, mix, pieces, lengths, offset, y):
+def combine(chunk, mix, left, pieces, lengths, offset, y):
     batch, n_tok, n_slots = mix.shape
     _, grp, dim = pieces[0][0].shape
     cs = COMBINE_SEQS
@@ -429,17 +434,18 @@
     base = first // cs
     in_specs = [
         pl.BlockSpec((cs, n_tok, n_slots), lambda b, *_: (base + b, 0, 0)),
+        *([] if left is None else [pl.BlockSpec((cs, n_tok, n_slots), lambda b, *_: (b, 0, 0))]),
         *[pl.BlockSpec((cs, grp, dim), functools.partial(lambda at, b, *_: (at // cs + b, 0, 0), at)) for _, at in pieces],
     ]
     pieces = [p for p, _ in pieces]
-    args = [lengths, offset, mix, *pieces]
+    args = [lengths, offset, mix, *([] if left is None else [left]), *pieces]
     alias = {}
     if y is not None:
         in_specs.append(pl.BlockSpec(memory_space=pl.ANY))
         args.append(y)
         alias = {len(args) - 1: 0}
     return pl.pallas_call(
-        functools.partial(combine_kernel, first, n_tok, n_p),
+        functools.partial(combine_kernel, first, n_tok, n_p, 0 if left is None else 1),
         grid_spec=pltpu.PrefetchScalarGridSpec(
             num_scalar_prefetch=2,
             grid=(step // cs,),
@@ -448,7 +454,7 @@
         ),
         out_shape=jax.ShapeDtypeStruct((batch, n_tok, dim), jnp.bfloat16),
         input_output_aliases=alias,
-        compiler_params=pltpu.CompilerParams(dimension_semantics=("arbitrary",), vmem_limit_bytes=32 * 1024 * 1024),
+        compiler_params=pltpu.CompilerParams(dimension_semantics=("arbitrary",), vmem_limit_bytes=COMBINE_VMEM * 1024 * 1024),
         cost_estimate=pl.CostEstimate(flops=2 * 2 * step * n_tok * n_slots * dim, bytes_accessed=2 * step * n_tok * (dim + n_slots), transcendentals=0),
         name="combine",
     )(*args)
@@ -464,7 +470,9 @@
         n_tok = tokens.shape[1]
         per_dev = slot_params.shape[1] // seq_size
         slot_per = per_dev // w_in.shape[0]
-        offset = (lax.axis_index("seq") * n_tok).reshape(1).astype(jnp.int32)
+        batch = tokens.shape[0]
+        left_first = lax.rem(lax.axis_index("model") * (batch // 2) + batch // 2 + IN_DISPATCH, batch)
+        offset = jnp.stack([lax.axis_index("seq") * n_tok, left_first]).astype(jnp.int32)
         xs, mix = dispatch(tokens, lengths, slot_params, logit_scale.reshape(1), per_dev)
         table = {}
         for group in range(GROUPS):
@@ -477,8 +485,9 @@
                 table[k, group, 1] = lax.ppermute(own, "seq", swap_c)
                 table[k, group, 2] = across
                 table[k, group, 3] = lax.ppermute(across, "seq", swap_c)
+        left = None
         for part in range(MIX_CALLS):
-            mix = mix_weights(part, tokens, lengths, slot_params, logit_scale.reshape(1), per_dev, mix)
+            left = mix_weights(part, tokens, lengths, slot_params, logit_scale.reshape(1), per_dev, left)
         y = None
         for k in range(MIX_CHUNKS):
             pieces = []
@@ -486,7 +495,7 @@
                 for group in range(GROUPS):
                     per = MIX_CHUNKS // CHUNKS[group]
                     pieces.append((table[k // per, group, q], k % per * (tokens.shape[0] // MIX_CHUNKS)))
-            y = combine(k, mix, pieces, lengths, offset, y)
+            y = combine(k, mix, left if k % 2 else None, pieces, lengths, offset, y)
         return y
 
 

time: 380 us -> 367 us (0.966)
  local copies, waits for them, and re-layouts: 14 us -> 4.31 us
    unnamed x88 -> x86, local copies, waits for them, and re-layouts: 14 us -> 4.31 us
  transfers between devices with their start and end apart: 40 -> 40, of which waited for: 15 -> 14; matrix products, arithmetic and copies ran while one was open for 1% -> 1% of each run, Pallas kernels for 25% -> 26%
where the time goes in v3:
time: 367 us
  Pallas kernels  200 us (54%)
  waiting for transfers between devices  134 us (37%)
  starting transfers between devices  24.2 us (7%)
  local copies, waits for them, and re-layouts  4.31 us (1%)
  other arithmetic  3.7 us (1%)
    ppermute x10, waiting for transfers between devices, local_layer(): across = lax.ppermute(own, 'seq', swap_x)  84.2 us
    pallas_call x1, Pallas kernels, dispatch(): pl.pallas_call(functools.partial(dispatch_kernel, half, n_tok, n_slots, p...  79.9 us
    pallas_call x4, Pallas kernels, ffn(): pl.pallas_call(functools.partial(ffn_kernel, batch, slot_per, n_out), gri...  56.9 us
    ppermute x10, waiting for transfers between devices, local_layer(): other = lax.ppermute(part, 'model', swap_y)  48.4 us
    pallas_call x4, Pallas kernels, combine(): pl.pallas_call(functools.partial(combine_kernel, first, n_tok, n_p, 0 if...  45.2 us
    pallas_call x2, Pallas kernels, mix_weights(): pl.pallas_call(functools.partial(mix_kernel, per_dev, seqs), grid_spec=pl...  17.7 us
    ppermute x10, starting transfers between devices, local_layer(): other = lax.ppermute(part, 'model', swap_y)  10.4 us
    ppermute x10, starting transfers between devices, local_layer(): across = lax.ppermute(own, 'seq', swap_x)  10.4 us
  transfers between devices with their start and end apart: 40, of which 14 were waited for; matrix products, arithmetic and copies ran while one was open for 1% of the time, Pallas kernels for 26%

profile of v3, /device:TPU:0, one launch (start us, length us, event | category | flops | bytes accessed | tf_op | source)
XLA Modules:
  0.0 366.5 jit_solution(7084220494036592724)
XLA Ops:
  0.7 79.9 %dispatch.1 = (bf16[64,32,1280]{2,1,0:T(8,128)(2,1)}, bf16[64,512,128]{2,1,0:T(8,128)(2,1)}) custom-call(bf16[1280,128]{1,0:T(8,128)(2,1)} %phi_ref.5, s32[64]{0:T(128)} %len_ref.13, f32[1]{0:T(128)} %bitcast.6.g_ref, bf16[64,512,1280]{2,1,0:T(8,128)(2,1)} %x_ref.3), custom_call_target="tpu_custom_call" | custom-call | tf_op jit(solution)/shard_map/dispatch/pallas_call | solution.py:298
  80.6 14.2 %ffn.7 = (bf16[16,8,1280]{2,1,0:T(8,128)(2,1)}, bf16[16,8,1280]{2,1,0:T(8,128)(2,1)}, bf16[16,8,1280]{2,1,0:T(8,128)(2,1)}, bf16[16,8,1280]{2,1,0:T(8,128)(2,1)}) custom-call(bf16[64,32,1280]{2,1,0:T(8,128)(2,1)} %get-tuple-element.18.x_ref, bf16[8,1280,2560]{2,1,0:T(8,128)(2,1)} %wi_ref.7, bf16[8,2560,1280]{2,1,0:T(8,128)(2,1)} %wo_ref.7), custom_call_target="tpu_custom_call" | custom-call | flops 6710886400 | bytes 26214400 | tf_op jit(solution)/shard_map/ffn/pallas_call | solution.py:393
  94.8 0.9 collective-permute-start.36
  95.7 14.2 %ffn.4 = (bf16[32,8,1280]{2,1,0:T(8,128)(2,1)}, bf16[32,8,1280]{2,1,0:T(8,128)(2,1)}) custom-call(bf16[64,32,1280]{2,1,0:T(8,128)(2,1)} %get-tuple-element.18.x_ref, bf16[8,1280,2560]{2,1,0:T(8,128)(2,1)} %wi_ref.7, bf16[8,2560,1280]{2,1,0:T(8,128)(2,1)} %wo_ref.7), custom_call_target="tpu_custom_call" | custom-call | flops 6710886400 | bytes 26214400 | tf_op jit(solution)/shard_map/ffn/pallas_call | solution.py:393
  109.9 1.1 collective-permute-start.20
  111.0 14.2 %ffn.5 = (bf16[32,8,1280]{2,1,0:T(8,128)(2,1)}, bf16[32,8,1280]{2,1,0:T(8,128)(2,1)}) custom-call(bf16[64,32,1280]{2,1,0:T(8,128)(2,1)} %get-tuple-element.18.x_ref, bf16[8,1280,2560]{2,1,0:T(8,128)(2,1)} %wi_ref.7, bf16[8,2560,1280]{2,1,0:T(8,128)(2,1)} %wo_ref.7), custom_call_target="tpu_custom_call" | custom-call | flops 6710886400 | bytes 26214400 | tf_op jit(solution)/shard_map/ffn/pallas_call | solution.py:393
  125.3 0.9 collective-permute-start.21
  126.2 14.2 %ffn.6 = (bf16[32,8,1280]{2,1,0:T(8,128)(2,1)}, bf16[32,8,1280]{2,1,0:T(8,128)(2,1)}) custom-call(bf16[64,32,1280]{2,1,0:T(8,128)(2,1)} %get-tuple-element.18.x_ref, bf16[8,1280,2560]{2,1,0:T(8,128)(2,1)} %wi_ref.7, bf16[8,2560,1280]{2,1,0:T(8,128)(2,1)} %wo_ref.7), custom_call_target="tpu_custom_call" | custom-call | flops 6710886400 | bytes 26214400 | tf_op jit(solution)/shard_map/ffn/pallas_call | solution.py:393
  140.4 1.2 collective-permute-start.22
  141.5 0.9 collective-permute-start.23
  142.4 1.2 collective-permute-start.16
  143.7 21.5 %collective-permute-done.23 = bf16[16,8,1280]{2,1,0:T(8,128)(2,1)S(1)} collective-permute-done((bf16[16,8,1280]{2,1,0:T(8,128)(2,1)S(1)}, bf16[16,8,1280]{2,1,0:T(8,128)(2,1)S(1)}, u32[]{:S(2)}, u32[]{:S(2)}) %collective-permute-start.23) | collective-permute-done | bytes 327712 | tf_op jit(solution)/shard_map/ppermute | solution.py:481
  165.2 1.2 collective-permute-start.2
  166.5 5.7 %collective-permute-done.16 = bf16[16,8,1280]{2,1,0:T(8,128)(2,1)S(1)} collective-permute-done((bf16[16,8,1280]{2,1,0:T(8,128)(2,1)S(1)}, bf16[16,8,1280]{2,1,0:T(8,128)(2,1)S(1)}, u32[]{:S(2)}, u32[]{:S(2)}) %collective-permute-start.16) | collective-permute-done | bytes 327712 | tf_op jit(solution)/shard_map/ppermute | solution.py:481
  172.2 1.2 collective-permute-start.3
  173.5 17.7 %collective-permute-done.3 = bf16[16,8,1280]{2,1,0:T(8,128)(2,1)S(1)} collective-permute-done((bf16[16,8,1280]{2,1,0:T(8,128)(2,1)S(1)}, bf16[16,8,1280]{2,1,0:T(8,128)(2,1)S(1)}, u32[]{:S(2)}, u32[]{:S(2)}) %collective-permute-start.3) | collective-permute-done | bytes 327712 | tf_op jit(solution)/shard_map/ppermute | solution.py:481
  191.2 1.1 collective-permute-start.38
  192.4 0.2 add_convert_fusion.2.rest_0_.rest_1_
  192.6 6.2 %collective-permute-done.38.rest_11_ = bf16[16,8,1280]{2,1,0:T(8,128)(2,1)S(1)} collective-permute-done((bf16[16,8,1280]{2,1,0:T(8,128)(2,1)S(1)}, bf16[16,8,1280]{2,1,0:T(8,128)(2,1)S(1)}, u32[]{:S(2)}, u32[]{:S(2)}) %collective-permute-start.38) | collective-permute-done | bytes 327712 | tf_op jit(solution)/shard_map/ppermute | solution.py:483
  198.8 0.9 collective-permute-start.1
  199.8 1.1 collective-permute-start
  200.8 1.0 collective-permute-start.31
  201.9 0.2 add_convert_fusion.1.rest_1_.rest_2_
  202.1 0.5 copy-done.17
  202.6 7.0 %collective-permute-done.31.rest_12_ = bf16[16,8,1280]{2,1,0:T(8,128)(2,1)S(1)} collective-permute-done((bf16[16,8,1280]{2,1,0:T(8,128)(2,1)S(1)}, bf16[16,8,1280]{2,1,0:T(8,128)(2,1)S(1)}, u32[]{:S(2)}, u32[]{:S(2)}) %collective-permute-start.31) | collective-permute-done | bytes 327712 | tf_op jit(solution)/shard_map/ppermute | solution.py:483
  209.6 1.1 collective-permute-start.18
  210.7 0.2 add_convert_fusion.rest_2_.rest_3_
  210.9 0.5 copy-done.23
  211.4 7.8 %collective-permute-done.18.rest_11_ = bf16[16,8,1280]{2,1,0:T(8,128)(2,1)S(1)} collective-permute-done((bf16[16,8,1280]{2,1,0:T(8,128)(2,1)S(1)}, bf16[16,8,1280]{2,1,0:T(8,128)(2,1)S(1)}, u32[]{:S(2)}, u32[]{:S(2)}) %collective-permute-start.18) | collective-permute-done | bytes 327712 | tf_op jit(solution)/shard_map/ppermute | solution.py:483
  219.2 1.1 collective-permute-start.11
  220.3 0.9 collective-permute-start.28
  221.2 1.1 collective-permute-start.29
  222.4 0.9 collective-permute-start.30
  223.3 3.4 collective-permute-done
  226.7 0.2 add_convert_fusion.3.rest_2_.rest_3_
  226.8 0.7 copy-done.31
  227.5 2.3 collective-permute-done.11.rest_12_
  229.8 0.5 collective-permute-start.19
  230.3 0.2 add_convert_fusion.4.rest_1_.rest_2_
  230.5 0.9 collective-permute-done.35.rest_16_
  231.4 0.7 copy-done.25
  232.3 0.7 copy-done.13
  233.0 0.4 collective-permute-start.25
  233.4 10.5 %collective-permute-done.28.rest_8_.rest_9_ = bf16[32,8,1280]{2,1,0:T(8,128)(2,1)} collective-permute-done((bf16[32,8,1280]{2,1,0:T(8,128)(2,1)S(1)}, bf16[32,8,1280]{2,1,0:T(8,128)(2,1)}, u32[]{:S(2)}, u32[]{:S(2)}) %collective-permute-start.28) | collective-permute-done | bytes 655392 | tf_op jit(solution)/shard_map/ppermute | solution.py:483
  243.9 14.0 %collective-permute-done.29.rest_9_.rest_10_ = bf16[32,8,1280]{2,1,0:T(8,128)(2,1)} collective-permute-done((bf16[32,8,1280]{2,1,0:T(8,128)(2,1)S(1)}, bf16[32,8,1280]{2,1,0:T(8,128)(2,1)}, u32[]{:S(2)}, u32[]{:S(2)}) %collective-permute-start.29) | collective-permute-done | bytes 655392 | tf_op jit(solution)/shard_map/ppermute | solution.py:483
  258.0 1.1 collective-permute-start.10
  259.1 12.9 %collective-permute-done.30.rest_10_.rest_11_ = bf16[32,8,1280]{2,1,0:T(8,128)(2,1)} collective-permute-done((bf16[32,8,1280]{2,1,0:T(8,128)(2,1)S(1)}, bf16[32,8,1280]{2,1,0:T(8,128)(2,1)}, u32[]{:S(2)}, u32[]{:S(2)}) %collective-permute-start.30) | collective-permute-done | bytes 655392 | tf_op jit(solution)/shard_map/ppermute | solution.py:483
  272.0 1.1 collective-permute-start.9
  273.2 2.3 add_convert_fusion.5.rest_0_.rest_1_
  275.6 0.9 collective-permute-start.8
  276.5 0.2 collective-permute-start.32
  276.7 9.4 %collective-permute-done.10.rest_10_.rest_11_ = bf16[32,8,1280]{2,1,0:T(8,128)(2,1)} collective-permute-done((bf16[32,8,1280]{2,1,0:T(8,128)(2,1)S(1)}, bf16[32,8,1280]{2,1,0:T(8,128)(2,1)}, u32[]{:S(2)}, u32[]{:S(2)}) %collective-permute-start.10) | collective-permute-done | bytes 655392 | tf_op jit(solution)/shard_map/ppermute | solution.py:483
  286.1 14.0 %collective-permute-done.9.rest_9_.rest_10_ = bf16[32,8,1280]{2,1,0:T(8,128)(2,1)} collective-permute-done((bf16[32,8,1280]{2,1,0:T(8,128)(2,1)S(1)}, bf16[32,8,1280]{2,1,0:T(8,128)(2,1)}, u32[]{:S(2)}, u32[]{:S(2)}) %collective-permute-start.9) | collective-permute-done | bytes 655392 | tf_op jit(solution)/shard_map/ppermute | solution.py:483
  300.3 1.0 copy-done
  301.2 8.6 %mix.2.rest_0_ = bf16[16,512,128]{2,1,0:T(8,128)(2,1)S(1)} custom-call(s32[2]{0:T(128)S(1)} %pad_add_fusion.2.idx_ref, s32[64]{0:T(128)S(1)} %copy-done.29, bf16[1280,128]{1,0:T(8,128)(2,1)S(1)} %copy-done, f32[1]{0:T(128)} %bitcast.7.g_ref, bf16[64,512,1280]{2,1,0:T(8,128)(2,1)} %x_ref.3), custom_call_target="tpu_custom_call" | custom-call | flops 2684354560 | bytes 10485760 | tf_op jit(solution)/shard_map/mix/pallas_call | solution.py:88
  309.9 9.1 %mix.3.rest_0_ = bf16[16,512,128]{2,1,0:T(8,128)(2,1)S(1)} custom-call(s32[2]{0:T(128)S(1)} %pad_add_fusion.1.idx_ref, s32[64]{0:T(128)S(1)} %copy-done.29, bf16[1280,128]{1,0:T(8,128)(2,1)S(1)} %copy-done, f32[1]{0:T(128)} %bitcast.8.g_ref, bf16[64,512,1280]{2,1,0:T(8,128)(2,1)} %x_ref.3, ...), custom_call_target="tpu_custom_call", output_to_operand_aliasing={{}: (5, {})} | custom-call | flops 2684354560 | bytes 10485760 | tf_op jit(solution)/shard_map/mix/pallas_call | solution.py:88
  319.0 0.5 collective-permute-start.5
  319.6 0.5 collective-permute-start.14
  320.1 0.5 collective-permute-start.12
  320.6 11.5 %combine.4.rest_17_ = bf16[64,512,1280]{2,1,0:T(8,128)(2,1)} custom-call(s32[64]{0:T(128)S(1)} %copy-done.29, s32[2]{0:T(128)S(1)} %pad_add_fusion.off_ref, bf16[64,512,128]{2,1,0:T(8,128)(2,1)S(1)} %bitcast.10, bf16[32,8,1280]{2,1,0:T(8,128)(2,1)S(1)} %add_convert_fusion.2.rest_0_.rest_1_, bf16[32,8,1280]{2,1,0:T(8,128)(2,1)S(1)} %add_convert_fusion.1.rest_1_.rest_2_, ...), custom_call_target="tpu_custom_call" | custom-call | flops 5368709120 | bytes 23068672 | tf_op jit(solution)/shard_map/combine/pallas_call | solution.py:447
  332.2 11.5 %combine.5.rest_16_ = bf16[64,512,1280]{2,1,0:T(8,128)(2,1)} custom-call(s32[64]{0:T(128)S(1)} %copy-done.29, s32[2]{0:T(128)S(1)} %pad_add_fusion.off_ref, bf16[64,512,128]{2,1,0:T(8,128)(2,1)S(1)} %bitcast.10, bf16[16,512,128]{2,1,0:T(8,128)(2,1)S(1)} %mix.3.rest_0_, ...), custom_call_target="tpu_custom_call", output_to_operand_aliasing={{}: (20, {})} | custom-call | flops 5368709120 | bytes 23068672 | tf_op jit(solution)/shard_map/combine/pallas_call | solution.py:447
  343.7 0.5 collective-permute-start.15
  344.2 11.1 %combine.6.rest_17_ = bf16[64,512,1280]{2,1,0:T(8,128)(2,1)} custom-call(s32[64]{0:T(128)S(1)} %copy-done.29, s32[2]{0:T(128)S(1)} %pad_add_fusion.off_ref, bf16[64,512,128]{2,1,0:T(8,128)(2,1)S(1)} %bitcast.10, bf16[32,8,1280]{2,1,0:T(8,128)(2,1)} %add_convert_fusion.5.rest_0_.rest_1_, ...), custom_call_target="tpu_custom_call", output_to_operand_aliasing={{}: (19, {})} | custom-call | flops 5368709120 | bytes 23068672 | tf_op jit(solution)/shard_map/combine/pallas_call | solution.py:447
  355.4 11.1 %combine.7 = bf16[64,512,1280]{2,1,0:T(8,128)(2,1)} custom-call(s32[64]{0:T(128)S(1)} %copy-done.29, s32[2]{0:T(128)S(1)} %pad_add_fusion.off_ref, bf16[64,512,128]{2,1,0:T(8,128)(2,1)S(1)} %bitcast.10, bf16[16,512,128]{2,1,0:T(8,128)(2,1)S(1)} %mix.3.rest_0_, ...), custom_call_target="tpu_custom_call", output_to_operand_aliasing={{}: (20, {})} | custom-call | flops 5368709120 | bytes 23068672 | tf_op jit(solution)/shard_map/combine/pallas_call | solution.py:447
  (127 shorter events, 1.2 us)
Async XLA Ops:
  94.8 47.6 %collective-permute-start.36 = (bf16[16,8,1280]{2,1,0:T(8,128)(2,1)}, bf16[16,8,1280]{2,1,0:T(8,128)(2,1)S(1)}, u32[]{:S(2)}, u32[]{:S(2)}) collective-permute-start(bf16[16,8,1280]{2,1,0:T(8,128)(2,1)} %get-tuple-element.28), channel_id=1, source_target_pairs={{0,4},{4,0},{1,5},{5,1},{2,6},{6,2},{3,7},{7,3}} | collective-permute-start | bytes 983048 | tf_op jit(solution)/shard_map/ppermute | solution.py:481
  109.9 82.5 %collective-permute-start.20 = (bf16[32,8,1280]{2,1,0:T(8,128)(2,1)}, bf16[32,8,1280]{2,1,0:T(8,128)(2,1)S(1)}, u32[]{:S(2)}, u32[]{:S(2)}) collective-permute-start(bf16[32,8,1280]{2,1,0:T(8,128)(2,1)} %get-tuple-element.24), channel_id=1, source_target_pairs={{0,4},{4,0},{1,5},{5,1},{2,6},{6,2},{3,7},{7,3}} | collective-permute-start | bytes 1966088 | tf_op jit(solution)/shard_map/ppermute | solution.py:481
  125.3 16.3 %copy-start.39 = (bf16[16,8,1280]{2,1,0:T(8,128)(2,1)S(1)}, bf16[16,8,1280]{2,1,0:T(8,128)(2,1)}, u32[]{:S(2)}) copy-start(bf16[16,8,1280]{2,1,0:T(8,128)(2,1)} %get-tuple-element.27) | copy-start | bytes 983044
  125.3 17.1 %copy-start.38 = (bf16[16,8,1280]{2,1,0:T(8,128)(2,1)S(1)}, bf16[16,8,1280]{2,1,0:T(8,128)(2,1)}, u32[]{:S(2)}) copy-start(bf16[16,8,1280]{2,1,0:T(8,128)(2,1)} %get-tuple-element.23) | copy-start | bytes 983044
  125.3 18.3 %copy-start.40 = (bf16[16,8,1280]{2,1,0:T(8,128)(2,1)S(1)}, bf16[16,8,1280]{2,1,0:T(8,128)(2,1)}, u32[]{:S(2)}) copy-start(bf16[16,8,1280]{2,1,0:T(8,128)(2,1)} %get-tuple-element.28) | copy-start | bytes 983044
  125.3 74.5 %collective-permute-start.21 = (bf16[32,8,1280]{2,1,0:T(8,128)(2,1)}, bf16[32,8,1280]{2,1,0:T(8,128)(2,1)S(1)}, u32[]{:S(2)}, u32[]{:S(2)}) collective-permute-start(bf16[32,8,1280]{2,1,0:T(8,128)(2,1)} %get-tuple-element.25), channel_id=1, source_target_pairs={{0,4},{4,0},{1,5},{5,1},{2,6},{6,2},{3,7},{7,3}} | collective-permute-start | bytes 1966088 | tf_op jit(solution)/shard_map/ppermute | solution.py:481
  140.4 31.9 %copy-start.37 = (bf16[16,8,1280]{2,1,0:T(8,128)(2,1)S(1)}, bf16[16,8,1280]{2,1,0:T(8,128)(2,1)}, u32[]{:S(2)}) copy-start(bf16[16,8,1280]{2,1,0:T(8,128)(2,1)} %get-tuple-element.22) | copy-start | bytes 983044
  140.4 60.5 %collective-permute-start.22 = (bf16[32,8,1280]{2,1,0:T(8,128)(2,1)}, bf16[32,8,1280]{2,1,0:T(8,128)(2,1)S(1)}, u32[]{:S(2)}, u32[]{:S(2)}) collective-permute-start(bf16[32,8,1280]{2,1,0:T(8,128)(2,1)} %get-tuple-element.26), channel_id=1, source_target_pairs={{0,4},{4,0},{1,5},{5,1},{2,6},{6,2},{3,7},{7,3}} | collective-permute-start | bytes 1966088 | tf_op jit(solution)/shard_map/ppermute | solution.py:481
  141.5 23.7 %collective-permute-start.23 = (bf16[16,8,1280]{2,1,0:T(8,128)(2,1)S(1)}, bf16[16,8,1280]{2,1,0:T(8,128)(2,1)S(1)}, u32[]{:S(2)}, u32[]{:S(2)}) collective-permute-start(bf16[16,8,1280]{2,1,0:T(8,128)(2,1)S(1)} %copy-done.39), channel_id=1, source_target_pairs={{0,4},{4,0},{1,5},{5,1},{2,6},{6,2},{3,7},{7,3}} | collective-permute-start | bytes 983048 | tf_op jit(solution)/shard_map/ppermute | solution.py:481
  142.4 29.8 %collective-permute-start.16 = (bf16[16,8,1280]{2,1,0:T(8,128)(2,1)S(1)}, bf16[16,8,1280]{2,1,0:T(8,128)(2,1)S(1)}, u32[]{:S(2)}, u32[]{:S(2)}) collective-permute-start(bf16[16,8,1280]{2,1,0:T(8,128)(2,1)S(1)} %copy-done.38), channel_id=1, source_target_pairs={{0,4},{4,0},{1,5},{5,1},{2,6},{6,2},{3,7},{7,3}} | collective-permute-start | bytes 983048 | tf_op jit(solution)/shard_map/ppermute | solution.py:481
  143.6 48.7 %copy-start.5 = (bf16[16,8,1280]{2,1,0:T(8,128)(2,1)}, bf16[16,8,1280]{2,1,0:T(8,128)(2,1)S(1)}, u32[]{:S(2)}) copy-start(bf16[16,8,1280]{2,1,0:T(8,128)(2,1)S(1)} %add_convert_fusion.6.rest_3_) | copy-start | bytes 983044
  165.2 27.2 %copy-start.36 = (bf16[32,8,1280]{2,1,0:T(8,128)(2,1)S(1)}, bf16[32,8,1280]{2,1,0:T(8,128)(2,1)}, u32[]{:S(2)}) copy-start(bf16[32,8,1280]{2,1,0:T(8,128)(2,1)} %get-tuple-element.24) | copy-start | bytes 1966084
  165.2 56.0 %collective-permute-start.2 = (bf16[32,8,1280]{2,1,0:T(8,128)(2,1)}, bf16[32,8,1280]{2,1,0:T(8,128)(2,1)S(1)}, u32[]{:S(2)}, u32[]{:S(2)}) collective-permute-start(bf16[32,8,1280]{2,1,0:T(8,128)(2,1)} %get-tuple-element.21), channel_id=1, source_target_pairs={{0,4},{4,0},{1,5},{5,1},{2,6},{6,2},{3,7},{7,3}} | collective-permute-start | bytes 1966088 | tf_op jit(solution)/shard_map/ppermute | solution.py:481
  166.5 35.4 %copy-start.7 = (bf16[16,8,1280]{2,1,0:T(8,128)(2,1)}, bf16[16,8,1280]{2,1,0:T(8,128)(2,1)S(1)}, u32[]{:S(2)}) copy-start(bf16[16,8,1280]{2,1,0:T(8,128)(2,1)S(1)} %add_convert_fusion.7.rest_4_) | copy-start | bytes 983044
  172.2 19.0 %collective-permute-start.3 = (bf16[16,8,1280]{2,1,0:T(8,128)(2,1)S(1)}, bf16[16,8,1280]{2,1,0:T(8,128)(2,1)S(1)}, u32[]{:S(2)}, u32[]{:S(2)}) collective-permute-start(bf16[16,8,1280]{2,1,0:T(8,128)(2,1)S(1)} %copy-done.37), channel_id=1, source_target_pairs={{0,4},{4,0},{1,5},{5,1},{2,6},{6,2},{3,7},{7,3}} | collective-permute-start | bytes 983048 | tf_op jit(solution)/shard_map/ppermute | solution.py:481
  173.5 37.2 %copy-start.1 = (bf16[16,8,1280]{2,1,0:T(8,128)(2,1)}, bf16[16,8,1280]{2,1,0:T(8,128)(2,1)S(1)}, u32[]{:S(2)}) copy-start(bf16[16,8,1280]{2,1,0:T(8,128)(2,1)S(1)} %add_convert_fusion.8.rest_3_) | copy-start | bytes 983044
  173.5 25.3 %copy-start.32 = (bf16[32,8,1280]{2,1,0:T(8,128)(2,1)S(1)}, bf16[32,8,1280]{2,1,0:T(8,128)(2,1)}, u32[]{:S(2)}) copy-start(bf16[32,8,1280]{2,1,0:T(8,128)(2,1)} %get-tuple-element.20) | copy-start | bytes 1966084
  173.5 26.3 %copy-start.30 = (bf16[32,8,1280]{2,1,0:T(8,128)(2,1)S(1)}, bf16[32,8,1280]{2,1,0:T(8,128)(2,1)}, u32[]{:S(2)}) copy-start(bf16[32,8,1280]{2,1,0:T(8,128)(2,1)} %get-tuple-element.19) | copy-start | bytes 1966084
  173.5 28.4 %copy-start.35 = (bf16[32,8,1280]{2,1,0:T(8,128)(2,1)S(1)}, bf16[32,8,1280]{2,1,0:T(8,128)(2,1)}, u32[]{:S(2)}) copy-start(bf16[32,8,1280]{2,1,0:T(8,128)(2,1)} %get-tuple-element.25) | copy-start | bytes 1966084
  191.2 7.6 %collective-permute-start.38 = (bf16[16,8,1280]{2,1,0:T(8,128)(2,1)S(1)}, bf16[16,8,1280]{2,1,0:T(8,128)(2,1)S(1)}, u32[]{:S(2)}, u32[]{:S(2)}) collective-permute-start(bf16[16,8,1280]{2,1,0:T(8,128)(2,1)S(1)} %add_convert_fusion.6.rest_3_), channel_id=1, source_target_pairs={{0,2},{1,3},{2,0},{3,1},{4,6},{5,7},{6,4},{7,5}} | collective-permute-start | bytes 983048 | tf_op jit(solution)/shard_map/ppermute | solution.py:483
  192.4 26.8 %copy-start.3 = (bf16[16,8,1280]{2,1,0:T(8,128)(2,1)}, bf16[16,8,1280]{2,1,0:T(8,128)(2,1)S(1)}, u32[]{:S(2)}) copy-start(bf16[16,8,1280]{2,1,0:T(8,128)(2,1)S(1)} %add_convert_fusion.9.rest_4_) | copy-start | bytes 983044
  192.4 9.5 %collective-permute-start.37 = (bf16[16,8,1280]{2,1,0:T(8,128)(2,1)S(1)}, bf16[16,8,1280]{2,1,0:T(8,128)(2,1)S(1)}, u32[]{:S(2)}, u32[]{:S(2)}) collective-permute-start(bf16[16,8,1280]{2,1,0:T(8,128)(2,1)S(1)} %add_convert_fusion.6.rest_3_), channel_id=1, source_target_pairs={{0,1},{1,0},{2,3},{3,2},{4,5},{5,4},{6,7},{7,6}} | collective-permute-start | bytes 983048 | tf_op jit(solution)/shard_map/ppermute | solution.py:485
  192.6 18.1 %copy-start.34 = (bf16[32,8,1280]{2,1,0:T(8,128)(2,1)S(1)}, bf16[32,8,1280]{2,1,0:T(8,128)(2,1)}, u32[]{:S(2)}) copy-start(bf16[32,8,1280]{2,1,0:T(8,128)(2,1)} %get-tuple-element.26) | copy-start | bytes 1966084
  198.8 27.8 %copy-start.15 = (bf16[16,8,1280]{2,1,0:T(8,128)(2,1)}, bf16[16,8,1280]{2,1,0:T(8,128)(2,1)S(1)}, u32[]{:S(2)}) copy-start(bf16[16,8,1280]{2,1,0:T(8,128)(2,1)S(1)} %collective-permute-done.38.rest_11_) | copy-start | bytes 983044
  198.8 23.5 %collective-permute-start.1 = (bf16[32,8,1280]{2,1,0:T(8,128)(2,1)S(1)}, bf16[32,8,1280]{2,1,0:T(8,128)(2,1)S(1)}, u32[]{:S(2)}, u32[]{:S(2)}) collective-permute-start(bf16[32,8,1280]{2,1,0:T(8,128)(2,1)S(1)} %copy-done.32), channel_id=1, source_target_pairs={{0,4},{4,0},{1,5},{5,1},{2,6},{6,2},{3,7},{7,3}} | collective-permute-start | bytes 1966088 | tf_op jit(solution)/shard_map/ppermute | solution.py:481
  199.8 26.9 %collective-permute-start = (bf16[32,8,1280]{2,1,0:T(8,128)(2,1)S(1)}, bf16[32,8,1280]{2,1,0:T(8,128)(2,1)S(1)}, u32[]{:S(2)}, u32[]{:S(2)}) collective-permute-start(bf16[32,8,1280]{2,1,0:T(8,128)(2,1)S(1)} %copy-done.30), channel_id=1, source_target_pairs={{0,4},{4,0},{1,5},{5,1},{2,6},{6,2},{3,7},{7,3}} | collective-permute-start | bytes 1966088 | tf_op jit(solution)/shard_map/ppermute | solution.py:481
  200.8 8.7 %collective-permute-start.31 = (bf16[16,8,1280]{2,1,0:T(8,128)(2,1)S(1)}, bf16[16,8,1280]{2,1,0:T(8,128)(2,1)S(1)}, u32[]{:S(2)}, u32[]{:S(2)}) collective-permute-start(bf16[16,8,1280]{2,1,0:T(8,128)(2,1)S(1)} %add_convert_fusion.7.rest_4_), channel_id=1, source_target_pairs={{0,2},{1,3},{2,0},{3,1},{4,6},{5,7},{6,4},{7,5}} | collective-permute-start | bytes 983048 | tf_op jit(solution)/shard_map/ppermute | solution.py:483
  201.9 8.8 %collective-permute-start.27 = (bf16[16,8,1280]{2,1,0:T(8,128)(2,1)S(1)}, bf16[16,8,1280]{2,1,0:T(8,128)(2,1)S(1)}, u32[]{:S(2)}, u32[]{:S(2)}) collective-permute-start(bf16[16,8,1280]{2,1,0:T(8,128)(2,1)S(1)} %add_convert_fusion.7.rest_4_), channel_id=1, source_target_pairs={{0,1},{1,0},{2,3},{3,2},{4,5},{5,4},{6,7},{7,6}} | collective-permute-start | bytes 983048 | tf_op jit(solution)/shard_map/ppermute | solution.py:485
  202.6 24.1 %copy-start.33 = (bf16[32,8,1280]{2,1,0:T(8,128)(2,1)S(1)}, bf16[32,8,1280]{2,1,0:T(8,128)(2,1)}, u32[]{:S(2)}) copy-start(bf16[32,8,1280]{2,1,0:T(8,128)(2,1)} %get-tuple-element.21) | copy-start | bytes 1966084
  209.6 20.2 %copy-start.21 = (bf16[16,8,1280]{2,1,0:T(8,128)(2,1)}, bf16[16,8,1280]{2,1,0:T(8,128)(2,1)S(1)}, u32[]{:S(2)}) copy-start(bf16[16,8,1280]{2,1,0:T(8,128)(2,1)S(1)} %collective-permute-done.31.rest_12_) | copy-start | bytes 983044
  209.6 9.6 %collective-permute-start.18 = (bf16[16,8,1280]{2,1,0:T(8,128)(2,1)S(1)}, bf16[16,8,1280]{2,1,0:T(8,128)(2,1)S(1)}, u32[]{:S(2)}, u32[]{:S(2)}) collective-permute-start(bf16[16,8,1280]{2,1,0:T(8,128)(2,1)S(1)} %add_convert_fusion.8.rest_3_), channel_id=1, source_target_pairs={{0,2},{1,3},{2,0},{3,1},{4,6},{5,7},{6,4},{7,5}} | collective-permute-start | bytes 983048 | tf_op jit(solution)/shard_map/ppermute | solution.py:483
  210.7 9.7 %collective-permute-start.17 = (bf16[16,8,1280]{2,1,0:T(8,128)(2,1)S(1)}, bf16[16,8,1280]{2,1,0:T(8,128)(2,1)S(1)}, u32[]{:S(2)}, u32[]{:S(2)}) collective-permute-start(bf16[16,8,1280]{2,1,0:T(8,128)(2,1)S(1)} %add_convert_fusion.8.rest_3_), channel_id=1, source_target_pairs={{0,1},{1,0},{2,3},{3,2},{4,5},{5,4},{6,7},{7,6}} | collective-permute-start | bytes 983048 | tf_op jit(solution)/shard_map/ppermute | solution.py:485
  219.2 10.6 %collective-permute-start.11 = (bf16[16,8,1280]{2,1,0:T(8,128)(2,1)S(1)}, bf16[16,8,1280]{2,1,0:T(8,128)(2,1)S(1)}, u32[]{:S(2)}, u32[]{:S(2)}) collective-permute-start(bf16[16,8,1280]{2,1,0:T(8,128)(2,1)S(1)} %add_convert_fusion.9.rest_4_), channel_id=1, source_target_pairs={{0,2},{1,3},{2,0},{3,1},{4,6},{5,7},{6,4},{7,5}} | collective-permute-start | bytes 983048 | tf_op jit(solution)/shard_map/ppermute | solution.py:483
  220.3 23.6 %collective-permute-start.28 = (bf16[32,8,1280]{2,1,0:T(8,128)(2,1)S(1)}, bf16[32,8,1280]{2,1,0:T(8,128)(2,1)}, u32[]{:S(2)}, u32[]{:S(2)}) collective-permute-start(bf16[32,8,1280]{2,1,0:T(8,128)(2,1)S(1)} %add_convert_fusion.2.rest_0_.rest_1_), channel_id=1, source_target_pairs={{0,2},{1,3},{2,0},{3,1},{4,6},{5,7},{6,4},{7,5}} | collective-permute-start | bytes 1966088 | tf_op jit(solution)/shard_map/ppermute | solution.py:483
  221.2 36.7 %collective-permute-start.29 = (bf16[32,8,1280]{2,1,0:T(8,128)(2,1)S(1)}, bf16[32,8,1280]{2,1,0:T(8,128)(2,1)}, u32[]{:S(2)}, u32[]{:S(2)}) collective-permute-start(bf16[32,8,1280]{2,1,0:T(8,128)(2,1)S(1)} %add_convert_fusion.1.rest_1_.rest_2_), channel_id=1, source_target_pairs={{0,2},{1,3},{2,0},{3,1},{4,6},{5,7},{6,4},{7,5}} | collective-permute-start | bytes 1966088 | tf_op jit(solution)/shard_map/ppermute | solution.py:483
  222.4 49.7 %collective-permute-start.30 = (bf16[32,8,1280]{2,1,0:T(8,128)(2,1)S(1)}, bf16[32,8,1280]{2,1,0:T(8,128)(2,1)}, u32[]{:S(2)}, u32[]{:S(2)}) collective-permute-start(bf16[32,8,1280]{2,1,0:T(8,128)(2,1)S(1)} %add_convert_fusion.rest_2_.rest_3_), channel_id=1, source_target_pairs={{0,2},{1,3},{2,0},{3,1},{4,6},{5,7},{6,4},{7,5}} | collective-permute-start | bytes 1966088 | tf_op jit(solution)/shard_map/ppermute | solution.py:483
  226.6 3.1 collective-permute-start.39
  229.8 42.2 %copy-start.19 = (bf16[16,8,1280]{2,1,0:T(8,128)(2,1)}, bf16[16,8,1280]{2,1,0:T(8,128)(2,1)S(1)}, u32[]{:S(2)}) copy-start(bf16[16,8,1280]{2,1,0:T(8,128)(2,1)S(1)} %collective-permute-done.11.rest_12_) | copy-start | bytes 983044
  229.8 1.6 collective-permute-start.35
  229.8 43.3 %copy-start.27 = (bf16[16,8,1280]{2,1,0:T(8,128)(2,1)}, bf16[16,8,1280]{2,1,0:T(8,128)(2,1)S(1)}, u32[]{:S(2)}) copy-start(bf16[16,8,1280]{2,1,0:T(8,128)(2,1)S(1)} %collective-permute-done.39.rest_15_) | copy-start | bytes 983044
  229.8 2.5 collective-permute-start.19
  230.5 69.8 %copy-start.29 = (s32[64]{0:T(128)S(1)}, s32[64]{0:T(128)}, u32[]{:S(2)}) copy-start(s32[64]{0:T(128)} %len_ref.13) | copy-start | bytes 772
  232.1 43.4 %collective-permute-start.24 = (bf16[32,8,1280]{2,1,0:T(8,128)(2,1)S(1)}, bf16[32,8,1280]{2,1,0:T(8,128)(2,1)}, u32[]{:S(2)}, u32[]{:S(2)}) collective-permute-start(bf16[32,8,1280]{2,1,0:T(8,128)(2,1)S(1)} %add_convert_fusion.2.rest_0_.rest_1_), channel_id=1, source_target_pairs={{0,1},{1,0},{2,3},{3,2},{4,5},{5,4},{6,7},{7,6}} | collective-permute-start | bytes 1966088 | tf_op jit(solution)/shard_map/ppermute | solution.py:485
  233.0 42.5 %collective-permute-start.25 = (bf16[32,8,1280]{2,1,0:T(8,128)(2,1)S(1)}, bf16[32,8,1280]{2,1,0:T(8,128)(2,1)}, u32[]{:S(2)}, u32[]{:S(2)}) collective-permute-start(bf16[32,8,1280]{2,1,0:T(8,128)(2,1)S(1)} %add_convert_fusion.1.rest_1_.rest_2_), channel_id=1, source_target_pairs={{0,1},{1,0},{2,3},{3,2},{4,5},{5,4},{6,7},{7,6}} | collective-permute-start | bytes 1966088 | tf_op jit(solution)/shard_map/ppermute | solution.py:485
  243.9 32.6 %collective-permute-start.26 = (bf16[32,8,1280]{2,1,0:T(8,128)(2,1)S(1)}, bf16[32,8,1280]{2,1,0:T(8,128)(2,1)}, u32[]{:S(2)}, u32[]{:S(2)}) collective-permute-start(bf16[32,8,1280]{2,1,0:T(8,128)(2,1)S(1)} %add_convert_fusion.rest_2_.rest_3_), channel_id=1, source_target_pairs={{0,1},{1,0},{2,3},{3,2},{4,5},{5,4},{6,7},{7,6}} | collective-permute-start | bytes 1966088 | tf_op jit(solution)/shard_map/ppermute | solution.py:485
  258.0 28.1 %collective-permute-start.10 = (bf16[32,8,1280]{2,1,0:T(8,128)(2,1)S(1)}, bf16[32,8,1280]{2,1,0:T(8,128)(2,1)}, u32[]{:S(2)}, u32[]{:S(2)}) collective-permute-start(bf16[32,8,1280]{2,1,0:T(8,128)(2,1)S(1)} %add_convert_fusion.3.rest_2_.rest_3_), channel_id=1, source_target_pairs={{0,2},{1,3},{2,0},{3,1},{4,6},{5,7},{6,4},{7,5}} | collective-permute-start | bytes 1966088 | tf_op jit(solution)/shard_map/ppermute | solution.py:483
  272.0 28.1 %collective-permute-start.9 = (bf16[32,8,1280]{2,1,0:T(8,128)(2,1)S(1)}, bf16[32,8,1280]{2,1,0:T(8,128)(2,1)}, u32[]{:S(2)}, u32[]{:S(2)}) collective-permute-start(bf16[32,8,1280]{2,1,0:T(8,128)(2,1)S(1)} %add_convert_fusion.4.rest_1_.rest_2_), channel_id=1, source_target_pairs={{0,2},{1,3},{2,0},{3,1},{4,6},{5,7},{6,4},{7,5}} | collective-permute-start | bytes 1966088 | tf_op jit(solution)/shard_map/ppermute | solution.py:483
  275.5 44.0 %collective-permute-start.6 = (bf16[32,8,1280]{2,1,0:T(8,128)(2,1)S(1)}, bf16[32,8,1280]{2,1,0:T(8,128)(2,1)}, u32[]{:S(2)}, u32[]{:S(2)}) collective-permute-start(bf16[32,8,1280]{2,1,0:T(8,128)(2,1)S(1)} %add_convert_fusion.3.rest_2_.rest_3_), channel_id=1, source_target_pairs={{0,1},{1,0},{2,3},{3,2},{4,5},{5,4},{6,7},{7,6}} | collective-permute-start | bytes 1966088 | tf_op jit(solution)/shard_map/ppermute | solution.py:485
  275.6 43.4 %collective-permute-start.8 = (bf16[32,8,1280]{2,1,0:T(8,128)(2,1)}, bf16[32,8,1280]{2,1,0:T(8,128)(2,1)}, u32[]{:S(2)}, u32[]{:S(2)}) collective-permute-start(bf16[32,8,1280]{2,1,0:T(8,128)(2,1)} %add_convert_fusion.5.rest_0_.rest_1_), channel_id=1, source_target_pairs={{0,2},{1,3},{2,0},{3,1},{4,6},{5,7},{6,4},{7,5}} | collective-permute-start | bytes 1966088 | tf_op jit(solution)/shard_map/ppermute | solution.py:483
  276.5 43.1 %collective-permute-start.32 = (bf16[32,8,1280]{2,1,0:T(8,128)(2,1)}, bf16[32,8,1280]{2,1,0:T(8,128)(2,1)}, u32[]{:S(2)}, u32[]{:S(2)}) collective-permute-start(bf16[32,8,1280]{2,1,0:T(8,128)(2,1)} %collective-permute-done.28.rest_8_.rest_9_), channel_id=1, source_target_pairs={{0,1},{1,0},{2,3},{3,2},{4,5},{5,4},{6,7},{7,6}} | collective-permute-start | bytes 1966088 | tf_op jit(solution)/shard_map/ppermute | solution.py:487
  286.1 34.0 %collective-permute-start.33 = (bf16[32,8,1280]{2,1,0:T(8,128)(2,1)}, bf16[32,8,1280]{2,1,0:T(8,128)(2,1)}, u32[]{:S(2)}, u32[]{:S(2)}) collective-permute-start(bf16[32,8,1280]{2,1,0:T(8,128)(2,1)} %collective-permute-done.29.rest_9_.rest_10_), channel_id=1, source_target_pairs={{0,1},{1,0},{2,3},{3,2},{4,5},{5,4},{6,7},{7,6}} | collective-permute-start | bytes 1966088 | tf_op jit(solution)/shard_map/ppermute | solution.py:487
  300.1 20.0 %collective-permute-start.34 = (bf16[32,8,1280]{2,1,0:T(8,128)(2,1)}, bf16[32,8,1280]{2,1,0:T(8,128)(2,1)}, u32[]{:S(2)}, u32[]{:S(2)}) collective-permute-start(bf16[32,8,1280]{2,1,0:T(8,128)(2,1)} %collective-permute-done.30.rest_10_.rest_11_), channel_id=1, source_target_pairs={{0,1},{1,0},{2,3},{3,2},{4,5},{5,4},{6,7},{7,6}} | collective-permute-start | bytes 1966088 | tf_op jit(solution)/shard_map/ppermute | solution.py:487
  319.0 24.7 %collective-permute-start.5 = (bf16[32,8,1280]{2,1,0:T(8,128)(2,1)S(1)}, bf16[32,8,1280]{2,1,0:T(8,128)(2,1)S(1)}, u32[]{:S(2)}, u32[]{:S(2)}) collective-permute-start(bf16[32,8,1280]{2,1,0:T(8,128)(2,1)S(1)} %add_convert_fusion.4.rest_1_.rest_2_), channel_id=1, source_target_pairs={{0,1},{1,0},{2,3},{3,2},{4,5},{5,4},{6,7},{7,6}} | collective-permute-start | bytes 1966088 | tf_op jit(solution)/shard_map/ppermute | solution.py:485
  319.5 24.2 %collective-permute-start.4 = (bf16[32,8,1280]{2,1,0:T(8,128)(2,1)}, bf16[32,8,1280]{2,1,0:T(8,128)(2,1)S(1)}, u32[]{:S(2)}, u32[]{:S(2)}) collective-permute-start(bf16[32,8,1280]{2,1,0:T(8,128)(2,1)} %add_convert_fusion.5.rest_0_.rest_1_), channel_id=1, source_target_pairs={{0,1},{1,0},{2,3},{3,2},{4,5},{5,4},{6,7},{7,6}} | collective-permute-start | bytes 1966088 | tf_op jit(solution)/shard_map/ppermute | solution.py:485
  319.6 24.6 %collective-permute-start.14 = (bf16[32,8,1280]{2,1,0:T(8,128)(2,1)}, bf16[32,8,1280]{2,1,0:T(8,128)(2,1)S(1)}, u32[]{:S(2)}, u32[]{:S(2)}) collective-permute-start(bf16[32,8,1280]{2,1,0:T(8,128)(2,1)} %collective-permute-done.10.rest_10_.rest_11_), channel_id=1, source_target_pairs={{0,1},{1,0},{2,3},{3,2},{4,5},{5,4},{6,7},{7,6}} | collective-permute-start | bytes 1966088 | tf_op jit(solution)/shard_map/ppermute | solution.py:487
  320.0 24.2 %collective-permute-start.13 = (bf16[32,8,1280]{2,1,0:T(8,128)(2,1)}, bf16[32,8,1280]{2,1,0:T(8,128)(2,1)S(1)}, u32[]{:S(2)}, u32[]{:S(2)}) collective-permute-start(bf16[32,8,1280]{2,1,0:T(8,128)(2,1)} %collective-permute-done.9.rest_9_.rest_10_), channel_id=1, source_target_pairs={{0,1},{1,0},{2,3},{3,2},{4,5},{5,4},{6,7},{7,6}} | collective-permute-start | bytes 1966088 | tf_op jit(solution)/shard_map/ppermute | solution.py:487
  320.1 24.1 %collective-permute-start.12 = (bf16[32,8,1280]{2,1,0:T(8,128)(2,1)}, bf16[32,8,1280]{2,1,0:T(8,128)(2,1)S(1)}, u32[]{:S(2)}, u32[]{:S(2)}) collective-permute-start(bf16[32,8,1280]{2,1,0:T(8,128)(2,1)} %collective-permute-done.8.rest_8_.rest_9_), channel_id=1, source_target_pairs={{0,1},{1,0},{2,3},{3,2},{4,5},{5,4},{6,7},{7,6}} | collective-permute-start | bytes 1966088 | tf_op jit(solution)/shard_map/ppermute | solution.py:487
  332.1 11.6 %copy-start.20 = (bf16[16,8,1280]{2,1,0:T(8,128)(2,1)S(1)}, bf16[16,8,1280]{2,1,0:T(8,128)(2,1)}, u32[]{:S(2)}) copy-start(bf16[16,8,1280]{2,1,0:T(8,128)(2,1)} %copy-done.19) | copy-start | bytes 983044
  332.1 12.1 %copy-start.2 = (bf16[16,8,1280]{2,1,0:T(8,128)(2,1)S(1)}, bf16[16,8,1280]{2,1,0:T(8,128)(2,1)}, u32[]{:S(2)}) copy-start(bf16[16,8,1280]{2,1,0:T(8,128)(2,1)} %copy-done.1) | copy-start | bytes 983044
  332.1 12.1 %copy-start.10 = (bf16[16,8,1280]{2,1,0:T(8,128)(2,1)S(1)}, bf16[16,8,1280]{2,1,0:T(8,128)(2,1)}, u32[]{:S(2)}) copy-start(bf16[16,8,1280]{2,1,0:T(8,128)(2,1)} %copy-done.9) | copy-start | bytes 983044
  332.2 12.1 %copy-start.12 = (bf16[16,8,1280]{2,1,0:T(8,128)(2,1)S(1)}, bf16[16,8,1280]{2,1,0:T(8,128)(2,1)}, u32[]{:S(2)}) copy-start(bf16[16,8,1280]{2,1,0:T(8,128)(2,1)} %copy-done.11) | copy-start | bytes 983044
  332.2 12.1 %copy-start.14 = (bf16[16,8,1280]{2,1,0:T(8,128)(2,1)S(1)}, bf16[16,8,1280]{2,1,0:T(8,128)(2,1)}, u32[]{:S(2)}) copy-start(bf16[16,8,1280]{2,1,0:T(8,128)(2,1)} %copy-done.13) | copy-start | bytes 983044
  343.7 11.7 %collective-permute-start.7 = (bf16[16,8,1280]{2,1,0:T(8,128)(2,1)S(1)}, bf16[16,8,1280]{2,1,0:T(8,128)(2,1)S(1)}, u32[]{:S(2)}, u32[]{:S(2)}) collective-permute-start(bf16[16,8,1280]{2,1,0:T(8,128)(2,1)S(1)} %copy-done.4), channel_id=1, source_target_pairs={{0,1},{1,0},{2,3},{3,2},{4,5},{5,4},{6,7},{7,6}} | collective-permute-start | bytes 983048 | tf_op jit(solution)/shard_map/ppermute | solution.py:485
  343.7 11.7 %collective-permute-start.15 = (bf16[16,8,1280]{2,1,0:T(8,128)(2,1)S(1)}, bf16[16,8,1280]{2,1,0:T(8,128)(2,1)S(1)}, u32[]{:S(2)}, u32[]{:S(2)}) collective-permute-start(bf16[16,8,1280]{2,1,0:T(8,128)(2,1)S(1)} %copy-done.20), channel_id=1, source_target_pairs={{0,1},{1,0},{2,3},{3,2},{4,5},{5,4},{6,7},{7,6}} | collective-permute-start | bytes 983048 | tf_op jit(solution)/shard_map/ppermute | solution.py:487
  (19 other events, 148.0 us)
